TPU v7x, 256 devices: a whole 4x4x8 slice. The times are simulated.
256 devices in a mesh: nodes: 64 (over z, y, core), rep: 4 (over x).
Axes of the slice: x: 4, y: 4, z: 8, core: 2. Of those that a mesh axis runs over, the one named last changes fastest.
Arguments:
- features: bfloat16 [131072, 256], P('nodes'), may hold values from -64 to 64
- virtual_state: bfloat16 [4, 256], replicated, may hold values from -64 to 64
- w_query: bfloat16 [256, 256], P(None, 'rep'), may hold values from -0.375 to 0.375
- w_key: bfloat16 [256, 256], P(None, 'rep'), may hold values from -0.375 to 0.375
- w_value: bfloat16 [256, 256], P(None, 'rep'), may hold values from -0.375 to 0.375
- w_out: bfloat16 [256, 256], P('rep'), may hold values from -0.375 to 0.375
- tile_map: int32 [1024, 4], P('nodes'), may hold values from 0 to 1023, as said below
- local_nbr: int32 [131072, 16], P('nodes'), may hold values from 0 to 127
Outputs:
- node_out: bfloat16 [131072, 256], P('nodes', 'rep')
- virtual_out: bfloat16 [4, 256], P(None, 'rep')
Inputs may be any that keep to these rules, and one draw needn't show every extreme that they name: `tile_map`: entry [c, j] is a block number. In the 16 aligned rows of one index e of nodes, the blocks numbered f * 16 to (f + 1) * 16 - 1 are named exactly 16 * 4 / 64 times, for every f.
All inputs are finite; a program needn't handle non-finite values.
Results may differ from a plain program's by a relative error of at most 0.0029.
The roundings to bfloat16 on the way count: a program that leaves them out, or rounds other values in their place, can miss the bound.
Values may be sent and summed in bfloat16 or wider, within the bound.
No kernel may reach another device: no remote copies, remote signals or barrier semaphores. Data moves between devices by JAX's collectives and lax.ppermute only.
A program may use at most 64 MiB of HBM per device.

v0:
```python
import math

import jax
import jax.numpy as jnp
from jax import lax
from jax.sharding import PartitionSpec as P

D = 256
H = 8
TILE = 128
G = 4


def copy_for_each(shard, axis):
    devices = lax.axis_size(axis)
    return lax.all_to_all(
        jnp.broadcast_to(shard[None], (devices, *shard.shape)), axis, 0, 0, tiled=True
    )


def all_in_one(shard, axis):
    leaves = jax.tree.leaves(shard)
    turns = sorted(range(len(leaves)), key=lambda k: -leaves[k].size)
    width = (1, *leaves[turns[0]].shape)[-1]
    lines = [
        jnp.pad(leaves[k].reshape(-1), (0, -leaves[k].size % width)).reshape(-1, width)
        for k in turns
    ]
    both, at, found = (copy_for_each(jnp.concatenate(lines), axis), 0, {})
    for k, line in zip(turns, lines):
        section = both[:, at : at + len(line)].reshape(len(both), -1)
        found[k] = section[:, : leaves[k].size].reshape(-1, *leaves[k].shape)
        at += len(line)
    numbers = iter(range(len(leaves)))
    return jax.tree.map(lambda _: found[next(numbers)], shard)


def joined_by_halves(pieces, combine):
    while len(jax.tree.leaves(pieces)[0]) > 1:
        pieces = jax.vmap(combine)(
            *(jax.tree.map(lambda part: part[side::2], pieces) for side in (0, 1))
        )
    return jax.tree.map(lambda part: part[0], pieces)


def combined_all(shard, axis, combine):
    pieces = all_in_one(shard, axis)
    return joined_by_halves(pieces, combine)


def in_order(parts, dim):
    parts = jnp.moveaxis(parts, 0, dim)
    lengths = parts.shape
    return parts.reshape(*lengths[:dim], lengths[dim] * lengths[dim + 1], *lengths[dim + 2 :])


def gathered_copies(shard, axis, dim):
    parts = copy_for_each(shard, axis)
    return in_order(parts, dim)


def side_by_side(arrays, axis, dim, along):
    both = jnp.concatenate(arrays, axis=along)
    result, at, done = (gathered_copies(both, axis, dim), 0, [])
    for a in arrays:
        done.append(lax.slice_in_dim(result, at, at + a.shape[along], axis=along))
        at += a.shape[along]
    return tuple(done)


def project(source, weight):
    return jnp.dot(source, weight, preferred_element_type=jnp.float32).astype(jnp.bfloat16)


def combine_parts(earlier, later):
    top_one, total_one, weighted_one = earlier
    top_two, total_two, weighted_two = later
    highest = jnp.maximum(top_one, top_two)
    factor_one = jnp.exp(top_one - highest)
    factor_two = jnp.exp(top_two - highest)
    return (
        highest,
        total_one * factor_one + total_two * factor_two,
        weighted_one * factor_one[..., None] + weighted_two * factor_two[..., None],
    )


def shards(features, virtual_state, w_query, w_key, w_value, w_out, tile_map, local_nbr):
    row_count = features.shape[0]
    part_width = w_query.shape[1]
    head_size = D // H
    head_count = part_width // head_size
    score_scale = 1.0 / math.sqrt(head_size)
    block_count = row_count // TILE
    degree = tile_map.shape[1]
    peer_count = lax.axis_size("nodes")
    per_peer = block_count * degree // peer_count
    request_count = block_count * degree
    queries = project(features, w_query)
    keys_here = project(features, w_key)
    values_here = project(features, w_value)
    key_value = jnp.concatenate([keys_here, values_here], axis=1)
    flat_ids = tile_map.reshape(-1)
    owner_dev = flat_ids // block_count
    within = flat_ids % block_count
    owner_hits = (owner_dev[:, None] == jnp.arange(peer_count, dtype=jnp.int32)[None, :]).astype(
        jnp.int32
    )
    earlier_hits = jnp.cumsum(owner_hits, axis=0) - owner_hits
    position = jnp.sum(earlier_hits * owner_hits, axis=1)
    slot_of = owner_dev * per_peer + position
    placed = slot_of[:, None] == jnp.arange(request_count, dtype=jnp.int32)[None, :]
    ordered = jnp.sum(jnp.where(placed, within[:, None], 0), axis=0)
    wanted = lax.all_to_all(
        ordered.reshape(peer_count, per_peer), "nodes", split_axis=0, concat_axis=0, tiled=True
    ).reshape(-1)
    outgoing = key_value.reshape(block_count, TILE, 2 * part_width)[wanted]
    arrived = lax.all_to_all(outgoing, "nodes", split_axis=0, concat_axis=0, tiled=True)
    neighbour_tiles = arrived[slot_of]
    virtual_queries = project(virtual_state, w_query).reshape(G, head_count, head_size)
    virtual_keys = project(virtual_state, w_key)
    virtual_values = project(virtual_state, w_value)
    virtual_scores = (
        jnp.einsum(
            "ghd,nhd->hgn",
            virtual_queries,
            keys_here.reshape(row_count, head_count, head_size),
            preferred_element_type=jnp.float32,
        )
        * score_scale
    )
    values_wide = values_here.reshape(row_count, head_count, head_size).astype(jnp.float32)
    local_high = jnp.max(virtual_scores, axis=2)
    weights = jnp.exp(virtual_scores - local_high[..., None])
    total_part = jnp.sum(weights, axis=2)
    weighted_part = jnp.einsum(
        "hgn,nhd->hgd", weights, values_wide, precision=lax.Precision.HIGHEST
    )
    merged = combined_all((local_high, total_part, weighted_part), "nodes", combine_parts)
    total_sum, weighted = (merged[1], merged[2])
    virtual_heads = (
        jnp.transpose(weighted / total_sum[..., None], (1, 0, 2))
        .reshape(G, part_width)
        .astype(jnp.bfloat16)
    )
    bundle = 4
    group_count = block_count // bundle
    virtual_pair = jnp.concatenate([virtual_keys, virtual_values], axis=1)
    columns = jnp.arange(TILE, dtype=jnp.int32)

    def attend(inputs_now):
        query_group, own_group, other_group, link_group = inputs_now
        virtual_rows = jnp.broadcast_to(virtual_pair[None], (bundle, G, 2 * part_width))
        gathered = jnp.concatenate([own_group, other_group, virtual_rows], axis=1)
        key_count = gathered.shape[1]
        key_part = gathered[:, :, :part_width].reshape(bundle, key_count, head_count, head_size)
        value_part = gathered[:, :, part_width:].reshape(bundle, key_count, head_count, head_size)
        scores = (
            jnp.einsum("bqhd,bkhd->bhqk", query_group, key_part, preferred_element_type=jnp.float32)
            * score_scale
        )
        linked = jnp.any(link_group[:, :, :, None] == columns[None, None, None, :], axis=2)
        allowed = jnp.concatenate(
            [linked, jnp.ones((bundle, TILE, key_count - TILE), jnp.bool_)], axis=2
        )
        scores = jnp.where(allowed[:, None], scores, -1e30)
        highest = jnp.max(scores, axis=3, keepdims=True)
        weights = jnp.exp(scores - highest)
        total_rows = jnp.sum(weights, axis=3)
        blended = jnp.einsum(
            "bhqk,bkhd->bqhd",
            weights.astype(jnp.bfloat16),
            value_part,
            preferred_element_type=jnp.float32,
        )
        blended = blended / jnp.transpose(total_rows, (0, 2, 1))[..., None]
        return blended.astype(jnp.bfloat16).reshape(bundle * TILE, part_width)

    head_rows = lax.map(
        attend,
        (
            queries.reshape(group_count, bundle, TILE, head_count, head_size),
            key_value.reshape(group_count, bundle, TILE, 2 * part_width),
            neighbour_tiles.reshape(group_count, bundle, degree * TILE, 2 * part_width),
            local_nbr.reshape(group_count, bundle, TILE, local_nbr.shape[1]),
        ),
    ).reshape(row_count, part_width)
    rows_whole, virtual_whole, weight_whole = (
        *side_by_side((head_rows, virtual_heads), "rep", 1, 0),
        gathered_copies(w_out, "rep", 0),
    )
    own_start = lax.axis_index("rep") * part_width
    weight_cols = lax.dynamic_slice_in_dim(weight_whole, own_start, part_width, 1)
    node_sum = jnp.dot(rows_whole, weight_cols, preferred_element_type=jnp.float32)
    virtual_sum = jnp.dot(virtual_whole, weight_cols, preferred_element_type=jnp.float32)
    return (node_sum.astype(jnp.bfloat16), virtual_sum.astype(jnp.bfloat16))


def solution(mesh):
    in_specs = (
        P("nodes", None),
        P(),
        P(None, "rep"),
        P(None, "rep"),
        P(None, "rep"),
        P("rep", None),
        P("nodes", None),
        P("nodes", None),
    )
    out_specs = (P("nodes", "rep"), P(None, "rep"))
    return jax.shard_map(shards, mesh=mesh, in_specs=in_specs, out_specs=out_specs, check_vma=False)
```

profile of v0, /device:TPU:32, one launch (start us, length us, event | category | flops | bytes accessed | tf_op | source)
XLA Modules:
  0.0 165.1 jit_solution(8079944317701131006)
XLA Ops:
  0.6 0.8 copy.129
  2.8 11.8 %all-to-all-start = ((s32[64,1,1]{2,1,0:T(1,128)}), s32[64,1,1]{2,1,0:T(1,128)S(1)}, u32[]{:S(2)}, u32[]{:S(2)}) async-start(s32[64,1,1]{2,1,0:T(1,128)} %copy.130), calls=%async_computation | async-start | bytes 65536 | tf_op jit(solution)/shard_map/all_to_all | solution.py:114
  14.5 0.9 convolution_convert_fusion.5
  15.5 1.2 convolution_convert_fusion.3
  17.3 1.2 convolution_convert_fusion.2
  19.0 0.9 reshape.311
  20.2 3.0 %all-to-all-done = s32[64,1,1]{2,1,0:T(1,128)S(1)} async-done(((s32[64,1,1]{2,1,0:T(1,128)}), s32[64,1,1]{2,1,0:T(1,128)S(1)}, u32[]{:S(2)}, u32[]{:S(2)}) %all-to-all-start) | async-done | bytes 288 | tf_op jit(solution)/shard_map/all_to_all | solution.py:114
  23.2 7.3 %all-to-all-start.2 = ((f32[64,1,320]{2,1,0:T(1,128)}), f32[64,1,320]{2,1,0:T(1,128)S(1)}, u32[]{:S(2)}, u32[]{:S(2)}) async-start(f32[64,1,320]{2,1,0:T(1,128)} %reshape.311), calls=%async_computation.2 | async-start | bytes 196608 | tf_op jit(solution)/shard_map/all_to_all | solution.py:16
  30.5 1.2 reduce
  31.7 2.2 %gather_fusion = bf16[64,128,128]{2,1,0:T(8,128)(2,1)} fusion(bf16[16,128,128]{2,1,0:T(8,128)(2,1)S(1)} %bitcast.152, s32[1024]{0:T(1024)S(1)} %pad_clamp_fusion.1), kind=kCustom, calls=%fused_computation | custom fusion | bytes 4194560 | tf_op jit(solution)/shard_map/gather | solution.py:117
  33.9 6.1 %all-to-all-done.2 = f32[64,1,320]{2,1,0:T(1,128)S(1)} async-done(((f32[64,1,320]{2,1,0:T(1,128)}), f32[64,1,320]{2,1,0:T(1,128)S(1)}, u32[]{:S(2)}, u32[]{:S(2)}) %all-to-all-start.2) | async-done | bytes 81952 | tf_op jit(solution)/shard_map/all_to_all | solution.py:16
  40.0 5.6 %all-to-all-start.1 = ((bf16[64,128,128]{2,1,0:T(8,128)(2,1)}), bf16[64,128,128]{2,1,0:T(8,128)(2,1)S(1)}, u32[]{:S(2)}, u32[]{:S(2)}) async-start(bf16[64,128,128]{2,1,0:T(8,128)(2,1)} %gather_fusion), calls=%async_computation.1 | async-start | bytes 4194304 | tf_op jit(solution)/shard_map/all_to_all | solution.py:118
  45.7 2.2 %reshape.268 = bf16[4,4,128,128]{2,1,0,3:T(4,128)(2,1)} reshape(bf16[2048,128]{0,1:T(8,128)(2,1)} %copy-done.1) | data formatting | bytes 1048576 | tf_op jit(solution)/shard_map/reshape | solution.py:183
  48.0 1.1 convolution_convert_fusion.1
  49.1 1.1 reshape.274
  50.2 1.7 %reshape.273 = s32[4,4,128,16]{2,1,0,3:T(4,128)} reshape(s32[2048,16]{0,1:T(8,128)} %param.17) | data formatting | bytes 262144 | tf_op jit(solution)/shard_map/reshape | solution.py:185
  52.0 0.9 convolution_convert_fusion.7
  54.2 1.5 reduce.7
  55.8 1.8 %reshape.312 = f32[64,10,32]{2,1,0:T(8,128)} reshape(f32[64,320]{1,0:T(8,128)} %reduce.7) | data formatting | bytes 163840
  57.6 1.1 fusion.44
  59.4 1.7 %slice.200 = f32[64,8,32]{2,1,0:T(8,128)} slice(f32[64,10,32]{2,1,0:T(8,128)} %reshape.312), slice={[0:64], [0:8], [0:32]} | slice | bytes 131072 | tf_op jit(solution)/shard_map/slice | solution.py:31
  66.6 0.8 copy.145
  68.1 1.4 copy.147
  69.4 1.3 copy.148
  70.8 1.3 multiply_add_fusion.5
  72.1 1.3 copy.149
  73.4 1.3 copy.150
  74.9 1.2 multiply_add_fusion
  76.2 0.8 multiply_add_fusion.2
  77.0 0.8 multiply_add_fusion.3
  77.8 0.8 multiply_add_fusion.4
  78.8 17.3 %all-to-all-done.1 = bf16[64,128,128]{2,1,0:T(8,128)(2,1)S(1)} async-done(((bf16[64,128,128]{2,1,0:T(8,128)(2,1)}), bf16[64,128,128]{2,1,0:T(8,128)(2,1)S(1)}, u32[]{:S(2)}, u32[]{:S(2)}) %all-to-all-start.1) | async-done | bytes 2097184 | tf_op jit(solution)/shard_map/all_to_all | solution.py:118
  96.1 2.3 %gather_fusion.1 = bf16[64,128,128]{2,1,0:T(8,128)(2,1)} fusion(bf16[64,128,128]{2,1,0:T(8,128)(2,1)S(1)} %all-to-all-done.1, s32[1024]{0:T(1024)} %pad_clamp_fusion), kind=kCustom, calls=%fused_computation.1 | custom fusion | bytes 4194560 | tf_op jit(solution)/shard_map/gather | solution.py:119
  98.4 33.7 %while.11 = (s32[]{:T(128)}, bf16[4,512,64]{1,2,0:T(8,128)(2,1)}, bf16[4,4,128,128]{2,1,0,3:T(4,128)(2,1)}, bf16[4,4,512,128]{3,2,1,0:T(8,128)(2,1)}, bf16[4,128...) while((s32[]{:T(128)}, bf16[4,512,64]{1,2,0:T(8,128)(2,1)}, ...), condition=%wide.region_7.8_spmd.clone, body=%wide.region_3.7_spmd.clone.sunk | while | flops 95737856 | bytes 16258670 | solution.py:179
  98.4 1.1 constant_dynamic-slice_fusion.8
  99.7 1.0 constant_dynamic-slice_fusion.9
  100.9 0.8 constant_dynamic-slice_fusion.10
  101.8 1.6 fusion.76
  103.6 0.9 fusion.77
  105.2 0.9 fusion.79
  106.8 1.1 constant_dynamic-slice_fusion.8
  108.1 1.0 constant_dynamic-slice_fusion.9
  109.3 0.8 constant_dynamic-slice_fusion.10
  110.2 1.6 fusion.76
  112.1 0.9 fusion.77
  113.6 0.9 fusion.79
  115.2 1.1 constant_dynamic-slice_fusion.8
  116.6 1.0 constant_dynamic-slice_fusion.9
  117.7 0.8 constant_dynamic-slice_fusion.10
  118.6 1.6 fusion.76
  120.5 0.9 fusion.77
  122.1 0.9 fusion.79
  123.7 1.1 constant_dynamic-slice_fusion.8
  125.0 1.0 constant_dynamic-slice_fusion.9
  126.2 0.8 constant_dynamic-slice_fusion.10
  127.1 1.6 fusion.76
  128.9 0.9 fusion.77
  130.5 0.9 fusion.79
  132.1 1.0 copy.167
  133.2 20.0 %all_to_all.32 = bf16[4,2052,64]{1,2,0:T(8,128)(2,1)S(1)} all-to-all(bf16[4,2052,64]{1,2,0:T(8,128)(2,1)S(1)} %broadcast_in_dim.34), channel_id=1, replica_groups=mesh['nodes'=64,'rep'=4] {'rep'}, dimensions={0} | all-to-all | bytes 2101248 | tf_op jit(solution)/shard_map/all_to_all | solution.py:16
  153.9 3.3 %all-to-all-start.4 = ((bf16[4,64,256]{2,1,0:T(8,128)(2,1)}), bf16[4,64,256]{2,1,0:T(8,128)(2,1)S(1)}, u32[]{:S(2)}, u32[]{:S(2)}) async-start(bf16[4,64,256]{2,1,0:T(8,128)(2,1)} %broadcast_in_dim.35), calls=%async_computation.4 | async-start | bytes 262144 | tf_op jit(solution)/shard_map/all_to_all | solution.py:16
  157.4 5.8 %all-to-all-done.4 = bf16[4,64,256]{2,1,0:T(8,128)(2,1)S(1)} async-done(((bf16[4,64,256]{2,1,0:T(8,128)(2,1)}), bf16[4,64,256]{2,1,0:T(8,128)(2,1)S(1)}, u32[]{:S(2)}, u32[]{:S(2)}) %all-to-all-start.4) | async-done | bytes 131104 | tf_op jit(solution)/shard_map/all_to_all | solution.py:16
  163.2 1.1 convolution_convert_fusion
  164.3 0.8 convolution_convert_fusion.4
  (135 shorter events, 21.1 us)
Async XLA Ops:
  0.6 14.9 %copy-start = (bf16[2048,256]{1,0:T(8,128)(2,1)S(1)}, bf16[2048,256]{1,0:T(8,128)(2,1)}, u32[]{:S(2)}) copy-start(bf16[2048,256]{1,0:T(8,128)(2,1)} %param.10) | copy-start | bytes 3145732
  2.8 20.4 %all-to-all-start = ((s32[64,1,1]{2,1,0:T(1,128)}), s32[64,1,1]{2,1,0:T(1,128)S(1)}, u32[]{:S(2)}, u32[]{:S(2)}) async-start(s32[64,1,1]{2,1,0:T(1,128)} %copy.130), calls=%async_computation | async-start | bytes 65536 | tf_op jit(solution)/shard_map/all_to_all | solution.py:114
  18.6 15.3 %copy-start.1 = (bf16[2048,128]{0,1:T(8,128)(2,1)}, bf16[2048,128]{0,1:T(8,128)(2,1)S(1)}, u32[]{:S(2)}) copy-start(bf16[2048,128]{0,1:T(8,128)(2,1)S(1)} %pad_maximum_fusion.1) | copy-start | bytes 1572868
  23.2 16.8 %all-to-all-start.2 = ((f32[64,1,320]{2,1,0:T(1,128)}), f32[64,1,320]{2,1,0:T(1,128)S(1)}, u32[]{:S(2)}, u32[]{:S(2)}) async-start(f32[64,1,320]{2,1,0:T(1,128)} %reshape.311), calls=%async_computation.2 | async-start | bytes 196608 | tf_op jit(solution)/shard_map/all_to_all | solution.py:16
  33.9 14.0 %copy-start.2 = (bf16[256,64]{0,1:T(8,128)(2,1)S(1)}, bf16[256,64]{0,1:T(8,128)(2,1)}, u32[]{:S(2)}) copy-start(bf16[256,64]{0,1:T(8,128)(2,1)} %param.12) | copy-start | bytes 98308
  33.9 18.0 %copy-start.3 = (bf16[256,64]{0,1:T(8,128)(2,1)S(1)}, bf16[256,64]{0,1:T(8,128)(2,1)}, u32[]{:S(2)}) copy-start(bf16[256,64]{0,1:T(8,128)(2,1)} %param.14) | copy-start | bytes 98308
  33.9 18.0 %copy-start.5 = (bf16[4,256]{1,0:T(4,128)(2,1)S(1)}, bf16[4,256]{1,0:T(4,128)(2,1)}, u32[]{:S(2)}) copy-start(bf16[4,256]{1,0:T(4,128)(2,1)} %param.11) | copy-start | bytes 6148
  40.0 56.0 %all-to-all-start.1 = ((bf16[64,128,128]{2,1,0:T(8,128)(2,1)}), bf16[64,128,128]{2,1,0:T(8,128)(2,1)S(1)}, u32[]{:S(2)}, u32[]{:S(2)}) async-start(bf16[64,128,128]{2,1,0:T(8,128)(2,1)} %gather_fusion), calls=%async_computation.1 | async-start | bytes 4194304 | tf_op jit(solution)/shard_map/all_to_all | solution.py:118
  132.1 21.1 %copy-start.4 = (bf16[64,256]{1,0:T(8,128)(2,1)S(1)}, bf16[64,256]{1,0:T(8,128)(2,1)}, u32[]{:S(2)}) copy-start(bf16[64,256]{1,0:T(8,128)(2,1)} %param.15) | copy-start | bytes 98308
  153.9 9.3 %all-to-all-start.4 = ((bf16[4,64,256]{2,1,0:T(8,128)(2,1)}), bf16[4,64,256]{2,1,0:T(8,128)(2,1)S(1)}, u32[]{:S(2)}, u32[]{:S(2)}) async-start(bf16[4,64,256]{2,1,0:T(8,128)(2,1)} %broadcast_in_dim.35), calls=%async_computation.4 | async-start | bytes 262144 | tf_op jit(solution)/shard_map/all_to_all | solution.py:16
where the time goes:
time: 167 us; the launch traced here: 165 us
  local copies, waits for them, and re-layouts  48.5 us (29%)
  waiting for transfers between devices  32.3 us (19%)
  starting transfers between devices  28 us (17%)
  blocking collectives  20 us (12%)
  other arithmetic  19.8 us (12%)
  matrix products  15.2 us (9%)
    all_to_all x1, blocking collectives, copy_for_each(): lax.all_to_all(jnp.broadcast_to(shard[None], (devices, *shard.shape)), ax...  20 us
    all_to_all x1, waiting for transfers between devices, shards(): lax.all_to_all(outgoing, 'nodes', split_axis=0, concat_axis=0, tiled=True)  17.3 us
    dynamic_slice x24, local copies, waits for them, and re-layouts, shards(): lax.map(attend, (queries.reshape(group_count, bundle, TILE, head_count, h...  12.3 us
    all_to_all x2, waiting for transfers between devices, copy_for_each(): lax.all_to_all(jnp.broadcast_to(shard[None], (devices, *shard.shape)), ax...  11.9 us
    all_to_all x1, starting transfers between devices, shards(): lax.all_to_all(ordered.reshape(peer_count, per_peer), 'nodes', split_axis...  11.8 us
    all_to_all x2, starting transfers between devices, copy_for_each(): lax.all_to_all(jnp.broadcast_to(shard[None], (devices, *shard.shape)), ax...  10.6 us
    reduce_or x4, other arithmetic, attend(): jnp.any(link_group[:, :, :, None] == columns[None, None, None, :], axis=2)  6.29 us
    all_to_all x1, starting transfers between devices, shards(): lax.all_to_all(outgoing, 'nodes', split_axis=0, concat_axis=0, tiled=True)  5.6 us
  transfers between devices with their start and end apart: 4, of which 4 were waited for; matrix products, arithmetic and copies ran while one was open for 26% of the time, Pallas kernels for 0%

commit v1 on v0

v1 whole, which is shorter than its diff:
```python
import math

import jax
import jax.numpy as jnp
from jax import lax
from jax.experimental import pallas as pl
from jax.experimental.pallas import tpu as pltpu
from jax.sharding import PartitionSpec as P

D = 256
H = 8
TILE = 128
G = 4
HEAD = D // H
REP = 4
PEERS = 64
WIDTH = D // REP
QUARTER = TILE // REP
SCORE_SCALE = 1.0 / math.sqrt(HEAD)
EXP2_SCALE = SCORE_SCALE * math.log2(math.e)
NEG = -1e30
NT = (((1,), (1,)), ((), ()))
NN = (((1,), (0,)), ((), ()))

ANY = pl.BlockSpec(memory_space=pl.ANY)
SMEM = pl.BlockSpec(memory_space=pltpu.SMEM)
VMEM = pl.BlockSpec(memory_space=pltpu.VMEM)


def dot(a, b, dims=NN, precision=None):
    return lax.dot_general(a, b, dims, precision=precision, preferred_element_type=jnp.float32)


def wanted_rows_kernel(map_ref, out_ref):
    def put(s, carry):
        block = map_ref[s // 4, s % 4]
        out_ref[block // 16] = jnp.full((1, TILE), block % 16, jnp.int32)
        return carry

    lax.fori_loop(0, PEERS, put, 0, unroll=8)


def gather_send_kernel(x_ref, want_ref, feat_ref, out_ref, sem):
    def issue(e, carry):
        pltpu.make_async_copy(feat_ref.at[want_ref[e, 0, 0] * REP + x_ref[0]], out_ref.at[e], sem).start()
        return carry

    lax.fori_loop(0, PEERS, issue, 0, unroll=8)
    pltpu.make_async_copy(out_ref, out_ref, sem).wait()


def gather_rep_kernel(x_ref, map_ref, arrived_ref, *outs_sem):
    outs, sem = outs_sem[:REP], outs_sem[REP]
    for d in range(REP):
        row = ((x_ref[0] + d) % REP) * 4

        def issue(j, carry):
            owner = map_ref[row + j // 4, j % 4] // 16
            pltpu.make_async_copy(arrived_ref.at[owner], outs[d].at[j], sem.at[d]).start()
            return carry

        lax.fori_loop(0, 16, issue, 0, unroll=8)
    for d in range(REP):
        pltpu.make_async_copy(outs[d], outs[d], sem.at[d]).wait()


def virtual_kernel(feat_ref, pack_ref, vs_ref, out_ref):
    kv = dot(feat_ref[...], pack_ref[:, :TILE]).astype(jnp.bfloat16)
    q = dot(vs_ref[...], pack_ref[:, TILE:]).astype(jnp.bfloat16)
    lane = lax.broadcasted_iota(jnp.int32, (2 * G, TILE), 1)
    row = lax.broadcasted_iota(jnp.int32, (2 * G, TILE), 0)
    first = WIDTH + HEAD * (row // G)
    q = jnp.where((lane >= first) & (lane < first + HEAD), q.astype(jnp.float32), 0.0).astype(jnp.bfloat16)
    s = dot(q, kv, NT)
    top = jnp.max(s, axis=1, keepdims=True)
    p = jnp.exp2((s - top) * EXP2_SCALE)
    total = jnp.sum(p, axis=1, keepdims=True)
    w = dot(p, kv.astype(jnp.float32), NN, lax.Precision.HIGHEST)
    out_ref[...] = jnp.where(lane < 64, w, jnp.where(lane < 96, total, top))


def attention_kernel(x_ref, *refs):
    xs, refs = refs[:2], refs[2:]
    ns, refs = (refs[:4], refs[4:8]), refs[8:]
    bias, refs = refs[:2], refs[2:]
    packs, refs = refs[:4], refs[4:]
    vs_ref, outs = refs[0], refs[1:]
    lane = lax.broadcasted_iota(jnp.int32, (TILE, TILE), 1)
    virtual_bias = jnp.where(lax.broadcasted_iota(jnp.int32, (1, TILE), 1) < G, 0.0, NEG)
    halves = []
    for half in range(2):
        own = xs[half][...]
        rows = [own] + [ns[half][d][...] for d in range(REP)] + [vs_ref[...]]
        source = jnp.concatenate(rows, axis=0)
        groups = []
        for g in range(REP):
            kv = dot(source, packs[g][:, :TILE]).astype(jnp.bfloat16)
            q = dot(own, packs[g][:, TILE:])
            q0 = jnp.where((lane >= WIDTH) & (lane < WIDTH + HEAD), q, 0.0)
            q1 = jnp.where(lane >= WIDTH + HEAD, q, 0.0)
            picked = []
            for qh in (q0, q1):
                s = dot(qh.astype(jnp.bfloat16), kv, NT)
                s = jnp.concatenate(
                    [s[:, :TILE] + bias[half][...], s[:, TILE : 5 * TILE], s[:, 5 * TILE :] + virtual_bias], axis=1
                )
                top = jnp.max(s, axis=1, keepdims=True)
                p = jnp.exp2((s - top) * EXP2_SCALE)
                total = jnp.sum(p, axis=1, keepdims=True)
                o = dot(p.astype(jnp.bfloat16), kv)
                picked.append(o * (1.0 / total))
            o = jnp.where(lane < HEAD, picked[0], jnp.where(lane < WIDTH, picked[1], 0.0))
            groups.append(o.astype(jnp.bfloat16))
        halves.append(jnp.concatenate(groups, axis=1))
    rows = jnp.concatenate(halves, axis=0)
    for d in range(REP):
        first = pl.multiple_of(((x_ref[0] + d) % REP) * WIDTH, WIDTH)
        w = jnp.concatenate([packs[g][pl.ds(first, WIDTH), TILE:] for g in range(REP)], axis=1)
        t = dot(rows, jnp.concatenate([w, w], axis=0), NT)
        outs[d][...] = jnp.where(lane < WIDTH, t[:TILE], t[TILE:]).astype(jnp.bfloat16)


def assemble_kernel(x_ref, *refs):
    out_ref = refs[REP]
    for d in range(REP):
        first = pl.multiple_of(((x_ref[0] + REP - d) % REP) * 512, 512)
        out_ref[pl.ds(first, 256), :] = refs[d][:, :WIDTH]
        out_ref[pl.ds(first + 256, 256), :] = refs[d][:, WIDTH:]


def over_rep(value):
    return [value] + [
        lax.ppermute(value, "rep", [(i, (i + d) % REP) for i in range(REP)]) for d in range(1, REP)
    ]


def send_rep(values):
    return [values[0]] + [
        lax.ppermute(values[d], "rep", [(i, (i + d) % REP) for i in range(REP)]) for d in range(1, REP)
    ]


def merged_virtual(state):
    index = lax.axis_index("nodes")
    lane = lax.broadcasted_iota(jnp.int32, state.shape, 1)
    for bit in (1, 2, 4, 8, 16, 32):
        other = lax.ppermute(state, "nodes", [(i, i ^ bit) for i in range(PEERS)])
        upper = (index & bit) != 0
        a = jnp.where(upper, other, state)
        b = jnp.where(upper, state, other)
        top_a, top_b = a[:, 96:97], b[:, 96:97]
        top = jnp.maximum(top_a, top_b)
        joined = a * jnp.exp((top_a - top) * SCORE_SCALE) + b * jnp.exp((top_b - top) * SCORE_SCALE)
        state = jnp.where(lane < 96, joined, top)
    return state


def shards(features, virtual_state, w_query, w_key, w_value, w_out, tile_map, local_nbr):
    bf16 = jnp.bfloat16
    x = lax.axis_index("rep")
    x_one = x.astype(jnp.int32).reshape(1)

    wanted_from = pl.pallas_call(
        wanted_rows_kernel,
        out_shape=jax.ShapeDtypeStruct((PEERS, 1, TILE), jnp.int32),
        in_specs=[SMEM],
        out_specs=VMEM,
        name="wanted_rows",
    )(tile_map)
    wanted = lax.all_to_all(wanted_from, "nodes", 0, 0, tiled=True)

    pack = jnp.concatenate([w_value, w_key, w_out.T, w_query], axis=1)
    packs = over_rep(pack)

    state = pl.pallas_call(
        virtual_kernel,
        out_shape=jax.ShapeDtypeStruct((2 * G, TILE), jnp.float32),
        name="virtual_part",
    )(features, pack, jnp.concatenate([virtual_state, virtual_state], axis=0))
    state = merged_virtual(state)

    outgoing = pl.pallas_call(
        gather_send_kernel,
        out_shape=jax.ShapeDtypeStruct((PEERS, QUARTER, D), bf16),
        in_specs=[SMEM, SMEM, ANY],
        out_specs=ANY,
        scratch_shapes=[pltpu.SemaphoreType.DMA],
        name="gather_send",
    )(x_one, wanted, features.reshape(PEERS, QUARTER, D))
    arrived = lax.all_to_all(outgoing, "nodes", 0, 0, tiled=True)

    sends = pl.pallas_call(
        gather_rep_kernel,
        out_shape=[jax.ShapeDtypeStruct((16, QUARTER, D), bf16)] * REP,
        in_specs=[SMEM, SMEM, ANY],
        out_specs=[ANY] * REP,
        scratch_shapes=[pltpu.SemaphoreType.DMA((REP,))],
        name="gather_rep",
    )(x_one, tile_map, arrived)
    pieces = [piece.reshape(16 * QUARTER, D) for piece in send_rep(sends)]

    own_links = lax.dynamic_slice_in_dim(local_nbr, x * 512, 512, 0)
    linked = jnp.any(own_links[:, :, None] == jnp.arange(TILE, dtype=jnp.int32), axis=1)
    bias = jnp.where(linked, 0.0, NEG).astype(jnp.float32)
    virtual_rows = jnp.pad(virtual_state, ((0, TILE - G), (0, 0)))

    tile = (TILE, D)
    low = lambda j, x: (j, 0)
    high = lambda j, x: (j + 2, 0)
    whole = lambda j, x: (0, 0)
    outs = pl.pallas_call(
        attention_kernel,
        grid_spec=pltpu.PrefetchScalarGridSpec(
            num_scalar_prefetch=1,
            grid=(2,),
            in_specs=[
                pl.BlockSpec(tile, lambda j, x: (x[0] * 4 + j, 0)),
                pl.BlockSpec(tile, lambda j, x: (x[0] * 4 + j + 2, 0)),
                *[pl.BlockSpec(tile, low)] * 4,
                *[pl.BlockSpec(tile, high)] * 4,
                pl.BlockSpec((TILE, TILE), low),
                pl.BlockSpec((TILE, TILE), high),
                *[pl.BlockSpec((D, D), whole)] * 4,
                pl.BlockSpec(tile, whole),
            ],
            out_specs=[pl.BlockSpec((TILE, TILE), low)] * 4,
        ),
        out_shape=[jax.ShapeDtypeStruct((2 * TILE, TILE), bf16)] * 4,
        name="attention",
    )(x_one, features, features, *pieces, *pieces, bias, bias, *packs, virtual_rows)
    received = send_rep(outs)
    node_out = pl.pallas_call(
        assemble_kernel,
        out_shape=jax.ShapeDtypeStruct((2048, WIDTH), bf16),
        in_specs=[SMEM] + [VMEM] * 4,
        out_specs=VMEM,
        name="assemble",
    )(x_one, *received)

    lane = lax.broadcasted_iota(jnp.int32, (G, TILE), 1)
    heads = state / state[:, 64:65]
    heads = jnp.where(lane < HEAD, heads[:G], jnp.where(lane < WIDTH, heads[G:], 0.0)).astype(bf16)
    heads_all = jnp.concatenate(over_rep(heads), axis=1)
    columns = jnp.concatenate(
        [lax.dynamic_slice(p, (x * WIDTH, TILE), (WIDTH, TILE)) for p in packs], axis=1
    )
    virtual_out = dot(heads_all, columns, NT).astype(bf16)
    return node_out, virtual_out


def solution(mesh):
    in_specs = (
        P("nodes", None),
        P(),
        P(None, "rep"),
        P(None, "rep"),
        P(None, "rep"),
        P("rep", None),
        P("nodes", None),
        P("nodes", None),
    )
    out_specs = (P("nodes", "rep"), P(None, "rep"))
    return jax.shard_map(shards, mesh=mesh, in_specs=in_specs, out_specs=out_specs, check_vma=False)
```

time: 167 us -> 205 us (1.23)
  Pallas kernels: 0 us -> 93.5 us
  local copies, waits for them, and re-layouts: 48.5 us -> 11.4 us
  starting transfers between devices: 28 us -> 48.3 us
  blocking collectives: 20 us -> 0 us
  matrix products: 15.2 us -> 0.7 us
  other arithmetic: 19.8 us -> 11.3 us
  waiting for transfers between devices: 32.3 us -> 37.5 us
    pallas_call x0 -> x6, Pallas kernels: none -> 93.5 us  [the longest x1 34.1 us: shards(): pl.pallas_call(gather_send_kernel, out_shape=jax.ShapeDtypeStruct((PEERS,...]
    ppermute x0 -> x18, waiting for transfers between devices: none -> 37.5 us  [the longest x6 26.5 us: merged_virtual(): other = lax.ppermute(state, 'nodes', [(i, i ^ bit) for i in range(PEERS)])]
    all_to_all x4 -> x2, waiting for transfers between devices: 32.3 us -> 0.01 us  [the longest x1 0.01 us: shards(): wanted = lax.all_to_all(wanted_from, 'nodes', 0, 0, tiled=True)]
    ppermute x0 -> x18, starting transfers between devices: none -> 28 us  [the longest x6 11.7 us: merged_virtual(): other = lax.ppermute(state, 'nodes', [(i, i ^ bit) for i in range(PEERS)])]
    all_to_all x1 -> x0, blocking collectives: 20 us -> none  [copy_for_each(): lax.all_to_all(jnp.broadcast_to(shard[None], (devices, *shard.shape)), ax...]
    dot_general x18 -> x1, matrix products: 15.2 us -> 0.7 us  [dot(): lax.dot_general(a, b, dims, precision=precision, preferred_element_type=j...]
    dynamic_slice x24 -> x6, local copies, waits for them, and re-layouts: 12.3 us -> 0.85 us  [the longest x4 0.72 us: shards(): lax.dynamic_slice(p, (x * WIDTH, TILE), (WIDTH, TILE))]
    all_to_all x4 -> x2, starting transfers between devices: 28 us -> 20.3 us  [the longest x1 11.8 us: shards(): wanted = lax.all_to_all(wanted_from, 'nodes', 0, 0, tiled=True)]
  transfers between devices with their start and end apart: 4 -> 20, of which waited for: 4 -> 9; matrix products, arithmetic and copies ran while one was open for 26% -> 7% of each run, Pallas kernels for 0% -> 45%
where the time goes in v1:
time: 205 us; the launch traced here: 204 us
  Pallas kernels  93.5 us (46%)
  starting transfers between devices  48.3 us (24%)
  waiting for transfers between devices  37.5 us (18%)
  local copies, waits for them, and re-layouts  11.4 us (6%)
  other arithmetic  11.3 us (6%)
    pallas_call x1, Pallas kernels, shards(): pl.pallas_call(gather_send_kernel, out_shape=jax.ShapeDtypeStruct((PEERS,...  34.1 us
    pallas_call x1, Pallas kernels, shards(): pl.pallas_call(gather_rep_kernel, out_shape=[jax.ShapeDtypeStruct((16, QU...  33.7 us
    ppermute x6, waiting for transfers between devices, merged_virtual(): other = lax.ppermute(state, 'nodes', [(i, i ^ bit) for i in range(PEERS)])  26.5 us
    pallas_call x1, Pallas kernels, shards(): pl.pallas_call(attention_kernel, grid_spec=pltpu.PrefetchScalarGridSpec(n...  18.1 us
    all_to_all x1, starting transfers between devices, shards(): wanted = lax.all_to_all(wanted_from, 'nodes', 0, 0, tiled=True)  11.8 us
    ppermute x6, starting transfers between devices, merged_virtual(): other = lax.ppermute(state, 'nodes', [(i, i ^ bit) for i in range(PEERS)])  11.7 us
    ppermute x6, waiting for transfers between devices, send_rep(): lax.ppermute(values[d], 'rep', [(i, (i + d) % REP) for i in range(REP)])  11 us
    unnamed x32, local copies, waits for them, and re-layouts  9.77 us
  transfers between devices with their start and end apart: 20, of which 9 were waited for; matrix products, arithmetic and copies ran while one was open for 7% of the time, Pallas kernels for 45%

profile of v1, /device:TPU:32, one launch (start us, length us, event | category | flops | bytes accessed | tf_op | source)
XLA Modules:
  0.0 203.6 jit_solution(72187162816676601)
XLA Ops:
  0.6 0.9 copy.32
  1.6 0.9 copy.29
  2.4 0.9 copy.31
  3.3 0.9 copy.30
  4.2 0.8 pad_maximum_fusion.refs_12_.pack_ref
  5.0 1.5 collective-permute-start.3
  6.5 2.7 %collective-permute-start.4 = (bf16[256,256]{1,0:T(8,128)(2,1)}, bf16[256,256]{1,0:T(8,128)(2,1)S(1)}, u32[]{:S(2)}, u32[]{:S(2)}) collective-permute-start(bf16[256,256]{1,0:T(8,128)(2,1)} %pad_maximum_fusion.refs_12_.pack_ref), channel_id=1, source_target_pairs={{0,2},{1,3},{2,0},{3,1},{4,6},{5,7},{6,4},{7,5},{8,10},{9,11},{10,... | collective-permute-start | bytes 393224 | tf_op jit(solution)/shard_map/ppermute | solution.py:133
  9.2 1.4 collective-permute-start.5
  10.6 1.3 copy.27.map_ref
  12.0 2.2 %wanted_rows.1 = s32[64,1,128]{2,1,0:T(1,128)} custom-call(s32[16,4]{1,0:T(8,128)} %copy.27.map_ref), custom_call_target="tpu_custom_call" | custom-call | tf_op jit(solution)/shard_map/wanted_rows/pallas_call | solution.py:163
  14.2 11.8 %all-to-all-start = ((s32[64,1,128]{2,1,0:T(1,128)}), s32[64,1,128]{2,1,0:T(1,128)S(1)}, u32[]{:S(2)}, u32[]{:S(2)}) async-start(s32[64,1,128]{2,1,0:T(1,128)} %wanted_rows.1), calls=%async_computation | async-start | bytes 65536 | tf_op jit(solution)/shard_map/all_to_all | solution.py:170
  26.0 1.4 pad_maximum_fusion.1.vs_ref
  27.3 3.4 %virtual_part.1 = f32[8,128]{1,0:T(8,128)} custom-call(bf16[2048,256]{1,0:T(8,128)(2,1)} %feat_ref.1, bf16[256,256]{1,0:T(8,128)(2,1)} %pad_maximum_fusion.refs_12_.pack_ref, bf16[8,256]{1,0:T(8,128)(2,1)} %pad_maximum_fusion.1.vs_ref), custom_call_target="tpu_custom_call" | custom-call | tf_op jit(solution)/shard_map/virtual_part/pallas_call | solution.py:175
  30.8 0.1 collective-permute-start.9
  30.9 1.3 collective-permute-done.9
  32.2 0.7 broadcast_select_fusion.2
  32.8 0.2 exponential_reduce_fusion.11
  33.1 0.1 add_select_fusion.5
  33.1 1.5 collective-permute-start.10
  34.6 0.1 copy.28
  34.8 2.0 collective-permute-done.10
  36.8 0.2 exponential_reduce_fusion.9
  37.0 0.1 add_select_fusion.4
  37.1 3.0 %collective-permute-start.11 = (f32[8,128]{1,0:T(8,128)S(1)}, f32[8,128]{1,0:T(8,128)S(1)}, u32[]{:S(2)}, u32[]{:S(2)}) collective-permute-start(f32[8,128]{1,0:T(8,128)S(1)} %add_select_fusion.4), channel_id=1, source_target_pairs={{0,16},{4,20},{8,24},{12,28},{16,0},{20,4},{24,8},{28,12},{32,48},... | collective-permute-start | bytes 12296 | tf_op jit(solution)/shard_map/ppermute | solution.py:147
  40.1 5.8 %fusion = pred[512,128]{1,0:T(8,128)(4,1)S(1)} fusion(s32[512,16]{1,0:T(8,128)S(1)} %copy.28), kind=kLoop, calls=%fused_computation.1 | loop fusion | flops 2031616 | bytes 98304 | tf_op jit(solution)/shard_map/reduce_or | solution.py:203
  45.9 0.2 exponential_reduce_fusion.7
  46.1 0.1 add_select_fusion.3
  46.2 0.6 collective-permute-start.12
  46.8 0.7 broadcast_select_fusion.refs_10_.refs_11_
  47.5 0.6 copy-done.8
  48.1 34.1 %gather_send.1 = bf16[64,32,256]{2,1,0:T(8,128)(2,1)} custom-call(s32[1]{0:T(128)} %bitcast.x_ref, s32[64,1,128]{2,1,0:T(1,128)} %copy-done.8, bf16[64,32,256]{2,1,0:T(8,128)(2,1)} %bitcast.7), custom_call_target="tpu_custom_call" | custom-call | tf_op jit(solution)/shard_map/gather_send/pallas_call | solution.py:182
  82.2 8.6 %all-to-all-start.1 = ((bf16[64,32,256]{2,1,0:T(8,128)(2,1)}), bf16[64,32,256]{2,1,0:T(8,128)(2,1)S(1)}, u32[]{:S(2)}, u32[]{:S(2)}) async-start(bf16[64,32,256]{2,1,0:T(8,128)(2,1)} %gather_send.1), calls=%async_computation.1 | async-start | bytes 2097152 | tf_op jit(solution)/shard_map/all_to_all | solution.py:190
  90.8 0.2 exponential_reduce_fusion.5
  91.1 2.4 %collective-permute-start.13 = (f32[8,128]{1,0:T(8,128)S(1)}, f32[8,128]{1,0:T(8,128)S(1)}, u32[]{:S(2)}, u32[]{:S(2)}) collective-permute-start(f32[8,128]{1,0:T(8,128)S(1)} %add_select_fusion.2), channel_id=1, source_target_pairs={{0,64},{4,68},{8,72},{12,76},{16,80},{20,84},{24,88},{28,92},{32,9... | collective-permute-start | bytes 12296 | tf_op jit(solution)/shard_map/ppermute | solution.py:147
  93.5 0.7 constant_dynamic-slice_fusion.3
  94.3 20.4 %collective-permute-done.13 = f32[8,128]{1,0:T(8,128)S(1)} collective-permute-done((f32[8,128]{1,0:T(8,128)S(1)}, f32[8,128]{1,0:T(8,128)S(1)}, u32[]{:S(2)}, u32[]{:S(2)}) %collective-permute-start.13) | collective-permute-done | bytes 4128 | tf_op jit(solution)/shard_map/ppermute | solution.py:147
  114.7 0.2 exponential_reduce_fusion.3
  115.0 4.1 %collective-permute-start.14 = (f32[8,128]{1,0:T(8,128)S(1)}, f32[8,128]{1,0:T(8,128)S(1)}, u32[]{:S(2)}, u32[]{:S(2)}) collective-permute-start(f32[8,128]{1,0:T(8,128)S(1)} %add_select_fusion.1), channel_id=1, source_target_pairs={{0,128},{4,132},{8,136},{12,140},{16,144},{20,148},{24,152},{28,15... | collective-permute-start | bytes 12296 | tf_op jit(solution)/shard_map/ppermute | solution.py:147
  119.1 0.6 pad.4.refs_16_
  119.7 2.9 %collective-permute-done.14 = f32[8,128]{1,0:T(8,128)S(1)} collective-permute-done((f32[8,128]{1,0:T(8,128)S(1)}, f32[8,128]{1,0:T(8,128)S(1)}, u32[]{:S(2)}, u32[]{:S(2)}) %collective-permute-start.14) | collective-permute-done | bytes 4128 | tf_op jit(solution)/shard_map/ppermute | solution.py:147
  122.6 0.2 exponential_reduce_fusion.1
  122.8 0.1 add_select_fusion
  122.9 0.2 slice_reduce_fusion
  123.1 1.0 copy-done.1
  124.1 33.7 %gather_rep.1 = (bf16[16,32,256]{2,1,0:T(8,128)(2,1)}, bf16[16,32,256]{2,1,0:T(8,128)(2,1)}, bf16[16,32,256]{2,1,0:T(8,128)(2,1)}, bf16[16,32,256]{2,1,0:T(8,128)(2,1)}) custom-call(s32[1]{0:T(128)} %bitcast.x_ref, s32[16,4]{1,0:T(8,128)} %copy.27.map_ref, bf16[64,32,256]{2,1,0:T(8,128)(2,1)} %copy-done.1), custom_call_target="tpu_custom_call" | custom-call | tf_op jit(solution)/shard_map/gather_rep/pallas_call | solution.py:192
  157.9 0.7 collective-permute-start
  158.5 0.9 collective-permute-start.1
  159.4 2.1 %collective-permute-start.2 = (bf16[16,32,256]{2,1,0:T(8,128)(2,1)}, bf16[16,32,256]{2,1,0:T(8,128)(2,1)S(1)}, u32[]{:S(2)}, u32[]{:S(2)}) collective-permute-start(bf16[16,32,256]{2,1,0:T(8,128)(2,1)} %get-tuple-element.13), channel_id=1, source_target_pairs={{0,3},{1,0},{2,1},{3,2},{4,7},{5,4},{6,5},{7,6},{8,11},{9,8},{10,9... | collective-permute-start | bytes 786440 | tf_op jit(solution)/shard_map/ppermute | solution.py:139
  161.5 1.2 collective-permute-start.17
  162.7 1.6 collective-permute-start.16
  164.3 6.6 %collective-permute-done = bf16[16,32,256]{2,1,0:T(8,128)(2,1)S(1)} collective-permute-done((bf16[16,32,256]{2,1,0:T(8,128)(2,1)}, bf16[16,32,256]{2,1,0:T(8,128)(2,1)S(1)}, u32[]{:S(2)}, u32[]{:S(2)}) %collective-permute-start) | collective-permute-done | bytes 262176 | tf_op jit(solution)/shard_map/ppermute | solution.py:139
  171.0 0.6 collective-permute-done.2
  171.6 0.1 copy-done.3
  171.7 0.5 copy-done.4
  172.3 18.1 %attention.1 = (bf16[256,128]{1,0:T(8,128)(2,1)}, bf16[256,128]{1,0:T(8,128)(2,1)}, bf16[256,128]{1,0:T(8,128)(2,1)}, bf16[256,128]{1,0:T(8,128)(2,1)}) custom-call(s32[1]{0:T(128)} %bitcast.x_ref, bf16[2048,256]{1,0:T(8,128)(2,1)} %feat_ref.1, bf16[2048,256]{1,0:T(8,128)(2,1)} %feat_ref.1, bf16[512,256]{1,0:T(8,128)(2,1)} %bitcast.8, ...), custom_call_target="tpu_custom_call" | custom-call | tf_op jit(solution)/shard_map/attention/pallas_call | solution.py:211
  190.4 0.6 collective-permute-start.6
  191.0 3.6 %collective-permute-start.7 = (bf16[256,128]{1,0:T(8,128)(2,1)}, bf16[256,128]{1,0:T(8,128)(2,1)S(1)}, u32[]{:S(2)}, u32[]{:S(2)}) collective-permute-start(bf16[256,128]{1,0:T(8,128)(2,1)} %get-tuple-element.16), channel_id=1, source_target_pairs={{0,2},{1,3},{2,0},{3,1},{4,6},{5,7},{6,4},{7,5},{8,10},{9,11},{10,... | collective-permute-start | bytes 196616 | tf_op jit(solution)/shard_map/ppermute | solution.py:139
  194.7 0.7 convolution_convert_fusion
  195.4 1.5 collective-permute-done.6.refs_1_
  196.8 1.0 collective-permute-done.7.refs_2_
  197.8 1.3 collective-permute-done.8.refs_3_
  199.1 0.6 copy-done.11
  199.7 1.9 assemble.1
  201.7 1.9 copy.33
  (49 shorter events, 0.4 us)
Async XLA Ops:
  0.6 34.0 %copy-start = (s32[2048,16]{0,1:T(8,128)S(1)}, s32[2048,16]{0,1:T(8,128)}, u32[]{:S(2)}) copy-start(s32[2048,16]{0,1:T(8,128)} %param.15) | copy-start | bytes 393220
  5.0 157.7 %collective-permute-start.3 = (bf16[256,256]{1,0:T(8,128)(2,1)}, bf16[256,256]{1,0:T(8,128)(2,1)S(1)}, u32[]{:S(2)}, u32[]{:S(2)}) collective-permute-start(bf16[256,256]{1,0:T(8,128)(2,1)} %pad_maximum_fusion.refs_12_.pack_ref), channel_id=1, source_target_pairs={{0,1},{1,2},{2,3},{3,0},{4,5},{5,6},{6,7},{7,4},{8,9},{9,10},{10,1... | collective-permute-start | bytes 393224 | tf_op jit(solution)/shard_map/ppermute | solution.py:133
  6.5 155.0 %collective-permute-start.4 = (bf16[256,256]{1,0:T(8,128)(2,1)}, bf16[256,256]{1,0:T(8,128)(2,1)S(1)}, u32[]{:S(2)}, u32[]{:S(2)}) collective-permute-start(bf16[256,256]{1,0:T(8,128)(2,1)} %pad_maximum_fusion.refs_12_.pack_ref), channel_id=1, source_target_pairs={{0,2},{1,3},{2,0},{3,1},{4,6},{5,7},{6,4},{7,5},{8,10},{9,11},{10,... | collective-permute-start | bytes 393224 | tf_op jit(solution)/shard_map/ppermute | solution.py:133
  9.2 150.2 %collective-permute-start.5 = (bf16[256,256]{1,0:T(8,128)(2,1)}, bf16[256,256]{1,0:T(8,128)(2,1)S(1)}, u32[]{:S(2)}, u32[]{:S(2)}) collective-permute-start(bf16[256,256]{1,0:T(8,128)(2,1)} %pad_maximum_fusion.refs_12_.pack_ref), channel_id=1, source_target_pairs={{0,3},{1,0},{2,1},{3,2},{4,7},{5,4},{6,5},{7,6},{8,11},{9,8},{10,9... | collective-permute-start | bytes 393224 | tf_op jit(solution)/shard_map/ppermute | solution.py:133
  14.2 33.3 %all-to-all-start = ((s32[64,1,128]{2,1,0:T(1,128)}), s32[64,1,128]{2,1,0:T(1,128)S(1)}, u32[]{:S(2)}, u32[]{:S(2)}) async-start(s32[64,1,128]{2,1,0:T(1,128)} %wanted_rows.1), calls=%async_computation | async-start | bytes 65536 | tf_op jit(solution)/shard_map/all_to_all | solution.py:170
  30.8 1.4 collective-permute-start.9
  33.1 3.6 %collective-permute-start.10 = (f32[8,128]{1,0:T(8,128)S(1)}, f32[8,128]{1,0:T(8,128)S(1)}, u32[]{:S(2)}, u32[]{:S(2)}) collective-permute-start(f32[8,128]{1,0:T(8,128)S(1)} %add_select_fusion.5), channel_id=1, source_target_pairs={{0,8},{4,12},{8,0},{12,4},{16,24},{20,28},{24,16},{28,20},{32,40},... | collective-permute-start | bytes 12296 | tf_op jit(solution)/shard_map/ppermute | solution.py:147
  37.1 8.8 %collective-permute-start.11 = (f32[8,128]{1,0:T(8,128)S(1)}, f32[8,128]{1,0:T(8,128)S(1)}, u32[]{:S(2)}, u32[]{:S(2)}) collective-permute-start(f32[8,128]{1,0:T(8,128)S(1)} %add_select_fusion.4), channel_id=1, source_target_pairs={{0,16},{4,20},{8,24},{12,28},{16,0},{20,4},{24,8},{28,12},{32,48},... | collective-permute-start | bytes 12296 | tf_op jit(solution)/shard_map/ppermute | solution.py:147
  46.2 44.6 %collective-permute-start.12 = (f32[8,128]{1,0:T(8,128)S(1)}, f32[8,128]{1,0:T(8,128)S(1)}, u32[]{:S(2)}, u32[]{:S(2)}) collective-permute-start(f32[8,128]{1,0:T(8,128)S(1)} %add_select_fusion.3), channel_id=1, source_target_pairs={{0,32},{4,36},{8,40},{12,44},{16,48},{20,52},{24,56},{28,60},{32,0... | collective-permute-start | bytes 12296 | tf_op jit(solution)/shard_map/ppermute | solution.py:147
  47.5 0.6 copy-start.8
  82.2 36.9 %copy-start.12 = (bf16[4,256]{1,0:T(4,128)(2,1)S(1)}, bf16[4,256]{1,0:T(4,128)(2,1)}, u32[]{:S(2)}) copy-start(bf16[4,256]{1,0:T(4,128)(2,1)} %param.9) | copy-start | bytes 6148
  82.2 40.9 %all-to-all-start.1 = ((bf16[64,32,256]{2,1,0:T(8,128)(2,1)}), bf16[64,32,256]{2,1,0:T(8,128)(2,1)S(1)}, u32[]{:S(2)}, u32[]{:S(2)}) async-start(bf16[64,32,256]{2,1,0:T(8,128)(2,1)} %gather_send.1), calls=%async_computation.1 | async-start | bytes 2097152 | tf_op jit(solution)/shard_map/all_to_all | solution.py:190
  91.1 23.6 %collective-permute-start.13 = (f32[8,128]{1,0:T(8,128)S(1)}, f32[8,128]{1,0:T(8,128)S(1)}, u32[]{:S(2)}, u32[]{:S(2)}) collective-permute-start(f32[8,128]{1,0:T(8,128)S(1)} %add_select_fusion.2), channel_id=1, source_target_pairs={{0,64},{4,68},{8,72},{12,76},{16,80},{20,84},{24,88},{28,92},{32,9... | collective-permute-start | bytes 12296 | tf_op jit(solution)/shard_map/ppermute | solution.py:147
  115.0 7.5 %collective-permute-start.14 = (f32[8,128]{1,0:T(8,128)S(1)}, f32[8,128]{1,0:T(8,128)S(1)}, u32[]{:S(2)}, u32[]{:S(2)}) collective-permute-start(f32[8,128]{1,0:T(8,128)S(1)} %add_select_fusion.1), channel_id=1, source_target_pairs={{0,128},{4,132},{8,136},{12,140},{16,144},{20,148},{24,152},{28,15... | collective-permute-start | bytes 12296 | tf_op jit(solution)/shard_map/ppermute | solution.py:147
  123.1 1.0 copy-start.1
  157.9 13.1 %collective-permute-start = (bf16[16,32,256]{2,1,0:T(8,128)(2,1)}, bf16[16,32,256]{2,1,0:T(8,128)(2,1)S(1)}, u32[]{:S(2)}, u32[]{:S(2)}) collective-permute-start(bf16[16,32,256]{2,1,0:T(8,128)(2,1)} %get-tuple-element.11), channel_id=1, source_target_pairs={{0,1},{1,2},{2,3},{3,0},{4,5},{5,6},{6,7},{7,4},{8,9},{9,10},{10,1... | collective-permute-start | bytes 786440 | tf_op jit(solution)/shard_map/ppermute | solution.py:139
  158.5 12.4 %collective-permute-start.1 = (bf16[16,32,256]{2,1,0:T(8,128)(2,1)}, bf16[16,32,256]{2,1,0:T(8,128)(2,1)S(1)}, u32[]{:S(2)}, u32[]{:S(2)}) collective-permute-start(bf16[16,32,256]{2,1,0:T(8,128)(2,1)} %get-tuple-element.12), channel_id=1, source_target_pairs={{0,2},{1,3},{2,0},{3,1},{4,6},{5,7},{6,4},{7,5},{8,10},{9,11},{10,... | collective-permute-start | bytes 786440 | tf_op jit(solution)/shard_map/ppermute | solution.py:139
  159.4 12.2 %copy-start.7 = (bf16[256,256]{1,0:T(8,128)(2,1)}, bf16[256,256]{1,0:T(8,128)(2,1)S(1)}, u32[]{:S(2)}) copy-start(bf16[256,256]{1,0:T(8,128)(2,1)S(1)} %collective-permute-done.5.refs_15_) | copy-start | bytes 393220
  159.4 12.2 %collective-permute-start.2 = (bf16[16,32,256]{2,1,0:T(8,128)(2,1)}, bf16[16,32,256]{2,1,0:T(8,128)(2,1)S(1)}, u32[]{:S(2)}, u32[]{:S(2)}) collective-permute-start(bf16[16,32,256]{2,1,0:T(8,128)(2,1)} %get-tuple-element.13), channel_id=1, source_target_pairs={{0,3},{1,0},{2,1},{3,2},{4,7},{5,4},{6,5},{7,6},{8,11},{9,8},{10,9... | collective-permute-start | bytes 786440 | tf_op jit(solution)/shard_map/ppermute | solution.py:139
  161.5 10.1 %copy-start.6 = (bf16[256,256]{1,0:T(8,128)(2,1)}, bf16[256,256]{1,0:T(8,128)(2,1)S(1)}, u32[]{:S(2)}) copy-start(bf16[256,256]{1,0:T(8,128)(2,1)S(1)} %collective-permute-done.4.refs_14_) | copy-start | bytes 393220
  161.5 33.1 %collective-permute-start.17 = (bf16[4,128]{1,0:T(4,128)(2,1)S(1)}, bf16[4,128]{1,0:T(4,128)(2,1)S(1)}, u32[]{:S(2)}, u32[]{:S(2)}) collective-permute-start(bf16[4,128]{1,0:T(4,128)(2,1)S(1)} %select_convert_fusion), channel_id=1, source_target_pairs={{0,3},{1,0},{2,1},{3,2},{4,7},{5,4},{6,5},{7,6},{8,11},{9,8},{10,9... | collective-permute-start | bytes 3080 | tf_op jit(solution)/shard_map/ppermute | solution.py:133
  162.7 8.9 %copy-start.5 = (bf16[256,256]{1,0:T(8,128)(2,1)}, bf16[256,256]{1,0:T(8,128)(2,1)S(1)}, u32[]{:S(2)}) copy-start(bf16[256,256]{1,0:T(8,128)(2,1)S(1)} %collective-permute-done.3.refs_13_) | copy-start | bytes 393220
  162.7 31.9 %collective-permute-start.16 = (bf16[4,128]{1,0:T(4,128)(2,1)S(1)}, bf16[4,128]{1,0:T(4,128)(2,1)S(1)}, u32[]{:S(2)}, u32[]{:S(2)}) collective-permute-start(bf16[4,128]{1,0:T(4,128)(2,1)S(1)} %select_convert_fusion), channel_id=1, source_target_pairs={{0,2},{1,3},{2,0},{3,1},{4,6},{5,7},{6,4},{7,5},{8,10},{9,11},{10,... | collective-permute-start | bytes 3080 | tf_op jit(solution)/shard_map/ppermute | solution.py:133
  171.0 0.7 copy-start.2
  171.0 23.7 %collective-permute-start.15 = (bf16[4,128]{1,0:T(4,128)(2,1)S(1)}, bf16[4,128]{1,0:T(4,128)(2,1)S(1)}, u32[]{:S(2)}, u32[]{:S(2)}) collective-permute-start(bf16[4,128]{1,0:T(4,128)(2,1)S(1)} %select_convert_fusion), channel_id=1, source_target_pairs={{0,1},{1,2},{2,3},{3,0},{4,5},{5,6},{6,7},{7,4},{8,9},{9,10},{10,1... | collective-permute-start | bytes 3080 | tf_op jit(solution)/shard_map/ppermute | solution.py:133
  171.0 0.8 copy-start.3
  171.6 0.7 copy-start.4
  190.4 6.4 %collective-permute-start.6 = (bf16[256,128]{1,0:T(8,128)(2,1)}, bf16[256,128]{1,0:T(8,128)(2,1)S(1)}, u32[]{:S(2)}, u32[]{:S(2)}) collective-permute-start(bf16[256,128]{1,0:T(8,128)(2,1)} %get-tuple-element.15), channel_id=1, source_target_pairs={{0,1},{1,2},{2,3},{3,0},{4,5},{5,6},{6,7},{7,4},{8,9},{9,10},{10,1... | collective-permute-start | bytes 196616 | tf_op jit(solution)/shard_map/ppermute | solution.py:139
  191.0 6.8 %collective-permute-start.7 = (bf16[256,128]{1,0:T(8,128)(2,1)}, bf16[256,128]{1,0:T(8,128)(2,1)S(1)}, u32[]{:S(2)}, u32[]{:S(2)}) collective-permute-start(bf16[256,128]{1,0:T(8,128)(2,1)} %get-tuple-element.16), channel_id=1, source_target_pairs={{0,2},{1,3},{2,0},{3,1},{4,6},{5,7},{6,4},{7,5},{8,10},{9,11},{10,... | collective-permute-start | bytes 196616 | tf_op jit(solution)/shard_map/ppermute | solution.py:139
  194.6 4.5 %collective-permute-start.8 = (bf16[256,128]{1,0:T(8,128)(2,1)}, bf16[256,128]{1,0:T(8,128)(2,1)S(1)}, u32[]{:S(2)}, u32[]{:S(2)}) collective-permute-start(bf16[256,128]{1,0:T(8,128)(2,1)} %get-tuple-element.17), channel_id=1, source_target_pairs={{0,3},{1,0},{2,1},{3,2},{4,7},{5,4},{6,5},{7,6},{8,11},{9,8},{10,9... | collective-permute-start | bytes 196616 | tf_op jit(solution)/shard_map/ppermute | solution.py:139
  196.8 2.3 %copy-start.9 = (bf16[256,128]{1,0:T(8,128)(2,1)}, bf16[256,128]{1,0:T(8,128)(2,1)S(1)}, u32[]{:S(2)}) copy-start(bf16[256,128]{1,0:T(8,128)(2,1)S(1)} %collective-permute-done.6.refs_1_) | copy-start | bytes 196612
  197.8 1.3 copy-start.10
  199.1 0.6 copy-start.11

commit v2 on v1

v2 whole, which is shorter than its diff:
```python
import math

import jax
import jax.numpy as jnp
from jax import lax
from jax.experimental import pallas as pl
from jax.experimental.pallas import tpu as pltpu
from jax.sharding import PartitionSpec as P

D = 256
H = 8
TILE = 128
G = 4
HEAD = D // H
REP = 4
PEERS = 64
WIDTH = D // REP
QUARTER = TILE // REP
SCORE_SCALE = 1.0 / math.sqrt(HEAD)
EXP2_SCALE = SCORE_SCALE * math.log2(math.e)
NEG = -1e30
NT = (((1,), (1,)), ((), ()))
NN = (((1,), (0,)), ((), ()))

SMEM = pl.BlockSpec(memory_space=pltpu.SMEM)
VMEM = pl.BlockSpec(memory_space=pltpu.VMEM)
CHUNKS = 2
PER_CHUNK = 4 // CHUNKS
SLOTS = 4 * PER_CHUNK
NODES_CHUNK = TILE * PER_CHUNK
BF16 = jnp.bfloat16


def dot(a, b, dims=NN, precision=None):
    return lax.dot_general(a, b, dims, precision=precision, preferred_element_type=jnp.float32)


def in_vmem(value):
    return pltpu.with_memory_space_constraint(value, pltpu.VMEM)


def vmem_out(shape, dtype):
    return pltpu.VMEM(shape, dtype)


def params(mib):
    return pltpu.CompilerParams(vmem_limit_bytes=mib * 1024 * 1024)


def wanted_rows_kernel(map_ref, out_ref):
    def put(s, carry):
        block = map_ref[s % 4, s // 4]
        out_ref[block // 16] = jnp.full((1, TILE), block % 16, jnp.int32)
        return carry

    lax.fori_loop(0, PEERS, put, 0, unroll=8)


def gather_send_kernel(x_ref, want_ref, feat_ref, out_ref, want_smem, sem):
    copy = pltpu.make_async_copy(want_ref, want_smem, sem)
    copy.start()
    copy.wait()

    def put(e, carry):
        out_ref[e] = feat_ref[want_smem[e, 0, 0] * REP + x_ref[0]]
        return carry

    lax.fori_loop(0, PEERS, put, 0, unroll=8)


def gather_rep_kernel(x_ref, map_ref, arrived_ref, state_ref, *outs):
    for k in range(CHUNKS):
        for d in range(REP):
            column = ((x_ref[0] + d) % REP) * 4 + k * PER_CHUNK
            for j in range(SLOTS):
                owner = map_ref[j % 4, column + j // 4] // 16
                outs[k * REP + d][j] = arrived_ref[owner]
    for e in range(PEERS):
        outs[-1][e] = state_ref[...]


def prepare_kernel(x_ref, feat_ref, pack_ref, vs_ref, links_ref, state_ref, bias_ref):
    kv = dot(feat_ref[...], pack_ref[:TILE, :], NT).astype(BF16)
    q = dot(vs_ref[...], pack_ref[TILE:, :], NT).astype(BF16)
    lane = lax.broadcasted_iota(jnp.int32, (2 * G, TILE), 1)
    row = lax.broadcasted_iota(jnp.int32, (2 * G, TILE), 0)
    first = WIDTH + HEAD * (row // G)
    q = jnp.where((lane >= first) & (lane < first + HEAD), q.astype(jnp.float32), 0.0).astype(BF16)
    s = dot(q, kv, NT)
    top = jnp.max(s, axis=1, keepdims=True)
    p = jnp.exp2((s - top) * EXP2_SCALE)
    total = jnp.sum(p, axis=1, keepdims=True)
    w = dot(p, kv.astype(jnp.float32), NN, lax.Precision.HIGHEST)
    state_ref[...] = jnp.where(lane < 64, w, jnp.where(lane < 96, total, top))
    column = lax.broadcasted_iota(jnp.int32, (TILE, TILE), 0)
    for c in range(4):
        first = pl.multiple_of(x_ref[0] * 512 + c * TILE, TILE)
        links = links_ref[:, pl.ds(first, TILE)]
        linked = column == links[0:1, :]
        for n in range(1, 16):
            linked = linked | (column == links[n : n + 1, :])
        bias_ref[c * TILE : (c + 1) * TILE, :] = jnp.where(linked, 0.0, NEG).T


def attention_rows(own, source, bias, packs):
    lane = lax.broadcasted_iota(jnp.int32, (TILE, TILE), 1)
    virtual_bias = jnp.where(lax.broadcasted_iota(jnp.int32, (1, TILE), 1) < G, 0.0, NEG)
    groups = []
    for g in range(REP):
        kv = dot(source, packs[g][:TILE, :], NT).astype(BF16)
        q = dot(own, packs[g][TILE:, :], NT)
        q0 = jnp.where((lane >= WIDTH) & (lane < WIDTH + HEAD), q, 0.0)
        q1 = jnp.where(lane >= WIDTH + HEAD, q, 0.0)
        picked = []
        for qh in (q0, q1):
            s = dot(qh.astype(BF16), kv, NT)
            s = jnp.concatenate([s[:, :TILE] + bias, s[:, TILE : 5 * TILE], s[:, 5 * TILE :] + virtual_bias], axis=1)
            top = jnp.max(s, axis=1, keepdims=True)
            p = jnp.exp2((s - top) * EXP2_SCALE)
            total = jnp.sum(p, axis=1, keepdims=True)
            o = dot(p.astype(BF16), kv)
            picked.append(o * (1.0 / total))
        o = jnp.where(lane < HEAD, picked[0], jnp.where(lane < WIDTH, picked[1], 0.0))
        groups.append(o.astype(BF16))
    return jnp.concatenate(groups, axis=1)


def attention_kernel(chunk, x_ref, feat_ref, *refs):
    ns, refs = refs[:REP], refs[REP:]
    bias_ref, refs = refs[0], refs[1:]
    packs, refs = refs[:REP], refs[REP:]
    vs_ref, refs = refs[0], refs[1:]
    if chunk == CHUNKS - 1:
        states_ref, refs = refs[0], refs[1:]
    outs, scratch = refs[:REP], refs[REP]
    rows = []
    for i in range(PER_CHUNK):
        c = chunk * PER_CHUNK + i
        own = feat_ref[pl.ds(pl.multiple_of(x_ref[0] * 512 + c * TILE, TILE), TILE), :]
        near = [n[4 * i : 4 * i + 4].reshape(TILE, D) for n in ns]
        source = jnp.concatenate([own, *near, vs_ref[...]], axis=0)
        rows.append(attention_rows(own, source, bias_ref[c * TILE : (c + 1) * TILE, :], packs))
    w = jnp.concatenate([p[TILE:, :] for p in packs], axis=0)
    scratch[...] = dot(jnp.concatenate(rows, axis=0), w).T
    for d in range(REP):
        first = pl.multiple_of(((x_ref[0] + d) % REP) * WIDTH, WIDTH)
        outs[d][:WIDTH, :] = scratch[pl.ds(first, WIDTH), :].astype(BF16)
    if chunk == CHUNKS - 1:
        states = states_ref[...]
        top = jnp.max(states[:, :, 96:97], axis=0, keepdims=True)
        joined = jnp.sum(states * jnp.exp2((states[:, :, 96:97] - top) * EXP2_SCALE), axis=0)
        heads = joined * (1.0 / joined[:, WIDTH : WIDTH + 1])
        lane = lax.broadcasted_iota(jnp.int32, (G, TILE), 1)
        heads = jnp.where(lane < HEAD, heads[:G], jnp.where(lane < WIDTH, heads[G:], 0.0))
        heads = jnp.concatenate([heads, jnp.zeros((G, TILE), jnp.float32)], axis=0)
        heads = jnp.concatenate([heads, jnp.zeros((2 * G, NODES_CHUNK - TILE), jnp.float32)], axis=1)
        for d in range(REP):
            outs[d][WIDTH:, :] = heads.astype(BF16)


def assemble_kernel(x_ref, *refs):
    pieces, refs = refs[: REP * CHUNKS], refs[REP * CHUNKS :]
    packs, (out_ref, virtual_ref, scratch) = refs[:REP], refs[REP:]
    total = jnp.zeros((2 * G, D), jnp.float32)
    for d in range(REP):
        first = pl.multiple_of(((x_ref[0] + REP - d) % REP) * 512, 512)
        for k in range(CHUNKS):
            out_ref[:, pl.ds(first + k * NODES_CHUNK, NODES_CHUNK)] = pieces[k * REP + d][:WIDTH, :]
        total = total + dot(pieces[(CHUNKS - 1) * REP + d][WIDTH:, :TILE], packs[d][TILE:, :])
    scratch[...] = total.T
    virtual_ref[...] = scratch[pl.ds(pl.multiple_of(x_ref[0] * WIDTH, WIDTH), WIDTH), :].astype(BF16)


def send_rep(values, name):
    with jax.named_scope(name):
        return [values[0]] + [
            lax.ppermute(values[d], "rep", [(i, (i + d) % REP) for i in range(REP)]) for d in range(1, REP)
        ]


def shards(features, virtual_state, w_query, w_key, w_value, w_out, tile_map, local_nbr):
    x = lax.axis_index("rep")
    x_one = x.astype(jnp.int32).reshape(1)
    map_t = tile_map.T

    wanted_from = pl.pallas_call(
        wanted_rows_kernel,
        out_shape=vmem_out((PEERS, 1, TILE), jnp.int32),
        in_specs=[SMEM],
        out_specs=VMEM,
        compiler_params=params(2),
        name="wanted_rows",
    )(map_t)
    with jax.named_scope("exchange_index"):
        wanted = lax.all_to_all(wanted_from, "nodes", 0, 0, tiled=True)

    pack = jnp.concatenate([w_value.T, w_key.T, w_out, w_query.T], axis=0)
    packs = [in_vmem(p) for p in send_rep([pack] * REP, "exchange_pack")]

    state, bias = pl.pallas_call(
        prepare_kernel,
        out_shape=[vmem_out((2 * G, TILE), jnp.float32), vmem_out((512, TILE), jnp.float32)],
        in_specs=[SMEM] + [VMEM] * 4,
        out_specs=[VMEM] * 2,
        compiler_params=params(16),
        name="prepare",
    )(x_one, in_vmem(features), in_vmem(pack), jnp.concatenate([virtual_state, virtual_state], axis=0), in_vmem(local_nbr.T))

    outgoing = pl.pallas_call(
        gather_send_kernel,
        out_shape=vmem_out((PEERS, QUARTER, D), BF16),
        in_specs=[SMEM, VMEM, VMEM],
        out_specs=VMEM,
        scratch_shapes=[pltpu.SMEM((PEERS, 1, TILE), jnp.int32), pltpu.SemaphoreType.DMA],
        compiler_params=params(2),
        name="gather_send",
    )(x_one, in_vmem(wanted), in_vmem(features.reshape(PEERS, QUARTER, D)))
    with jax.named_scope("exchange_features"):
        arrived = lax.all_to_all(outgoing, "nodes", 0, 0, tiled=True)

    sends = pl.pallas_call(
        gather_rep_kernel,
        out_shape=[vmem_out((SLOTS, QUARTER, D), BF16)] * (CHUNKS * REP) + [vmem_out((PEERS, 2 * G, TILE), jnp.float32)],
        in_specs=[SMEM, SMEM, VMEM, VMEM],
        out_specs=[VMEM] * (CHUNKS * REP + 1),
        compiler_params=params(2),
        name="gather_rep",
    )(x_one, map_t, in_vmem(arrived), in_vmem(state))
    pieces = [send_rep(sends[k * REP : k * REP + REP], f"exchange_rep{k}") for k in range(CHUNKS)]
    with jax.named_scope("exchange_virtual"):
        states = lax.all_to_all(sends[-1], "nodes", 0, 0, tiled=True)

    virtual_rows = jnp.pad(virtual_state, ((0, TILE - G), (0, 0)))
    received = []
    for k in range(CHUNKS):
        last = k == CHUNKS - 1
        height = WIDTH + (2 * G if last else 0)
        args = [x_one, in_vmem(features), *map(in_vmem, pieces[k]), bias, *packs, in_vmem(virtual_rows)]
        args += [in_vmem(states)] if last else []
        outs = pl.pallas_call(
            lambda *refs, k=k: attention_kernel(k, *refs),
            out_shape=[vmem_out((height, NODES_CHUNK), BF16)] * REP,
            in_specs=[SMEM] + [VMEM] * (len(args) - 1),
            out_specs=[VMEM] * REP,
            scratch_shapes=[pltpu.VMEM((D, NODES_CHUNK), jnp.float32)],
            compiler_params=params(24),
            name=f"attention{k}",
        )(*args)
        received += send_rep(outs, f"exchange_out{k}")
    node_out, virtual_out = pl.pallas_call(
        assemble_kernel,
        out_shape=[jax.ShapeDtypeStruct((WIDTH, 2048), BF16), jax.ShapeDtypeStruct((WIDTH, 2 * G), BF16)],
        in_specs=[SMEM] + [VMEM] * (REP * CHUNKS + REP),
        out_specs=[VMEM] * 2,
        scratch_shapes=[pltpu.VMEM((D, 2 * G), jnp.float32)],
        compiler_params=params(4),
        name="assemble",
    )(x_one, *map(in_vmem, received), *packs)
    return node_out.T, virtual_out[:, :G].T


def solution(mesh):
    in_specs = (
        P("nodes", None),
        P(),
        P(None, "rep"),
        P(None, "rep"),
        P(None, "rep"),
        P("rep", None),
        P("nodes", None),
        P("nodes", None),
    )
    out_specs = (P("nodes", "rep"), P(None, "rep"))
    return jax.shard_map(shards, mesh=mesh, in_specs=in_specs, out_specs=out_specs, check_vma=False)
```

time: 205 us -> 119 us (0.58)
  Pallas kernels: 93.5 us -> 24.6 us
  other arithmetic: 11.3 us -> 0.02 us
  local copies, waits for them, and re-layouts: 11.4 us -> 4.12 us
  waiting for transfers between devices: 37.5 us -> 40.8 us
    pallas_call x6 -> x7, Pallas kernels: 93.5 us -> 24.6 us  [the longest x2 16 us: shards(): pl.pallas_call(lambda *refs, k=k: attention_kernel(k, *refs), out_shape=[...]
    ppermute x12 -> x0, waiting for transfers between devices: 26.6 us -> none  [the longest x6 26.5 us: merged_virtual(): other = lax.ppermute(state, 'nodes', [(i, i ^ bit) for i in range(PEERS)])]
    all_to_all x1, waiting for transfers between devices: 0.01 us -> 25.2 us  [shards(): arrived = lax.all_to_all(outgoing, 'nodes', 0, 0, tiled=True)]
    ppermute x12 -> x0, starting transfers between devices: 20.1 us -> none  [the longest x6 11.7 us: merged_virtual(): other = lax.ppermute(state, 'nodes', [(i, i ^ bit) for i in range(PEERS)])]
    ppermute x6 -> x15, starting transfers between devices: 7.9 us -> 24.1 us  [send_rep(): lax.ppermute(values[d], 'rep', [(i, (i + d) % REP) for i in range(REP)])]
    all_to_all x1, waiting for transfers between devices: 0.01 us -> 8.57 us  [shards(): wanted = lax.all_to_all(wanted_from, 'nodes', 0, 0, tiled=True)]
    all_to_all x0 -> x1, starting transfers between devices: none -> 6.72 us  [shards(): states = lax.all_to_all(sends[-1], 'nodes', 0, 0, tiled=True)]
    reduce_or x1 -> x0, other arithmetic: 5.77 us -> none  [shards(): jnp.any(own_links[:, :, None] == jnp.arange(TILE, dtype=jnp.int32), axis=1)]
  transfers between devices with their start and end apart: 20 -> 18, of which waited for: 9 -> 6; matrix products, arithmetic and copies ran while one was open for 7% -> 0% of each run, Pallas kernels for 45% -> 15%
where the time goes in v2:
time: 119 us
  starting transfers between devices  48.3 us (41%)
  waiting for transfers between devices  40.8 us (34%)
  Pallas kernels  24.6 us (21%)
  local copies, waits for them, and re-layouts  4.12 us (3%)
    all_to_all x1, waiting for transfers between devices, shards(): arrived = lax.all_to_all(outgoing, 'nodes', 0, 0, tiled=True)  25.2 us
    ppermute x15, starting transfers between devices, send_rep(): lax.ppermute(values[d], 'rep', [(i, (i + d) % REP) for i in range(REP)])  24.1 us
    pallas_call x2, Pallas kernels, shards(): pl.pallas_call(lambda *refs, k=k: attention_kernel(k, *refs), out_shape=[...  16 us
    all_to_all x1, starting transfers between devices, shards(): wanted = lax.all_to_all(wanted_from, 'nodes', 0, 0, tiled=True)  11.8 us
    all_to_all x1, waiting for transfers between devices, shards(): wanted = lax.all_to_all(wanted_from, 'nodes', 0, 0, tiled=True)  8.57 us
    ppermute x15, waiting for transfers between devices, send_rep(): lax.ppermute(values[d], 'rep', [(i, (i + d) % REP) for i in range(REP)])  7.02 us
    all_to_all x1, starting transfers between devices, shards(): states = lax.all_to_all(sends[-1], 'nodes', 0, 0, tiled=True)  6.72 us
    all_to_all x1, starting transfers between devices, shards(): arrived = lax.all_to_all(outgoing, 'nodes', 0, 0, tiled=True)  5.71 us
  transfers between devices with their start and end apart: 18, of which 6 were waited for; matrix products, arithmetic and copies ran while one was open for 0% of the time, Pallas kernels for 15%

profile of v2, /device:TPU:32, one launch (start us, length us, event | category | flops | bytes accessed | tf_op | source)
XLA Modules:
  0.0 118.7 jit_solution(15175205147952463399)
XLA Ops:
  0.6 0.0 copy-start.3
  0.6 0.7 copy-done.3
  1.3 2.0 %wanted_rows.1 = s32[64,1,128]{2,1,0:T(1,128)} custom-call(s32[4,16]{1,0:T(4,128)S(1)} %bitcast.12), custom_call_target="tpu_custom_call" | custom-call | tf_op jit(solution)/shard_map/wanted_rows/pallas_call | solution.py:186
  3.3 11.8 %all-to-all-start = ((s32[64,1,128]{2,1,0:T(1,128)}), s32[64,1,128]{2,1,0:T(1,128)S(1)}, u32[]{:S(2)}, u32[]{:S(2)}) async-start(s32[64,1,128]{2,1,0:T(1,128)} %wanted_rows.1), calls=%async_computation | async-start | bytes 65536 | tf_op jit(solution)/shard_map/exchange_index/all_to_all | solution.py:195
  15.1 8.6 %all-to-all-done.want_ref = s32[64,1,128]{2,1,0:T(1,128)S(1)} async-done(((s32[64,1,128]{2,1,0:T(1,128)}), s32[64,1,128]{2,1,0:T(1,128)S(1)}, u32[]{:S(2)}, u32[]{:S(2)}) %all-to-all-start) | async-done | bytes 32800 | tf_op jit(solution)/shard_map/exchange_index/all_to_all | solution.py:195
  23.7 1.2 %copy-done = bf16[2048,256]{1,0:T(8,128)(2,1)S(1)} copy-done((bf16[2048,256]{1,0:T(8,128)(2,1)S(1)}, bf16[2048,256]{1,0:T(8,128)(2,1)}, u32[]{:S(2)}) %copy-start) | copy-done | bytes 1048600
  24.9 2.2 %gather_send.1 = bf16[64,32,256]{2,1,0:T(8,128)(2,1)} custom-call(s32[1]{0:T(128)} %bitcast.x_ref.refs_0_, s32[64,1,128]{2,1,0:T(1,128)S(1)} %all-to-all-done.want_ref, bf16[64,32,256]{2,1,0:T(8,128)(2,1)S(1)} %bitcast.10), custom_call_target="tpu_custom_call" | custom-call | tf_op jit(solution)/shard_map/gather_send/pallas_call | solution.py:209
  27.1 0.0 copy-start.11
  27.1 0.0 copy-start.7
  27.1 0.0 copy-start.8
  27.1 0.0 copy-start.9
  27.1 0.0 copy-start.10
  27.2 0.0 copy-start.1
  27.2 5.7 %all-to-all-start.1 = ((bf16[64,32,256]{2,1,0:T(8,128)(2,1)}), bf16[64,32,256]{2,1,0:T(8,128)(2,1)S(1)}, u32[]{:S(2)}, u32[]{:S(2)}) async-start(bf16[64,32,256]{2,1,0:T(8,128)(2,1)} %gather_send.1), calls=%async_computation.1 | async-start | bytes 2097152 | tf_op jit(solution)/shard_map/exchange_features/all_to_all | solution.py:219
  32.9 0.0 copy-done.11
  32.9 0.0 copy-done.7
  32.9 0.0 copy-done.8
  32.9 0.0 copy-done.9
  32.9 0.0 copy-done.10
  33.0 0.0 copy-start.2
  33.0 0.0 copy-done.1
  33.0 0.9 copy-done.2
  33.9 1.8 %prepare.1 = (f32[8,128]{1,0:T(8,128)S(1)}, f32[512,128]{1,0:T(8,128)S(1)}) custom-call(s32[1]{0:T(128)} %bitcast.x_ref.refs_0_, bf16[2048,256]{1,0:T(8,128)(2,1)S(1)} %copy-done.1, bf16[256,256]{1,0:T(8,128)(2,1)S(1)} %pad_maximum_fusion.pack_ref.refs_7_.refs_8_, bf16[8,256]{1,0:T(8,128)(2,1)S(1)} %pad_maximum_fusion.1.vs_ref, s32[16,2048]{1,0:T(8,128)S(1)} %bitcast.11), custom_call_target="tpu_custom_call" | custom-call | tf_op jit(solution)/shard_map/prepare/pallas_call | solution.py:200
  35.6 25.2 %all-to-all-done.1.arrived_ref = bf16[64,32,256]{2,1,0:T(8,128)(2,1)S(1)} async-done(((bf16[64,32,256]{2,1,0:T(8,128)(2,1)}), bf16[64,32,256]{2,1,0:T(8,128)(2,1)S(1)}, u32[]{:S(2)}, u32[]{:S(2)}) %all-to-all-start.1) | async-done | bytes 1048608 | tf_op jit(solution)/shard_map/exchange_features/all_to_all | solution.py:219
  60.9 0.0 copy-done.4
  60.9 1.7 %gather_rep.1 = (bf16[8,32,256]{2,1,0:T(8,128)(2,1)S(1)}, bf16[8,32,256]{2,1,0:T(8,128)(2,1)S(1)}, bf16[8,32,256]{2,1,0:T(8,128)(2,1)}, bf16[8,32,256]{2,1,0:T(8...) custom-call(s32[1]{0:T(128)} %bitcast.x_ref.refs_0_, ...), custom_call_target="tpu_custom_call" | custom-call | tf_op jit(solution)/shard_map/gather_rep/pallas_call | solution.py:221
  62.6 0.6 copy-done.5
  63.2 6.7 %all-to-all-start.2 = ((f32[64,8,128]{2,1,0:T(8,128)}), f32[64,8,128]{2,1,0:T(8,128)S(1)}, u32[]{:S(2)}, u32[]{:S(2)}) async-start(f32[64,8,128]{2,1,0:T(8,128)} %get-tuple-element.37), calls=%async_computation.2 | async-start | bytes 524288 | tf_op jit(solution)/shard_map/exchange_virtual/all_to_all | solution.py:231
  69.9 1.6 %collective-permute-start.3 = (bf16[256,256]{1,0:T(8,128)(2,1)S(1)}, bf16[256,256]{1,0:T(8,128)(2,1)S(1)}, u32[]{:S(2)}, u32[]{:S(2)}) collective-permute-start(bf16[256,256]{1,0:T(8,128)(2,1)S(1)} %pad_maximum_fusion.pack_ref.refs_7_.refs_8_), channel_id=1, source_target_pairs={{0,1},{1,2},{2,3},{3,0},{4,5},{5,6},{6,7},{7,4},{8,9},{9,10},{10,1... | collective-permute-start | bytes 393224 | tf_op jit(solution)/shard_map/exchange_pack/ppermute | solution.py:177
  71.5 2.7 %collective-permute-start.4 = (bf16[256,256]{1,0:T(8,128)(2,1)S(1)}, bf16[256,256]{1,0:T(8,128)(2,1)S(1)}, u32[]{:S(2)}, u32[]{:S(2)}) collective-permute-start(bf16[256,256]{1,0:T(8,128)(2,1)S(1)} %pad_maximum_fusion.pack_ref.refs_7_.refs_8_), channel_id=1, source_target_pairs={{0,2},{1,3},{2,0},{3,1},{4,6},{5,7},{6,4},{7,5},{8,10},{9,11},{10,... | collective-permute-start | bytes 393224 | tf_op jit(solution)/shard_map/exchange_pack/ppermute | solution.py:177
  74.2 1.4 %collective-permute-start.5 = (bf16[256,256]{1,0:T(8,128)(2,1)S(1)}, bf16[256,256]{1,0:T(8,128)(2,1)S(1)}, u32[]{:S(2)}, u32[]{:S(2)}) collective-permute-start(bf16[256,256]{1,0:T(8,128)(2,1)S(1)} %pad_maximum_fusion.pack_ref.refs_7_.refs_8_), channel_id=1, source_target_pairs={{0,3},{1,0},{2,1},{3,2},{4,7},{5,4},{6,5},{7,6},{8,11},{9,8},{10,9... | collective-permute-start | bytes 393224 | tf_op jit(solution)/shard_map/exchange_pack/ppermute | solution.py:177
  75.7 0.0 copy-done.6
  75.7 0.6 collective-permute-start
  76.3 0.9 collective-permute-start.1
  77.1 0.0 collective-permute-done.3.refs_8_.refs_9_
  77.1 2.0 %collective-permute-start.2 = (bf16[8,32,256]{2,1,0:T(8,128)(2,1)S(1)}, bf16[8,32,256]{2,1,0:T(8,128)(2,1)S(1)}, u32[]{:S(2)}, u32[]{:S(2)}) collective-permute-start(bf16[8,32,256]{2,1,0:T(8,128)(2,1)S(1)} %get-tuple-element.27), channel_id=1, source_target_pairs={{0,3},{1,0},{2,1},{3,2},{4,7},{5,4},{6,5},{7,6},{8,11},{9,8},{10,9... | collective-permute-start | bytes 393224 | tf_op jit(solution)/shard_map/exchange_rep0/ppermute | solution.py:177
  79.1 2.2 %collective-permute-done.4.refs_9_.refs_10_ = bf16[256,256]{1,0:T(8,128)(2,1)S(1)} collective-permute-done((bf16[256,256]{1,0:T(8,128)(2,1)S(1)}, bf16[256,256]{1,0:T(8,128)(2,1)S(1)}, u32[]{:S(2)}, u32[]{:S(2)}) %collective-permute-start.4) | collective-permute-done | bytes 131104 | tf_op jit(solution)/shard_map/exchange_pack/ppermute | solution.py:177
  81.4 0.8 collective-permute-start.10
  82.1 0.0 collective-permute-done.5.refs_10_.refs_11_
  82.1 3.4 %collective-permute-start.11 = (bf16[8,32,256]{2,1,0:T(8,128)(2,1)S(1)}, bf16[8,32,256]{2,1,0:T(8,128)(2,1)S(1)}, u32[]{:S(2)}, u32[]{:S(2)}) collective-permute-start(bf16[8,32,256]{2,1,0:T(8,128)(2,1)S(1)} %get-tuple-element.36), channel_id=1, source_target_pairs={{0,3},{1,0},{2,1},{3,2},{4,7},{5,4},{6,5},{7,6},{8,11},{9,8},{10,9... | collective-permute-start | bytes 393224 | tf_op jit(solution)/shard_map/exchange_rep1/ppermute | solution.py:177
  85.6 0.0 collective-permute-done.refs_3_
  85.6 0.0 collective-permute-start.9
  85.6 1.4 %collective-permute-done.1.refs_4_ = bf16[8,32,256]{2,1,0:T(8,128)(2,1)S(1)} collective-permute-done((bf16[8,32,256]{2,1,0:T(8,128)(2,1)}, bf16[8,32,256]{2,1,0:T(8,128)(2,1)S(1)}, u32[]{:S(2)}, u32[]{:S(2)}) %collective-permute-start.1) | collective-permute-done | bytes 131104 | tf_op jit(solution)/shard_map/exchange_rep0/ppermute | solution.py:177
  87.0 0.1 collective-permute-done.2.refs_5_
  87.1 7.9 %attention0.1 = (bf16[64,256]{1,0:T(8,128)(2,1)S(1)}, bf16[64,256]{1,0:T(8,128)(2,1)S(1)}, bf16[64,256]{1,0:T(8,128)(2,1)S(1)}, bf16[64,256]{1,0:T(8,128)(2,1)S(1)}) custom-call(s32[1]{0:T(128)} %bitcast.x_ref.refs_0_, bf16[2048,256]{1,0:T(8,128)(2,1)S(1)} %copy-done.1, bf16[8,32,256]{2,1,0:T(8,128)(2,1)S(1)} %get-tuple-element.24.refs_2_, ...), custom_call_target="tpu_custom_call" | custom-call | tf_op jit(solution)/shard_map/attention0/pallas_call | solution.py:240
  95.0 2.3 %collective-permute-start.6 = (bf16[64,256]{1,0:T(8,128)(2,1)S(1)}, bf16[64,256]{1,0:T(8,128)(2,1)S(1)}, u32[]{:S(2)}, u32[]{:S(2)}) collective-permute-start(bf16[64,256]{1,0:T(8,128)(2,1)S(1)} %get-tuple-element.30), channel_id=1, source_target_pairs={{0,1},{1,2},{2,3},{3,0},{4,5},{5,6},{6,7},{7,4},{8,9},{9,10},{10,1... | collective-permute-start | bytes 98312 | tf_op jit(solution)/shard_map/exchange_out0/ppermute | solution.py:177
  97.3 0.0 collective-permute-done.10.refs_4_
  97.3 0.0 collective-permute-done.11.refs_5_
  97.3 0.0 collective-permute-done.9.refs_3_
  97.3 0.0 all-to-all-done.2.refs_12_
  97.4 8.1 %attention1.1 = (bf16[72,256]{1,0:T(8,128)(2,1)S(1)}, bf16[72,256]{1,0:T(8,128)(2,1)S(1)}, bf16[72,256]{1,0:T(8,128)(2,1)S(1)}, bf16[72,256]{1,0:T(8,128)(2,1)S(1)}) custom-call(s32[1]{0:T(128)} %bitcast.x_ref.refs_0_, bf16[2048,256]{1,0:T(8,128)(2,1)S(1)} %copy-done.1, bf16[8,32,256]{2,1,0:T(8,128)(2,1)S(1)} %get-tuple-element.33.refs_2_, ...), custom_call_target="tpu_custom_call" | custom-call | tf_op jit(solution)/shard_map/attention1/pallas_call | solution.py:240
  105.5 0.7 collective-permute-start.12
  106.2 2.9 %collective-permute-start.13 = (bf16[72,256]{1,0:T(8,128)(2,1)S(1)}, bf16[72,256]{1,0:T(8,128)(2,1)S(1)}, u32[]{:S(2)}, u32[]{:S(2)}) collective-permute-start(bf16[72,256]{1,0:T(8,128)(2,1)S(1)} %get-tuple-element.40), channel_id=1, source_target_pairs={{0,2},{1,3},{2,0},{3,1},{4,6},{5,7},{6,4},{7,5},{8,10},{9,11},{10,... | collective-permute-start | bytes 110600 | tf_op jit(solution)/shard_map/exchange_out1/ppermute | solution.py:177
  109.2 2.5 %collective-permute-start.14 = (bf16[72,256]{1,0:T(8,128)(2,1)S(1)}, bf16[72,256]{1,0:T(8,128)(2,1)S(1)}, u32[]{:S(2)}, u32[]{:S(2)}) collective-permute-start(bf16[72,256]{1,0:T(8,128)(2,1)S(1)} %get-tuple-element.41), channel_id=1, source_target_pairs={{0,3},{1,0},{2,1},{3,2},{4,7},{5,4},{6,5},{7,6},{8,11},{9,8},{10,9... | collective-permute-start | bytes 110600 | tf_op jit(solution)/shard_map/exchange_out1/ppermute | solution.py:177
  111.7 0.2 collective-permute-start.7
  111.9 0.0 collective-permute-done.6.refs_1_
  111.9 2.0 %collective-permute-start.8 = (bf16[64,256]{1,0:T(8,128)(2,1)S(1)}, bf16[64,256]{1,0:T(8,128)(2,1)S(1)}, u32[]{:S(2)}, u32[]{:S(2)}) collective-permute-start(bf16[64,256]{1,0:T(8,128)(2,1)S(1)} %get-tuple-element.32), channel_id=1, source_target_pairs={{0,3},{1,0},{2,1},{3,2},{4,7},{5,4},{6,5},{7,6},{8,11},{9,8},{10,9... | collective-permute-start | bytes 98312 | tf_op jit(solution)/shard_map/exchange_out0/ppermute | solution.py:177
  113.9 3.2 %collective-permute-done.7.refs_2_ = bf16[64,256]{1,0:T(8,128)(2,1)S(1)} collective-permute-done((bf16[64,256]{1,0:T(8,128)(2,1)S(1)}, bf16[64,256]{1,0:T(8,128)(2,1)S(1)}, u32[]{:S(2)}, u32[]{:S(2)}) %collective-permute-start.7) | collective-permute-done | bytes 32800 | tf_op jit(solution)/shard_map/exchange_out0/ppermute | solution.py:177
  117.1 0.0 collective-permute-done.8.refs_3_
  117.1 0.0 collective-permute-done.12.refs_5_
  117.1 0.0 collective-permute-done.13.refs_6_
  117.1 0.0 collective-permute-done.14.refs_7_
  117.1 0.9 assemble.1
  118.1 0.7 copy.10
  (8 shorter events, 0.0 us)
Async XLA Ops:
  0.6 0.7 copy-start.3
  3.3 20.3 %all-to-all-start = ((s32[64,1,128]{2,1,0:T(1,128)}), s32[64,1,128]{2,1,0:T(1,128)S(1)}, u32[]{:S(2)}, u32[]{:S(2)}) async-start(s32[64,1,128]{2,1,0:T(1,128)} %wanted_rows.1), calls=%async_computation | async-start | bytes 65536 | tf_op jit(solution)/shard_map/exchange_index/all_to_all | solution.py:195
  23.7 1.2 %copy-start = (bf16[2048,256]{1,0:T(8,128)(2,1)S(1)}, bf16[2048,256]{1,0:T(8,128)(2,1)}, u32[]{:S(2)}) copy-start(bf16[2048,256]{1,0:T(8,128)(2,1)} %refs_1_.3) | copy-start | bytes 3145732
  27.1 5.8 %copy-start.11 = (bf16[4,256]{1,0:T(4,128)(2,1)S(1)}, bf16[4,256]{1,0:T(4,128)(2,1)}, u32[]{:S(2)}) copy-start(bf16[4,256]{1,0:T(4,128)(2,1)} %param.9) | copy-start | bytes 6148
  27.1 5.8 %copy-start.7 = (bf16[256,64]{0,1:T(8,128)(2,1)S(1)}, bf16[256,64]{0,1:T(8,128)(2,1)}, u32[]{:S(2)}) copy-start(bf16[256,64]{0,1:T(8,128)(2,1)} %param.10) | copy-start | bytes 98308
  27.1 5.8 %copy-start.8 = (bf16[64,256]{1,0:T(8,128)(2,1)S(1)}, bf16[64,256]{1,0:T(8,128)(2,1)}, u32[]{:S(2)}) copy-start(bf16[64,256]{1,0:T(8,128)(2,1)} %param.13) | copy-start | bytes 98308
  27.1 5.8 %copy-start.9 = (bf16[256,64]{0,1:T(8,128)(2,1)S(1)}, bf16[256,64]{0,1:T(8,128)(2,1)}, u32[]{:S(2)}) copy-start(bf16[256,64]{0,1:T(8,128)(2,1)} %param.11) | copy-start | bytes 98308
  27.1 5.8 %copy-start.10 = (bf16[256,64]{0,1:T(8,128)(2,1)S(1)}, bf16[256,64]{0,1:T(8,128)(2,1)}, u32[]{:S(2)}) copy-start(bf16[256,64]{0,1:T(8,128)(2,1)} %param.12) | copy-start | bytes 98308
  27.2 5.8 %copy-start.1 = (bf16[2048,256]{1,0:T(8,128)(2,1)S(1)}, bf16[2048,256]{1,0:T(8,128)(2,1)}, u32[]{:S(2)}) copy-start(bf16[2048,256]{1,0:T(8,128)(2,1)} %refs_1_.3) | copy-start | bytes 3145732
  27.2 33.7 %all-to-all-start.1 = ((bf16[64,32,256]{2,1,0:T(8,128)(2,1)}), bf16[64,32,256]{2,1,0:T(8,128)(2,1)S(1)}, u32[]{:S(2)}, u32[]{:S(2)}) async-start(bf16[64,32,256]{2,1,0:T(8,128)(2,1)} %gather_send.1), calls=%async_computation.1 | async-start | bytes 2097152 | tf_op jit(solution)/shard_map/exchange_features/all_to_all | solution.py:219
  33.0 0.9 copy-start.2
  33.9 27.0 %copy-start.4 = (s32[16,4]{0,1:T(4,128)S(1)}, s32[16,4]{0,1:T(4,128)}, u32[]{:S(2)}) copy-start(s32[16,4]{0,1:T(4,128)} %param.14) | copy-start | bytes 772
  62.6 0.6 copy-start.5
  63.2 12.5 %copy-start.6 = (bf16[8,32,256]{2,1,0:T(8,128)(2,1)S(1)}, bf16[8,32,256]{2,1,0:T(8,128)(2,1)}, u32[]{:S(2)}) copy-start(bf16[8,32,256]{2,1,0:T(8,128)(2,1)} %copy-done.5) | copy-start | bytes 393220
  63.2 34.1 %all-to-all-start.2 = ((f32[64,8,128]{2,1,0:T(8,128)}), f32[64,8,128]{2,1,0:T(8,128)S(1)}, u32[]{:S(2)}, u32[]{:S(2)}) async-start(f32[64,8,128]{2,1,0:T(8,128)} %get-tuple-element.37), calls=%async_computation.2 | async-start | bytes 524288 | tf_op jit(solution)/shard_map/exchange_virtual/all_to_all | solution.py:231
  69.9 7.2 %collective-permute-start.3 = (bf16[256,256]{1,0:T(8,128)(2,1)S(1)}, bf16[256,256]{1,0:T(8,128)(2,1)S(1)}, u32[]{:S(2)}, u32[]{:S(2)}) collective-permute-start(bf16[256,256]{1,0:T(8,128)(2,1)S(1)} %pad_maximum_fusion.pack_ref.refs_7_.refs_8_), channel_id=1, source_target_pairs={{0,1},{1,2},{2,3},{3,0},{4,5},{5,6},{6,7},{7,4},{8,9},{9,10},{10,1... | collective-permute-start | bytes 393224 | tf_op jit(solution)/shard_map/exchange_pack/ppermute | solution.py:177
  71.5 9.9 %collective-permute-start.4 = (bf16[256,256]{1,0:T(8,128)(2,1)S(1)}, bf16[256,256]{1,0:T(8,128)(2,1)S(1)}, u32[]{:S(2)}, u32[]{:S(2)}) collective-permute-start(bf16[256,256]{1,0:T(8,128)(2,1)S(1)} %pad_maximum_fusion.pack_ref.refs_7_.refs_8_), channel_id=1, source_target_pairs={{0,2},{1,3},{2,0},{3,1},{4,6},{5,7},{6,4},{7,5},{8,10},{9,11},{10,... | collective-permute-start | bytes 393224 | tf_op jit(solution)/shard_map/exchange_pack/ppermute | solution.py:177
  74.2 7.9 %collective-permute-start.5 = (bf16[256,256]{1,0:T(8,128)(2,1)S(1)}, bf16[256,256]{1,0:T(8,128)(2,1)S(1)}, u32[]{:S(2)}, u32[]{:S(2)}) collective-permute-start(bf16[256,256]{1,0:T(8,128)(2,1)S(1)} %pad_maximum_fusion.pack_ref.refs_7_.refs_8_), channel_id=1, source_target_pairs={{0,3},{1,0},{2,1},{3,2},{4,7},{5,4},{6,5},{7,6},{8,11},{9,8},{10,9... | collective-permute-start | bytes 393224 | tf_op jit(solution)/shard_map/exchange_pack/ppermute | solution.py:177
  75.7 9.9 %collective-permute-start = (bf16[8,32,256]{2,1,0:T(8,128)(2,1)S(1)}, bf16[8,32,256]{2,1,0:T(8,128)(2,1)S(1)}, u32[]{:S(2)}, u32[]{:S(2)}) collective-permute-start(bf16[8,32,256]{2,1,0:T(8,128)(2,1)S(1)} %copy-done.6), channel_id=1, source_target_pairs={{0,1},{1,2},{2,3},{3,0},{4,5},{5,6},{6,7},{7,4},{8,9},{9,10},{10,1... | collective-permute-start | bytes 393224 | tf_op jit(solution)/shard_map/exchange_rep0/ppermute | solution.py:177
  76.3 10.7 %collective-permute-start.1 = (bf16[8,32,256]{2,1,0:T(8,128)(2,1)}, bf16[8,32,256]{2,1,0:T(8,128)(2,1)S(1)}, u32[]{:S(2)}, u32[]{:S(2)}) collective-permute-start(bf16[8,32,256]{2,1,0:T(8,128)(2,1)} %get-tuple-element.26), channel_id=1, source_target_pairs={{0,2},{1,3},{2,0},{3,1},{4,6},{5,7},{6,4},{7,5},{8,10},{9,11},{10,... | collective-permute-start | bytes 393224 | tf_op jit(solution)/shard_map/exchange_rep0/ppermute | solution.py:177
  77.1 10.0 %collective-permute-start.2 = (bf16[8,32,256]{2,1,0:T(8,128)(2,1)S(1)}, bf16[8,32,256]{2,1,0:T(8,128)(2,1)S(1)}, u32[]{:S(2)}, u32[]{:S(2)}) collective-permute-start(bf16[8,32,256]{2,1,0:T(8,128)(2,1)S(1)} %get-tuple-element.27), channel_id=1, source_target_pairs={{0,3},{1,0},{2,1},{3,2},{4,7},{5,4},{6,5},{7,6},{8,11},{9,8},{10,9... | collective-permute-start | bytes 393224 | tf_op jit(solution)/shard_map/exchange_rep0/ppermute | solution.py:177
  81.4 16.0 %collective-permute-start.10 = (bf16[8,32,256]{2,1,0:T(8,128)(2,1)S(1)}, bf16[8,32,256]{2,1,0:T(8,128)(2,1)S(1)}, u32[]{:S(2)}, u32[]{:S(2)}) collective-permute-start(bf16[8,32,256]{2,1,0:T(8,128)(2,1)S(1)} %get-tuple-element.35), channel_id=1, source_target_pairs={{0,2},{1,3},{2,0},{3,1},{4,6},{5,7},{6,4},{7,5},{8,10},{9,11},{10,... | collective-permute-start | bytes 393224 | tf_op jit(solution)/shard_map/exchange_rep1/ppermute | solution.py:177
  82.1 15.2 %collective-permute-start.11 = (bf16[8,32,256]{2,1,0:T(8,128)(2,1)S(1)}, bf16[8,32,256]{2,1,0:T(8,128)(2,1)S(1)}, u32[]{:S(2)}, u32[]{:S(2)}) collective-permute-start(bf16[8,32,256]{2,1,0:T(8,128)(2,1)S(1)} %get-tuple-element.36), channel_id=1, source_target_pairs={{0,3},{1,0},{2,1},{3,2},{4,7},{5,4},{6,5},{7,6},{8,11},{9,8},{10,9... | collective-permute-start | bytes 393224 | tf_op jit(solution)/shard_map/exchange_rep1/ppermute | solution.py:177
  85.6 11.7 %collective-permute-start.9 = (bf16[8,32,256]{2,1,0:T(8,128)(2,1)S(1)}, bf16[8,32,256]{2,1,0:T(8,128)(2,1)S(1)}, u32[]{:S(2)}, u32[]{:S(2)}) collective-permute-start(bf16[8,32,256]{2,1,0:T(8,128)(2,1)S(1)} %get-tuple-element.34), channel_id=1, source_target_pairs={{0,1},{1,2},{2,3},{3,0},{4,5},{5,6},{6,7},{7,4},{8,9},{9,10},{10,1... | collective-permute-start | bytes 393224 | tf_op jit(solution)/shard_map/exchange_rep1/ppermute | solution.py:177
  95.0 16.9 %collective-permute-start.6 = (bf16[64,256]{1,0:T(8,128)(2,1)S(1)}, bf16[64,256]{1,0:T(8,128)(2,1)S(1)}, u32[]{:S(2)}, u32[]{:S(2)}) collective-permute-start(bf16[64,256]{1,0:T(8,128)(2,1)S(1)} %get-tuple-element.30), channel_id=1, source_target_pairs={{0,1},{1,2},{2,3},{3,0},{4,5},{5,6},{6,7},{7,4},{8,9},{9,10},{10,1... | collective-permute-start | bytes 98312 | tf_op jit(solution)/shard_map/exchange_out0/ppermute | solution.py:177
  105.5 11.6 %collective-permute-start.12 = (bf16[72,256]{1,0:T(8,128)(2,1)S(1)}, bf16[72,256]{1,0:T(8,128)(2,1)S(1)}, u32[]{:S(2)}, u32[]{:S(2)}) collective-permute-start(bf16[72,256]{1,0:T(8,128)(2,1)S(1)} %get-tuple-element.39), channel_id=1, source_target_pairs={{0,1},{1,2},{2,3},{3,0},{4,5},{5,6},{6,7},{7,4},{8,9},{9,10},{10,1... | collective-permute-start | bytes 110600 | tf_op jit(solution)/shard_map/exchange_out1/ppermute | solution.py:177
  106.2 10.9 %collective-permute-start.13 = (bf16[72,256]{1,0:T(8,128)(2,1)S(1)}, bf16[72,256]{1,0:T(8,128)(2,1)S(1)}, u32[]{:S(2)}, u32[]{:S(2)}) collective-permute-start(bf16[72,256]{1,0:T(8,128)(2,1)S(1)} %get-tuple-element.40), channel_id=1, source_target_pairs={{0,2},{1,3},{2,0},{3,1},{4,6},{5,7},{6,4},{7,5},{8,10},{9,11},{10,... | collective-permute-start | bytes 110600 | tf_op jit(solution)/shard_map/exchange_out1/ppermute | solution.py:177
  109.2 8.0 %collective-permute-start.14 = (bf16[72,256]{1,0:T(8,128)(2,1)S(1)}, bf16[72,256]{1,0:T(8,128)(2,1)S(1)}, u32[]{:S(2)}, u32[]{:S(2)}) collective-permute-start(bf16[72,256]{1,0:T(8,128)(2,1)S(1)} %get-tuple-element.41), channel_id=1, source_target_pairs={{0,3},{1,0},{2,1},{3,2},{4,7},{5,4},{6,5},{7,6},{8,11},{9,8},{10,9... | collective-permute-start | bytes 110600 | tf_op jit(solution)/shard_map/exchange_out1/ppermute | solution.py:177
  111.7 5.4 %collective-permute-start.7 = (bf16[64,256]{1,0:T(8,128)(2,1)S(1)}, bf16[64,256]{1,0:T(8,128)(2,1)S(1)}, u32[]{:S(2)}, u32[]{:S(2)}) collective-permute-start(bf16[64,256]{1,0:T(8,128)(2,1)S(1)} %get-tuple-element.31), channel_id=1, source_target_pairs={{0,2},{1,3},{2,0},{3,1},{4,6},{5,7},{6,4},{7,5},{8,10},{9,11},{10,... | collective-permute-start | bytes 98312 | tf_op jit(solution)/shard_map/exchange_out0/ppermute | solution.py:177
  111.9 5.2 %collective-permute-start.8 = (bf16[64,256]{1,0:T(8,128)(2,1)S(1)}, bf16[64,256]{1,0:T(8,128)(2,1)S(1)}, u32[]{:S(2)}, u32[]{:S(2)}) collective-permute-start(bf16[64,256]{1,0:T(8,128)(2,1)S(1)} %get-tuple-element.32), channel_id=1, source_target_pairs={{0,3},{1,0},{2,1},{3,2},{4,7},{5,4},{6,5},{7,6},{8,11},{9,8},{10,9... | collective-permute-start | bytes 98312 | tf_op jit(solution)/shard_map/exchange_out0/ppermute | solution.py:177

commit v3 on v2

v3 whole, which is shorter than its diff:
```python
import math

import jax
import jax.numpy as jnp
from jax import lax
from jax.experimental import pallas as pl
from jax.experimental.pallas import tpu as pltpu
from jax.sharding import PartitionSpec as P


D = 256
H = 8
TILE = 128
G = 4
HEAD = D // H
REP = 4
PEERS = 64
WIDTH = D // REP
QUARTER = TILE // REP
SCORE_SCALE = 1.0 / math.sqrt(HEAD)
EXP2_SCALE = SCORE_SCALE * math.log2(math.e)
NEG = -1e30
NT = (((1,), (1,)), ((), ()))
NN = (((1,), (0,)), ((), ()))

SMEM = pl.BlockSpec(memory_space=pltpu.SMEM)
VMEM = pl.BlockSpec(memory_space=pltpu.VMEM)
CHUNKS = 2
PER_CHUNK = 4 // CHUNKS
SLOTS = 4 * PER_CHUNK
NODES_CHUNK = TILE * PER_CHUNK
BF16 = jnp.bfloat16


def dot(a, b, dims=NN, precision=None):
    return lax.dot_general(a, b, dims, precision=precision, preferred_element_type=jnp.float32)


def in_vmem(value):
    return pltpu.with_memory_space_constraint(value, pltpu.VMEM)


def vmem_out(shape, dtype):
    return pltpu.VMEM(shape, dtype)


def params(mib):
    return pltpu.CompilerParams(vmem_limit_bytes=mib * 1024 * 1024)


def wanted_rows_kernel(map_ref, out_ref):
    blocks = map_ref[...]
    peer = lax.broadcasted_iota(jnp.int32, (PEERS, 16), 0)
    found = jnp.zeros((PEERS, 16), jnp.int32)
    for j in range(4):
        row = blocks[j : j + 1, :]
        found = found + jnp.where(peer == row // 16, row % 16, 0)
    out_ref[...] = jnp.broadcast_to(jnp.sum(found, axis=1, keepdims=True), (PEERS, TILE))


def gather_send_kernel(x_ref, want_ref, feat_ref, out_ref, row_ref, want_smem, sem):
    lane = lax.broadcasted_iota(jnp.int32, (PEERS, TILE), 1)
    peer = lax.broadcasted_iota(jnp.int32, (PEERS, TILE), 0)
    row_ref[...] = jnp.sum(jnp.where(lane == peer, want_ref[...], 0), axis=0, keepdims=True)
    copy = pltpu.make_async_copy(row_ref, want_smem, sem)
    copy.start()
    copy.wait()
    for e in range(PEERS):
        out_ref[e] = feat_ref[want_smem[0, e] * REP + x_ref[0]]


def gather_rep_kernel(x_ref, map_ref, arrived_ref, state_ref, *refs):
    outs = refs[REP - 1 :]
    for k in range(CHUNKS):
        for d in range(REP):
            column = ((x_ref[0] + d) % REP) * 4 + k * PER_CHUNK
            for j in range(SLOTS):
                owner = map_ref[j % 4, column + j // 4] // 16
                outs[k * REP + d][j] = arrived_ref[owner]
    for e in range(PEERS):
        outs[-1][e] = state_ref[...]


def prepare_kernel(
    x_ref, feat_in, value_ref, key_ref, out_w_ref, query_ref, vs_ref, links_ref,
    feat_ref, pack_ref, virtual_ref, state_ref, bias_ref,
):
    feat_ref[...] = feat_in[...]
    for i, part in enumerate((value_ref, key_ref, out_w_ref, query_ref)):
        pack_ref[i * WIDTH : (i + 1) * WIDTH, :] = part[...]
    vs = vs_ref[...]
    virtual_ref[...] = jnp.concatenate([vs, jnp.zeros((TILE - G, D), BF16)], axis=0)
    kv = dot(feat_in[...], pack_ref[:TILE, :], NT).astype(BF16)
    q = dot(jnp.concatenate([vs, vs], axis=0), pack_ref[TILE:, :], NT).astype(BF16)
    lane = lax.broadcasted_iota(jnp.int32, (2 * G, TILE), 1)
    row = lax.broadcasted_iota(jnp.int32, (2 * G, TILE), 0)
    first = WIDTH + HEAD * (row // G)
    q = jnp.where((lane >= first) & (lane < first + HEAD), q.astype(jnp.float32), 0.0).astype(BF16)
    s = dot(q, kv, NT)
    top = jnp.max(s, axis=1, keepdims=True)
    p = jnp.exp2((s - top) * EXP2_SCALE)
    total = jnp.sum(p, axis=1, keepdims=True)
    w = dot(p, kv.astype(jnp.float32), NN, lax.Precision.HIGHEST)
    state_ref[...] = jnp.where(lane < 64, w, jnp.where(lane < 96, total, top))
    column = lax.broadcasted_iota(jnp.int32, (TILE, TILE), 0)
    for c in range(4):
        first = pl.multiple_of(x_ref[0] * 512 + c * TILE, TILE)
        links = links_ref[:, pl.ds(first, TILE)]
        linked = column == links[0:1, :]
        for n in range(1, 16):
            linked = linked | (column == links[n : n + 1, :])
        bias_ref[c * TILE : (c + 1) * TILE, :] = jnp.where(linked, 0.0, NEG).T


def attention_rows(own, source, bias, packs, kv_ref):
    lane = lax.broadcasted_iota(jnp.int32, (TILE, TILE), 1)
    virtual_bias = jnp.where(lax.broadcasted_iota(jnp.int32, (1, TILE), 1) < G, 0.0, NEG)
    for pair in range(2):
        w = jnp.concatenate([packs[2 * pair][:TILE, :], packs[2 * pair + 1][:TILE, :]], axis=0)
        kv_ref[:, pair * D : (pair + 1) * D] = dot(source, w, NT).astype(BF16)
    q_all = dot(own, jnp.concatenate([p[TILE:, :] for p in packs], axis=0), NT)
    bias = jnp.concatenate([bias, bias], axis=0)
    groups = []
    for g in range(REP):
        q = q_all[:, g * TILE : (g + 1) * TILE]
        first = jnp.where((lane >= WIDTH) & (lane < WIDTH + HEAD), q, 0.0)
        second = jnp.where(lane >= WIDTH + HEAD, q, 0.0)
        kv = kv_ref[:, g * TILE : (g + 1) * TILE]
        s = dot(jnp.concatenate([first, second], axis=0).astype(BF16), kv, NT)
        s = jnp.concatenate([s[:, :TILE] + bias, s[:, TILE : 5 * TILE], s[:, 5 * TILE :] + virtual_bias], axis=1)
        top = jnp.max(s, axis=1, keepdims=True)
        p = jnp.exp2((s - top) * EXP2_SCALE)
        total = jnp.sum(p, axis=1, keepdims=True)
        o = dot(p.astype(BF16), kv) * (1.0 / total)
        o = jnp.where(lane < HEAD, o[:TILE], jnp.where(lane < WIDTH, o[TILE:], 0.0))
        groups.append(o.astype(BF16))
    return jnp.concatenate(groups, axis=1)


def attention_kernel(chunk, x_ref, feat_ref, *refs):
    ns, refs = refs[:REP], refs[REP:]
    bias_ref, refs = refs[0], refs[1:]
    packs, refs = refs[:REP], refs[REP:]
    vs_ref, refs = refs[0], refs[1:]
    if chunk == CHUNKS - 1:
        states_ref, refs = refs[0], refs[1:]
    outs, scratch, kv_ref = refs[:REP], refs[REP], refs[REP + 1]
    rows = []
    for i in range(PER_CHUNK):
        c = chunk * PER_CHUNK + i
        own = feat_ref[pl.ds(pl.multiple_of(x_ref[0] * 512 + c * TILE, TILE), TILE), :]
        near = [n[4 * i : 4 * i + 4].reshape(TILE, D) for n in ns]
        source = jnp.concatenate([own, *near, vs_ref[...]], axis=0)
        rows.append(attention_rows(own, source, bias_ref[c * TILE : (c + 1) * TILE, :], packs, kv_ref))
    w = jnp.concatenate([p[TILE:, :] for p in packs], axis=0)
    scratch[...] = dot(jnp.concatenate(rows, axis=0), w).T
    for d in range(REP):
        first = pl.multiple_of(((x_ref[0] + d) % REP) * WIDTH, WIDTH)
        outs[d][:WIDTH, :] = scratch[pl.ds(first, WIDTH), :].astype(BF16)
    if chunk == CHUNKS - 1:
        states = states_ref[...]
        top = jnp.max(states[:, :, 96:97], axis=0, keepdims=True)
        joined = jnp.sum(states * jnp.exp2((states[:, :, 96:97] - top) * EXP2_SCALE), axis=0)
        heads = joined * (1.0 / joined[:, WIDTH : WIDTH + 1])
        lane = lax.broadcasted_iota(jnp.int32, (G, TILE), 1)
        heads = jnp.where(lane < HEAD, heads[:G], jnp.where(lane < WIDTH, heads[G:], 0.0))
        heads = jnp.concatenate([heads, jnp.zeros((G, TILE), jnp.float32)], axis=0)
        heads = jnp.concatenate([heads, jnp.zeros((2 * G, NODES_CHUNK - TILE), jnp.float32)], axis=1)
        for d in range(REP):
            outs[d][WIDTH:, :] = heads.astype(BF16)


def assemble_kernel(x_ref, *refs):
    pieces, refs = refs[: REP * CHUNKS], refs[REP * CHUNKS :]
    packs, (out_ref, virtual_ref, scratch) = refs[:REP], refs[REP:]
    total = jnp.zeros((2 * G, D), jnp.float32)
    for d in range(REP):
        first = pl.multiple_of(((x_ref[0] + REP - d) % REP) * 512, 512)
        for k in range(CHUNKS):
            out_ref[:, pl.ds(first + k * NODES_CHUNK, NODES_CHUNK)] = pieces[k * REP + d][:WIDTH, :]
        total = total + dot(pieces[(CHUNKS - 1) * REP + d][WIDTH:, :TILE], packs[d][TILE:, :])
    scratch[...] = total.T
    own = scratch[pl.ds(pl.multiple_of(x_ref[0] * WIDTH, WIDTH), WIDTH), :]
    virtual_ref[...] = own.T[:G, :].astype(BF16)


def send_rep(values):
    return [values[0]] + [
        lax.ppermute(values[d], "rep", [(i, (i + d) % REP) for i in range(REP)]) for d in range(1, REP)
    ]


def shards(features, virtual_state, w_query, w_key, w_value, w_out, tile_map, local_nbr):
    x = lax.axis_index("rep")
    x_one = x.astype(jnp.int32).reshape(1)
    map_t = tile_map.T

    wanted_from = pl.pallas_call(
        wanted_rows_kernel,
        out_shape=vmem_out((PEERS, TILE), jnp.int32),
        in_specs=[VMEM],
        out_specs=VMEM,
        compiler_params=params(2),
        name="wanted_rows",
    )(in_vmem(map_t))
    wanted = lax.all_to_all(wanted_from.reshape(PEERS, 1, TILE), "nodes", 0, 0, tiled=True)

    rows_in_vmem, pack, virtual_rows, state, bias = pl.pallas_call(
        prepare_kernel,
        out_shape=[
            vmem_out((2048, D), BF16),
            vmem_out((D, D), BF16),
            vmem_out((TILE, D), BF16),
            vmem_out((2 * G, TILE), jnp.float32),
            vmem_out((512, TILE), jnp.float32),
        ],
        in_specs=[SMEM] + [VMEM] * 7,
        out_specs=[VMEM] * 5,
        compiler_params=params(16),
        name="prepare",
    )(x_one, features, w_value.T, w_key.T, w_out, w_query.T, virtual_state, local_nbr.T)
    packs = [in_vmem(p) for p in send_rep([pack] * REP)]

    outgoing = pl.pallas_call(
        gather_send_kernel,
        out_shape=vmem_out((PEERS, QUARTER, D), BF16),
        in_specs=[SMEM, VMEM, VMEM],
        out_specs=VMEM,
        scratch_shapes=[
            pltpu.VMEM((1, TILE), jnp.int32),
            pltpu.SMEM((1, TILE), jnp.int32),
            pltpu.SemaphoreType.DMA,
        ],
        compiler_params=params(2),
        name="gather_send",
    )(x_one, in_vmem(wanted.reshape(PEERS, TILE)), in_vmem(rows_in_vmem.reshape(PEERS, QUARTER, D)))
    arrived = lax.all_to_all(outgoing, "nodes", 0, 0, tiled=True)

    sends = pl.pallas_call(
        gather_rep_kernel,
        out_shape=[vmem_out((SLOTS, QUARTER, D), BF16)] * (CHUNKS * REP) + [vmem_out((PEERS, 2 * G, TILE), jnp.float32)],
        in_specs=[SMEM, SMEM] + [VMEM] * (REP + 1),
        out_specs=[VMEM] * (CHUNKS * REP + 1),
        compiler_params=params(2),
        name="gather_rep",
    )(x_one, map_t, in_vmem(arrived), in_vmem(state), *packs[1:])
    pieces = [send_rep(sends[k * REP : k * REP + REP]) for k in range(CHUNKS)]
    states = lax.all_to_all(sends[-1], "nodes", 0, 0, tiled=True)

    received = []
    for k in range(CHUNKS):
        last = k == CHUNKS - 1
        height = WIDTH + (2 * G if last else 0)
        args = [x_one, in_vmem(rows_in_vmem), *map(in_vmem, pieces[k]), in_vmem(bias), *packs, in_vmem(virtual_rows)]
        args += [in_vmem(states)] if last else []
        outs = pl.pallas_call(
            lambda *refs, k=k: attention_kernel(k, *refs),
            out_shape=[vmem_out((height, NODES_CHUNK), BF16)] * REP,
            in_specs=[SMEM] + [VMEM] * (len(args) - 1),
            out_specs=[VMEM] * REP,
            scratch_shapes=[pltpu.VMEM((D, NODES_CHUNK), jnp.float32), pltpu.VMEM((6 * TILE, 2 * D), BF16)],
            compiler_params=params(24),
        )(*args)
        received += send_rep(outs)
    node_out, virtual_out = pl.pallas_call(
        assemble_kernel,
        out_shape=[jax.ShapeDtypeStruct((WIDTH, 2048), BF16), jax.ShapeDtypeStruct((G, WIDTH), BF16)],
        in_specs=[SMEM] + [VMEM] * (REP * CHUNKS + REP),
        out_specs=[VMEM] * 2,
        scratch_shapes=[pltpu.VMEM((D, 2 * G), jnp.float32)],
        compiler_params=params(4),
        name="assemble",
    )(x_one, *map(in_vmem, received), *packs)
    return node_out.T, virtual_out


def solution(mesh):
    in_specs = (
        P("nodes", None),
        P(),
        P(None, "rep"),
        P(None, "rep"),
        P(None, "rep"),
        P("rep", None),
        P("nodes", None),
        P("nodes", None),
    )
    out_specs = (P("nodes", "rep"), P(None, "rep"))
    return jax.shard_map(shards, mesh=mesh, in_specs=in_specs, out_specs=out_specs, check_vma=False)
```

time: 119 us -> 106 us (0.89)
  Pallas kernels: 24.6 us -> 16.3 us
  waiting for transfers between devices: 40.8 us -> 32.8 us
  starting transfers between devices: 48.3 us -> 49.8 us
  local copies, waits for them, and re-layouts: 4.12 us -> 5.49 us
    all_to_all x1, waiting for transfers between devices: 25.2 us -> 15.5 us  [shards(): arrived = lax.all_to_all(outgoing, 'nodes', 0, 0, tiled=True)]
    ppermute x15, waiting for transfers between devices: 7.02 us -> 14.1 us  [send_rep(): lax.ppermute(values[d], 'rep', [(i, (i + d) % REP) for i in range(REP)])]
    pallas_call x2, Pallas kernels: 16 us -> 9.36 us  [shards(): pl.pallas_call(lambda *refs, k=k: attention_kernel(k, *refs), out_shape=[...]
    all_to_all x1, waiting for transfers between devices: 8.57 us -> 3.17 us  [shards(): lax.all_to_all(wanted_from.reshape(PEERS, 1, TILE), 'nodes', 0, 0, tiled=...]
    all_to_all x1, starting transfers between devices: 5.71 us -> 7.14 us  [shards(): arrived = lax.all_to_all(outgoing, 'nodes', 0, 0, tiled=True)]
    unnamed x25 -> x26, local copies, waits for them, and re-layouts: 4.11 us -> 5.49 us
    pallas_call x2, Pallas kernels: 3.79 us -> 2.54 us  [the longest x1 1.82 us: shards(): pl.pallas_call(prepare_kernel, out_shape=[vmem_out((2048, D), BF16), vmem...]
  transfers between devices with their start and end apart: 18 -> 18, of which waited for: 6 -> 8; matrix products, arithmetic and copies ran while one was open for 0% -> 0% of each run, Pallas kernels for 15% -> 11%
where the time goes in v3:
time: 106 us; the launch traced here: 105 us
  starting transfers between devices  49.8 us (47%)
  waiting for transfers between devices  32.8 us (31%)
  Pallas kernels  16.3 us (15%)
  local copies, waits for them, and re-layouts  5.49 us (5%)
    ppermute x15, starting transfers between devices, send_rep(): lax.ppermute(values[d], 'rep', [(i, (i + d) % REP) for i in range(REP)])  24.1 us
    all_to_all x1, waiting for transfers between devices, shards(): arrived = lax.all_to_all(outgoing, 'nodes', 0, 0, tiled=True)  15.5 us
    ppermute x15, waiting for transfers between devices, send_rep(): lax.ppermute(values[d], 'rep', [(i, (i + d) % REP) for i in range(REP)])  14.1 us
    all_to_all x1, starting transfers between devices, shards(): lax.all_to_all(wanted_from.reshape(PEERS, 1, TILE), 'nodes', 0, 0, tiled=...  11.9 us
    pallas_call x2, Pallas kernels, shards(): pl.pallas_call(lambda *refs, k=k: attention_kernel(k, *refs), out_shape=[...  9.36 us
    all_to_all x1, starting transfers between devices, shards(): arrived = lax.all_to_all(outgoing, 'nodes', 0, 0, tiled=True)  7.14 us
    all_to_all x1, starting transfers between devices, shards(): states = lax.all_to_all(sends[-1], 'nodes', 0, 0, tiled=True)  6.66 us
    unnamed x26, local copies, waits for them, and re-layouts  5.49 us
  transfers between devices with their start and end apart: 18, of which 8 were waited for; matrix products, arithmetic and copies ran while one was open for 0% of the time, Pallas kernels for 11%

profile of v3, /device:TPU:32, one launch (start us, length us, event | category | flops | bytes accessed | tf_op | source)
XLA Modules:
  0.0 105.1 jit_solution(2957971095117654810)
XLA Ops:
  0.6 0.0 copy-start.6
  0.6 0.7 copy-done.6
  1.3 0.0 copy-start.4
  1.3 0.7 wanted_rows.1
  2.0 0.0 copy-start.2
  2.0 0.0 copy-start.3
  2.0 11.9 %all-to-all-start = ((s32[64,1,128]{2,1,0:T(1,128)}), s32[64,1,128]{2,1,0:T(1,128)S(1)}, u32[]{:S(2)}, u32[]{:S(2)}) async-start(s32[64,1,128]{2,1,0:T(1,128)} %bitcast.7), calls=%async_computation | async-start | bytes 65536 | tf_op jit(solution)/shard_map/all_to_all | solution.py:206
  14.0 0.0 copy-start.8
  14.0 0.0 copy-done.4
  14.0 0.0 copy-done.2
  14.0 0.0 copy-done.3
  14.0 0.6 copy-done.8
  14.6 0.0 copy-start
  14.6 1.2 %copy-done = bf16[2048,256]{1,0:T(8,128)(2,1)S(1)} copy-done((bf16[2048,256]{1,0:T(8,128)(2,1)S(1)}, bf16[2048,256]{1,0:T(8,128)(2,1)}, u32[]{:S(2)}) %copy-start) | copy-done | bytes 1048600
  15.9 0.9 copy-done.1
  16.8 0.8 copy-done.5
  17.5 1.8 %prepare.1 = (bf16[2048,256]{1,0:T(8,128)(2,1)S(1)}, bf16[256,256]{1,0:T(8,128)(2,1)S(1)}, bf16[128,256]{1,0:T(8,128)(2,1)S(1)}, f32[8,128]{1,0:T(8,128)S(1)}, f32[512,128]{1,0:T(8,128)S(1)}) custom-call(s32[1]{0:T(128)} %bitcast.x_ref.refs_0_, bf16[2048,256]{1,0:T(8,128)(2,1)S(1)} %copy-done, bf16[64,256]{1,0:T(8,128)(2,1)S(1)} %bitcast.15, ...), custom_call_target="tpu_custom_call" | custom-call | tf_op jit(solution)/shard_map/prepare/pallas_call | solution.py:208
  19.3 3.2 %all-to-all-done = s32[64,1,128]{2,1,0:T(1,128)S(1)} async-done(((s32[64,1,128]{2,1,0:T(1,128)}), s32[64,1,128]{2,1,0:T(1,128)S(1)}, u32[]{:S(2)}, u32[]{:S(2)}) %all-to-all-start) | async-done | bytes 32800 | tf_op jit(solution)/shard_map/all_to_all | solution.py:206
  22.5 1.6 %gather_send.1 = bf16[64,32,256]{2,1,0:T(8,128)(2,1)} custom-call(s32[1]{0:T(128)} %bitcast.x_ref.refs_0_, s32[64,128]{1,0:T(8,128)S(1)} %bitcast.13, bf16[64,32,256]{2,1,0:T(8,128)(2,1)S(1)} %bitcast.12), custom_call_target="tpu_custom_call" | custom-call | tf_op jit(solution)/shard_map/gather_send/pallas_call | solution.py:224
  24.1 7.1 %all-to-all-start.1 = ((bf16[64,32,256]{2,1,0:T(8,128)(2,1)}), bf16[64,32,256]{2,1,0:T(8,128)(2,1)S(1)}, u32[]{:S(2)}, u32[]{:S(2)}) async-start(bf16[64,32,256]{2,1,0:T(8,128)(2,1)} %gather_send.1), calls=%async_computation.1 | async-start | bytes 2097152 | tf_op jit(solution)/shard_map/all_to_all | solution.py:237
  31.3 0.0 copy-start.7
  31.3 2.8 %collective-permute-start.2 = (bf16[256,256]{1,0:T(8,128)(2,1)S(1)}, bf16[256,256]{1,0:T(8,128)(2,1)S(1)}, u32[]{:S(2)}, u32[]{:S(2)}) collective-permute-start(bf16[256,256]{1,0:T(8,128)(2,1)S(1)} %get-tuple-element.28.refs_7_.refs_8_), channel_id=1, source_target_pairs={{0,3},{1,0},{2,1},{3,2},{4,7},{5,4},{6,5},{7,6},{8,11},{9,8},{10,9... | collective-permute-start | bytes 393224 | tf_op jit(solution)/shard_map/ppermute | solution.py:189
  34.1 0.8 collective-permute-start.1
  34.9 0.9 collective-permute-start
  35.8 4.2 %collective-permute-done.2.refs_2_.refs_10_.refs_11_ = bf16[256,256]{1,0:T(8,128)(2,1)S(1)} collective-permute-done((bf16[256,256]{1,0:T(8,128)(2,1)S(1)}, bf16[256,256]{1,0:T(8,128)(2,1)S(1)}, u32[]{:S(2)}, u32[]{:S(2)}) %collective-permute-start.2) | collective-permute-done | bytes 131104 | tf_op jit(solution)/shard_map/ppermute | solution.py:189
  40.0 2.0 %collective-permute-done.1.refs_1_.refs_9_.refs_10_ = bf16[256,256]{1,0:T(8,128)(2,1)S(1)} collective-permute-done((bf16[256,256]{1,0:T(8,128)(2,1)S(1)}, bf16[256,256]{1,0:T(8,128)(2,1)S(1)}, u32[]{:S(2)}, u32[]{:S(2)}) %collective-permute-start.1) | collective-permute-done | bytes 131104 | tf_op jit(solution)/shard_map/ppermute | solution.py:189
  42.0 1.7 %collective-permute-done.refs_0_.refs_8_.refs_9_ = bf16[256,256]{1,0:T(8,128)(2,1)S(1)} collective-permute-done((bf16[256,256]{1,0:T(8,128)(2,1)S(1)}, bf16[256,256]{1,0:T(8,128)(2,1)S(1)}, u32[]{:S(2)}, u32[]{:S(2)}) %collective-permute-start) | collective-permute-done | bytes 131104 | tf_op jit(solution)/shard_map/ppermute | solution.py:189
  43.7 15.5 %all-to-all-done.1.arrived_ref = bf16[64,32,256]{2,1,0:T(8,128)(2,1)S(1)} async-done(((bf16[64,32,256]{2,1,0:T(8,128)(2,1)}), bf16[64,32,256]{2,1,0:T(8,128)(2,1)S(1)}, u32[]{:S(2)}, u32[]{:S(2)}) %all-to-all-start.1) | async-done | bytes 1048608 | tf_op jit(solution)/shard_map/all_to_all | solution.py:237
  59.2 0.0 copy-done.7
  59.2 1.7 %gather_rep.1 = (bf16[8,32,256]{2,1,0:T(8,128)(2,1)S(1)}, bf16[8,32,256]{2,1,0:T(8,128)(2,1)S(1)}, bf16[8,32,256]{2,1,0:T(8,128)(2,1)}, bf16[8,32,256]{2,1,0:T(8...) custom-call(s32[1]{0:T(128)} %bitcast.x_ref.refs_0_, ...), custom_call_target="tpu_custom_call" | custom-call | tf_op jit(solution)/shard_map/gather_rep/pallas_call | solution.py:239
  60.9 0.6 copy-done.9
  61.6 6.7 %all-to-all-start.2 = ((f32[64,8,128]{2,1,0:T(8,128)}), f32[64,8,128]{2,1,0:T(8,128)S(1)}, u32[]{:S(2)}, u32[]{:S(2)}) async-start(f32[64,8,128]{2,1,0:T(8,128)} %get-tuple-element.43), calls=%async_computation.2 | async-start | bytes 524288 | tf_op jit(solution)/shard_map/all_to_all | solution.py:248
  68.3 0.0 copy-done.10
  68.3 1.6 %collective-permute-start.3 = (bf16[8,32,256]{2,1,0:T(8,128)(2,1)S(1)}, bf16[8,32,256]{2,1,0:T(8,128)(2,1)S(1)}, u32[]{:S(2)}, u32[]{:S(2)}) collective-permute-start(bf16[8,32,256]{2,1,0:T(8,128)(2,1)S(1)} %copy-done.10), channel_id=1, source_target_pairs={{0,1},{1,2},{2,3},{3,0},{4,5},{5,6},{6,7},{7,4},{8,9},{9,10},{10,1... | collective-permute-start | bytes 393224 | tf_op jit(solution)/shard_map/ppermute | solution.py:189
  69.8 2.7 %collective-permute-start.4 = (bf16[8,32,256]{2,1,0:T(8,128)(2,1)}, bf16[8,32,256]{2,1,0:T(8,128)(2,1)S(1)}, u32[]{:S(2)}, u32[]{:S(2)}) collective-permute-start(bf16[8,32,256]{2,1,0:T(8,128)(2,1)} %get-tuple-element.31), channel_id=1, source_target_pairs={{0,2},{1,3},{2,0},{3,1},{4,6},{5,7},{6,4},{7,5},{8,10},{9,11},{10,... | collective-permute-start | bytes 393224 | tf_op jit(solution)/shard_map/ppermute | solution.py:189
  72.6 1.4 %collective-permute-start.5 = (bf16[8,32,256]{2,1,0:T(8,128)(2,1)}, bf16[8,32,256]{2,1,0:T(8,128)(2,1)S(1)}, u32[]{:S(2)}, u32[]{:S(2)}) collective-permute-start(bf16[8,32,256]{2,1,0:T(8,128)(2,1)} %get-tuple-element.32), channel_id=1, source_target_pairs={{0,3},{1,0},{2,1},{3,2},{4,7},{5,4},{6,5},{7,6},{8,11},{9,8},{10,9... | collective-permute-start | bytes 393224 | tf_op jit(solution)/shard_map/ppermute | solution.py:189
  74.0 0.6 collective-permute-start.9
  74.6 0.9 collective-permute-start.10
  75.5 0.0 collective-permute-done.3.refs_3_
  75.5 2.0 %collective-permute-start.11 = (bf16[8,32,256]{2,1,0:T(8,128)(2,1)S(1)}, bf16[8,32,256]{2,1,0:T(8,128)(2,1)S(1)}, u32[]{:S(2)}, u32[]{:S(2)}) collective-permute-start(bf16[8,32,256]{2,1,0:T(8,128)(2,1)S(1)} %get-tuple-element.42), channel_id=1, source_target_pairs={{0,3},{1,0},{2,1},{3,2},{4,7},{5,4},{6,5},{7,6},{8,11},{9,8},{10,9... | collective-permute-start | bytes 393224 | tf_op jit(solution)/shard_map/ppermute | solution.py:189
  77.5 2.2 %collective-permute-done.4.refs_4_ = bf16[8,32,256]{2,1,0:T(8,128)(2,1)S(1)} collective-permute-done((bf16[8,32,256]{2,1,0:T(8,128)(2,1)}, bf16[8,32,256]{2,1,0:T(8,128)(2,1)S(1)}, u32[]{:S(2)}, u32[]{:S(2)}) %collective-permute-start.4) | collective-permute-done | bytes 131104 | tf_op jit(solution)/shard_map/ppermute | solution.py:189
  79.7 0.8 collective-permute-done.5.refs_5_
  80.5 4.9 %shard_map.95 = (bf16[64,256]{1,0:T(8,128)(2,1)S(1)}, bf16[64,256]{1,0:T(8,128)(2,1)}, bf16[64,256]{1,0:T(8,128)(2,1)S(1)}, bf16[64,256]{1,0:T(8,128)(2,1)S(1)}) custom-call(s32[1]{0:T(128)} %bitcast.x_ref.refs_0_, bf16[2048,256]{1,0:T(8,128)(2,1)S(1)} %get-tuple-element.26.refs_1_, bf16[8,32,256]{2,1,0:T(8,128)(2,1)S(1)} %get-tuple-element.29.refs_2_, ...), custom_call_target="tpu_custom_call" | custom-call | tf_op jit(solution)/shard_map/pallas_call | solution.py:256
  85.4 0.6 copy-done.11
  86.0 1.8 %collective-permute-start.6 = (bf16[64,256]{1,0:T(8,128)(2,1)}, bf16[64,256]{1,0:T(8,128)(2,1)S(1)}, u32[]{:S(2)}, u32[]{:S(2)}) collective-permute-start(bf16[64,256]{1,0:T(8,128)(2,1)} %get-tuple-element.36), channel_id=1, source_target_pairs={{0,1},{1,2},{2,3},{3,0},{4,5},{5,6},{6,7},{7,4},{8,9},{9,10},{10,1... | collective-permute-start | bytes 98312 | tf_op jit(solution)/shard_map/ppermute | solution.py:189
  87.8 0.0 collective-permute-done.9.refs_3_
  87.8 0.0 collective-permute-done.10.refs_4_
  87.8 0.0 collective-permute-done.11.refs_5_
  87.8 0.0 all-to-all-done.2.refs_12_
  87.8 0.0 copy-start.12
  87.8 4.5 %shard_map.96 = (bf16[72,256]{1,0:T(8,128)(2,1)S(1)}, bf16[72,256]{1,0:T(8,128)(2,1)S(1)}, bf16[72,256]{1,0:T(8,128)(2,1)S(1)}, bf16[72,256]{1,0:T(8,128)(2,1)S(1)}) custom-call(s32[1]{0:T(128)} %bitcast.x_ref.refs_0_, bf16[2048,256]{1,0:T(8,128)(2,1)S(1)} %get-tuple-element.26.refs_1_, bf16[8,32,256]{2,1,0:T(8,128)(2,1)S(1)} %get-tuple-element.39.refs_2_, ...), custom_call_target="tpu_custom_call" | custom-call | tf_op jit(solution)/shard_map/pallas_call | solution.py:256
  92.3 0.5 collective-permute-start.12
  92.8 3.4 %collective-permute-start.13 = (bf16[72,256]{1,0:T(8,128)(2,1)S(1)}, bf16[72,256]{1,0:T(8,128)(2,1)S(1)}, u32[]{:S(2)}, u32[]{:S(2)}) collective-permute-start(bf16[72,256]{1,0:T(8,128)(2,1)S(1)} %get-tuple-element.46), channel_id=1, source_target_pairs={{0,2},{1,3},{2,0},{3,1},{4,6},{5,7},{6,4},{7,5},{8,10},{9,11},{10,... | collective-permute-start | bytes 110600 | tf_op jit(solution)/shard_map/ppermute | solution.py:189
  96.2 2.5 %collective-permute-start.14 = (bf16[72,256]{1,0:T(8,128)(2,1)S(1)}, bf16[72,256]{1,0:T(8,128)(2,1)S(1)}, u32[]{:S(2)}, u32[]{:S(2)}) collective-permute-start(bf16[72,256]{1,0:T(8,128)(2,1)S(1)} %get-tuple-element.47), channel_id=1, source_target_pairs={{0,3},{1,0},{2,1},{3,2},{4,7},{5,4},{6,5},{7,6},{8,11},{9,8},{10,9... | collective-permute-start | bytes 110600 | tf_op jit(solution)/shard_map/ppermute | solution.py:189
  98.7 0.0 copy-done.12
  98.7 0.0 collective-permute-start.7
  98.7 0.0 collective-permute-done.6.refs_1_
  98.7 2.2 %collective-permute-start.8 = (bf16[64,256]{1,0:T(8,128)(2,1)S(1)}, bf16[64,256]{1,0:T(8,128)(2,1)S(1)}, u32[]{:S(2)}, u32[]{:S(2)}) collective-permute-start(bf16[64,256]{1,0:T(8,128)(2,1)S(1)} %get-tuple-element.38), channel_id=1, source_target_pairs={{0,3},{1,0},{2,1},{3,2},{4,7},{5,4},{6,5},{7,6},{8,11},{9,8},{10,9... | collective-permute-start | bytes 98312 | tf_op jit(solution)/shard_map/ppermute | solution.py:189
  100.9 3.2 %collective-permute-done.7.refs_2_ = bf16[64,256]{1,0:T(8,128)(2,1)S(1)} collective-permute-done((bf16[64,256]{1,0:T(8,128)(2,1)S(1)}, bf16[64,256]{1,0:T(8,128)(2,1)S(1)}, u32[]{:S(2)}, u32[]{:S(2)}) %collective-permute-start.7) | collective-permute-done | bytes 32800 | tf_op jit(solution)/shard_map/ppermute | solution.py:189
  104.1 0.0 collective-permute-done.8.refs_3_
  104.1 0.0 collective-permute-done.12.refs_5_
  104.1 0.0 collective-permute-done.13.refs_6_
  104.1 0.0 collective-permute-done.14.refs_7_
  104.1 1.0 assemble.1
  (5 shorter events, 0.0 us)
Async XLA Ops:
  0.6 0.7 copy-start.6
  1.3 12.7 %copy-start.4 = (bf16[64,256]{1,0:T(8,128)(2,1)S(1)}, bf16[64,256]{1,0:T(8,128)(2,1)}, u32[]{:S(2)}) copy-start(bf16[64,256]{1,0:T(8,128)(2,1)} %out_w_ref.1) | copy-start | bytes 98308
  2.0 11.9 %copy-start.2 = (bf16[256,64]{0,1:T(8,128)(2,1)S(1)}, bf16[256,64]{0,1:T(8,128)(2,1)}, u32[]{:S(2)}) copy-start(bf16[256,64]{0,1:T(8,128)(2,1)} %param.12) | copy-start | bytes 98308
  2.0 11.9 %copy-start.3 = (bf16[256,64]{0,1:T(8,128)(2,1)S(1)}, bf16[256,64]{0,1:T(8,128)(2,1)}, u32[]{:S(2)}) copy-start(bf16[256,64]{0,1:T(8,128)(2,1)} %param.11) | copy-start | bytes 98308
  2.0 20.5 %all-to-all-start = ((s32[64,1,128]{2,1,0:T(1,128)}), s32[64,1,128]{2,1,0:T(1,128)S(1)}, u32[]{:S(2)}, u32[]{:S(2)}) async-start(s32[64,1,128]{2,1,0:T(1,128)} %bitcast.7), calls=%async_computation | async-start | bytes 65536 | tf_op jit(solution)/shard_map/all_to_all | solution.py:206
  14.0 0.7 copy-start.8
  14.6 1.2 %copy-start = (bf16[2048,256]{1,0:T(8,128)(2,1)S(1)}, bf16[2048,256]{1,0:T(8,128)(2,1)}, u32[]{:S(2)}) copy-start(bf16[2048,256]{1,0:T(8,128)(2,1)} %feat_in.1) | copy-start | bytes 3145732
  15.9 0.9 copy-start.1
  16.8 0.8 copy-start.5
  24.1 35.1 %all-to-all-start.1 = ((bf16[64,32,256]{2,1,0:T(8,128)(2,1)}), bf16[64,32,256]{2,1,0:T(8,128)(2,1)S(1)}, u32[]{:S(2)}, u32[]{:S(2)}) async-start(bf16[64,32,256]{2,1,0:T(8,128)(2,1)} %gather_send.1), calls=%async_computation.1 | async-start | bytes 2097152 | tf_op jit(solution)/shard_map/all_to_all | solution.py:237
  31.3 27.9 %copy-start.7 = (s32[16,4]{0,1:T(4,128)S(1)}, s32[16,4]{0,1:T(4,128)}, u32[]{:S(2)}) copy-start(s32[16,4]{0,1:T(4,128)} %param.14) | copy-start | bytes 772
  31.3 8.7 %collective-permute-start.2 = (bf16[256,256]{1,0:T(8,128)(2,1)S(1)}, bf16[256,256]{1,0:T(8,128)(2,1)S(1)}, u32[]{:S(2)}, u32[]{:S(2)}) collective-permute-start(bf16[256,256]{1,0:T(8,128)(2,1)S(1)} %get-tuple-element.28.refs_7_.refs_8_), channel_id=1, source_target_pairs={{0,3},{1,0},{2,1},{3,2},{4,7},{5,4},{6,5},{7,6},{8,11},{9,8},{10,9... | collective-permute-start | bytes 393224 | tf_op jit(solution)/shard_map/ppermute | solution.py:189
  34.1 7.9 %collective-permute-start.1 = (bf16[256,256]{1,0:T(8,128)(2,1)S(1)}, bf16[256,256]{1,0:T(8,128)(2,1)S(1)}, u32[]{:S(2)}, u32[]{:S(2)}) collective-permute-start(bf16[256,256]{1,0:T(8,128)(2,1)S(1)} %get-tuple-element.28.refs_7_.refs_8_), channel_id=1, source_target_pairs={{0,2},{1,3},{2,0},{3,1},{4,6},{5,7},{6,4},{7,5},{8,10},{9,11},{10,... | collective-permute-start | bytes 393224 | tf_op jit(solution)/shard_map/ppermute | solution.py:189
  34.9 8.8 %collective-permute-start = (bf16[256,256]{1,0:T(8,128)(2,1)S(1)}, bf16[256,256]{1,0:T(8,128)(2,1)S(1)}, u32[]{:S(2)}, u32[]{:S(2)}) collective-permute-start(bf16[256,256]{1,0:T(8,128)(2,1)S(1)} %get-tuple-element.28.refs_7_.refs_8_), channel_id=1, source_target_pairs={{0,1},{1,2},{2,3},{3,0},{4,5},{5,6},{6,7},{7,4},{8,9},{9,10},{10,1... | collective-permute-start | bytes 393224 | tf_op jit(solution)/shard_map/ppermute | solution.py:189
  60.9 0.6 copy-start.9
  61.6 6.7 %copy-start.10 = (bf16[8,32,256]{2,1,0:T(8,128)(2,1)S(1)}, bf16[8,32,256]{2,1,0:T(8,128)(2,1)}, u32[]{:S(2)}) copy-start(bf16[8,32,256]{2,1,0:T(8,128)(2,1)} %copy-done.9) | copy-start | bytes 393220
  61.6 26.2 %all-to-all-start.2 = ((f32[64,8,128]{2,1,0:T(8,128)}), f32[64,8,128]{2,1,0:T(8,128)S(1)}, u32[]{:S(2)}, u32[]{:S(2)}) async-start(f32[64,8,128]{2,1,0:T(8,128)} %get-tuple-element.43), calls=%async_computation.2 | async-start | bytes 524288 | tf_op jit(solution)/shard_map/all_to_all | solution.py:248
  68.3 7.2 %collective-permute-start.3 = (bf16[8,32,256]{2,1,0:T(8,128)(2,1)S(1)}, bf16[8,32,256]{2,1,0:T(8,128)(2,1)S(1)}, u32[]{:S(2)}, u32[]{:S(2)}) collective-permute-start(bf16[8,32,256]{2,1,0:T(8,128)(2,1)S(1)} %copy-done.10), channel_id=1, source_target_pairs={{0,1},{1,2},{2,3},{3,0},{4,5},{5,6},{6,7},{7,4},{8,9},{9,10},{10,1... | collective-permute-start | bytes 393224 | tf_op jit(solution)/shard_map/ppermute | solution.py:189
  69.8 9.9 %collective-permute-start.4 = (bf16[8,32,256]{2,1,0:T(8,128)(2,1)}, bf16[8,32,256]{2,1,0:T(8,128)(2,1)S(1)}, u32[]{:S(2)}, u32[]{:S(2)}) collective-permute-start(bf16[8,32,256]{2,1,0:T(8,128)(2,1)} %get-tuple-element.31), channel_id=1, source_target_pairs={{0,2},{1,3},{2,0},{3,1},{4,6},{5,7},{6,4},{7,5},{8,10},{9,11},{10,... | collective-permute-start | bytes 393224 | tf_op jit(solution)/shard_map/ppermute | solution.py:189
  72.6 7.9 %collective-permute-start.5 = (bf16[8,32,256]{2,1,0:T(8,128)(2,1)}, bf16[8,32,256]{2,1,0:T(8,128)(2,1)S(1)}, u32[]{:S(2)}, u32[]{:S(2)}) collective-permute-start(bf16[8,32,256]{2,1,0:T(8,128)(2,1)} %get-tuple-element.32), channel_id=1, source_target_pairs={{0,3},{1,0},{2,1},{3,2},{4,7},{5,4},{6,5},{7,6},{8,11},{9,8},{10,9... | collective-permute-start | bytes 393224 | tf_op jit(solution)/shard_map/ppermute | solution.py:189
  74.0 13.8 %collective-permute-start.9 = (bf16[8,32,256]{2,1,0:T(8,128)(2,1)}, bf16[8,32,256]{2,1,0:T(8,128)(2,1)S(1)}, u32[]{:S(2)}, u32[]{:S(2)}) collective-permute-start(bf16[8,32,256]{2,1,0:T(8,128)(2,1)} %get-tuple-element.40), channel_id=1, source_target_pairs={{0,1},{1,2},{2,3},{3,0},{4,5},{5,6},{6,7},{7,4},{8,9},{9,10},{10,1... | collective-permute-start | bytes 393224 | tf_op jit(solution)/shard_map/ppermute | solution.py:189
  74.6 13.2 %collective-permute-start.10 = (bf16[8,32,256]{2,1,0:T(8,128)(2,1)S(1)}, bf16[8,32,256]{2,1,0:T(8,128)(2,1)S(1)}, u32[]{:S(2)}, u32[]{:S(2)}) collective-permute-start(bf16[8,32,256]{2,1,0:T(8,128)(2,1)S(1)} %get-tuple-element.41), channel_id=1, source_target_pairs={{0,2},{1,3},{2,0},{3,1},{4,6},{5,7},{6,4},{7,5},{8,10},{9,11},{10,... | collective-permute-start | bytes 393224 | tf_op jit(solution)/shard_map/ppermute | solution.py:189
  75.5 12.3 %collective-permute-start.11 = (bf16[8,32,256]{2,1,0:T(8,128)(2,1)S(1)}, bf16[8,32,256]{2,1,0:T(8,128)(2,1)S(1)}, u32[]{:S(2)}, u32[]{:S(2)}) collective-permute-start(bf16[8,32,256]{2,1,0:T(8,128)(2,1)S(1)} %get-tuple-element.42), channel_id=1, source_target_pairs={{0,3},{1,0},{2,1},{3,2},{4,7},{5,4},{6,5},{7,6},{8,11},{9,8},{10,9... | collective-permute-start | bytes 393224 | tf_op jit(solution)/shard_map/ppermute | solution.py:189
  85.4 0.6 copy-start.11
  86.0 12.7 %collective-permute-start.6 = (bf16[64,256]{1,0:T(8,128)(2,1)}, bf16[64,256]{1,0:T(8,128)(2,1)S(1)}, u32[]{:S(2)}, u32[]{:S(2)}) collective-permute-start(bf16[64,256]{1,0:T(8,128)(2,1)} %get-tuple-element.36), channel_id=1, source_target_pairs={{0,1},{1,2},{2,3},{3,0},{4,5},{5,6},{6,7},{7,4},{8,9},{9,10},{10,1... | collective-permute-start | bytes 98312 | tf_op jit(solution)/shard_map/ppermute | solution.py:189
  87.8 10.9 %copy-start.12 = (bf16[64,256]{1,0:T(8,128)(2,1)S(1)}, bf16[64,256]{1,0:T(8,128)(2,1)}, u32[]{:S(2)}) copy-start(bf16[64,256]{1,0:T(8,128)(2,1)} %copy-done.11) | copy-start | bytes 98308
  92.3 11.8 %collective-permute-start.12 = (bf16[72,256]{1,0:T(8,128)(2,1)S(1)}, bf16[72,256]{1,0:T(8,128)(2,1)S(1)}, u32[]{:S(2)}, u32[]{:S(2)}) collective-permute-start(bf16[72,256]{1,0:T(8,128)(2,1)S(1)} %get-tuple-element.45), channel_id=1, source_target_pairs={{0,1},{1,2},{2,3},{3,0},{4,5},{5,6},{6,7},{7,4},{8,9},{9,10},{10,1... | collective-permute-start | bytes 110600 | tf_op jit(solution)/shard_map/ppermute | solution.py:189
  92.8 11.3 %collective-permute-start.13 = (bf16[72,256]{1,0:T(8,128)(2,1)S(1)}, bf16[72,256]{1,0:T(8,128)(2,1)S(1)}, u32[]{:S(2)}, u32[]{:S(2)}) collective-permute-start(bf16[72,256]{1,0:T(8,128)(2,1)S(1)} %get-tuple-element.46), channel_id=1, source_target_pairs={{0,2},{1,3},{2,0},{3,1},{4,6},{5,7},{6,4},{7,5},{8,10},{9,11},{10,... | collective-permute-start | bytes 110600 | tf_op jit(solution)/shard_map/ppermute | solution.py:189
  96.2 8.0 %collective-permute-start.14 = (bf16[72,256]{1,0:T(8,128)(2,1)S(1)}, bf16[72,256]{1,0:T(8,128)(2,1)S(1)}, u32[]{:S(2)}, u32[]{:S(2)}) collective-permute-start(bf16[72,256]{1,0:T(8,128)(2,1)S(1)} %get-tuple-element.47), channel_id=1, source_target_pairs={{0,3},{1,0},{2,1},{3,2},{4,7},{5,4},{6,5},{7,6},{8,11},{9,8},{10,9... | collective-permute-start | bytes 110600 | tf_op jit(solution)/shard_map/ppermute | solution.py:189
  98.7 5.4 %collective-permute-start.7 = (bf16[64,256]{1,0:T(8,128)(2,1)S(1)}, bf16[64,256]{1,0:T(8,128)(2,1)S(1)}, u32[]{:S(2)}, u32[]{:S(2)}) collective-permute-start(bf16[64,256]{1,0:T(8,128)(2,1)S(1)} %copy-done.12), channel_id=1, source_target_pairs={{0,2},{1,3},{2,0},{3,1},{4,6},{5,7},{6,4},{7,5},{8,10},{9,11},{10,... | collective-permute-start | bytes 98312 | tf_op jit(solution)/shard_map/ppermute | solution.py:189
  98.7 5.4 %collective-permute-start.8 = (bf16[64,256]{1,0:T(8,128)(2,1)S(1)}, bf16[64,256]{1,0:T(8,128)(2,1)S(1)}, u32[]{:S(2)}, u32[]{:S(2)}) collective-permute-start(bf16[64,256]{1,0:T(8,128)(2,1)S(1)} %get-tuple-element.38), channel_id=1, source_target_pairs={{0,3},{1,0},{2,1},{3,2},{4,7},{5,4},{6,5},{7,6},{8,11},{9,8},{10,9... | collective-permute-start | bytes 98312 | tf_op jit(solution)/shard_map/ppermute | solution.py:189

commit v4 on v3

--- a/solution.py
+++ b/solution.py
@@ -58,27 +58,51 @@
     out_ref[...] = jnp.broadcast_to(jnp.sum(found, axis=1, keepdims=True), (PEERS, TILE))
 
 
-def gather_send_kernel(x_ref, want_ref, feat_ref, out_ref, row_ref, want_smem, sem):
+def gather_send_kernel(x_ref, want_ref, feat_ref, state_ref, out_ref, row_ref, want_smem, sem):
     lane = lax.broadcasted_iota(jnp.int32, (PEERS, TILE), 1)
     peer = lax.broadcasted_iota(jnp.int32, (PEERS, TILE), 0)
     row_ref[...] = jnp.sum(jnp.where(lane == peer, want_ref[...], 0), axis=0, keepdims=True)
     copy = pltpu.make_async_copy(row_ref, want_smem, sem)
     copy.start()
     copy.wait()
+    state = state_ref[...]
     for e in range(PEERS):
-        out_ref[e] = feat_ref[want_smem[0, e] * REP + x_ref[0]]
-
-
-def gather_rep_kernel(x_ref, map_ref, arrived_ref, state_ref, *refs):
+        rows = feat_ref[want_smem[0, e] * REP + x_ref[0]]
+        for t in range(8):
+            out_ref[e, :, t * TILE : (t + 1) * TILE] = rows[t // 2 * 8 : t // 2 * 8 + 8, t % 2 * TILE : (t % 2 + 1) * TILE]
+        out_ref[e, :, 8 * TILE :] = state
+
+
+def gather_rep_kernel(x_ref, map_ref, arrived_ref, *refs):
     outs = refs[REP - 1 :]
     for k in range(CHUNKS):
         for d in range(REP):
             column = ((x_ref[0] + d) % REP) * 4 + k * PER_CHUNK
             for j in range(SLOTS):
                 owner = map_ref[j % 4, column + j // 4] // 16
-                outs[k * REP + d][j] = arrived_ref[owner]
-    for e in range(PEERS):
-        outs[-1][e] = state_ref[...]
+                for t in range(8):
+                    piece = arrived_ref[owner, :, t * TILE : (t + 1) * TILE]
+                    outs[k * REP + d][j, t // 2 * 8 : t // 2 * 8 + 8, t % 2 * TILE : (t % 2 + 1) * TILE] = piece
+
+
+def thirds(value):
+    high = value.astype(BF16).astype(jnp.float32)
+    middle = (value - high).astype(BF16).astype(jnp.float32)
+    return high, middle, value - high - middle
+
+
+def join_virtual_kernel(arrived_ref, heads_ref):
+    parts = arrived_ref[:, :, 8 * TILE :].astype(jnp.float32)
+    flat = parts.reshape(PEERS * 2 * G, TILE)
+    weighted = (flat + pltpu.roll(flat, TILE - HEAD, 1) + pltpu.roll(flat, TILE - 2 * HEAD, 1)).reshape(parts.shape)
+    total = parts[:, :, 96:97] + parts[:, :, 97:98] + parts[:, :, 98:99]
+    top = parts[:, :, 99:100] + parts[:, :, 100:101] + parts[:, :, 101:102]
+    scale = jnp.exp2((top - jnp.max(top, axis=0, keepdims=True)) * EXP2_SCALE)
+    heads = jnp.sum(weighted * scale, axis=0) * (1.0 / jnp.sum(total * scale, axis=0))
+    lane = lax.broadcasted_iota(jnp.int32, (2 * G, TILE), 1)
+    heads = jnp.where(lane < HEAD, heads, 0.0)
+    moved = pltpu.roll(heads, HEAD, 1)
+    heads_ref[...] = jnp.concatenate([heads[:G] + moved[G:], jnp.zeros((G, TILE), jnp.float32)], axis=0).astype(BF16)
 
 
 def prepare_kernel(
@@ -101,7 +125,14 @@
     p = jnp.exp2((s - top) * EXP2_SCALE)
     total = jnp.sum(p, axis=1, keepdims=True)
     w = dot(p, kv.astype(jnp.float32), NN, lax.Precision.HIGHEST)
-    state_ref[...] = jnp.where(lane < 64, w, jnp.where(lane < 96, total, top))
+    w = jnp.where(row < G, w, pltpu.roll(w, TILE - HEAD, 1))
+    parts = thirds(w)
+    state = jnp.where(lane < HEAD, parts[0], 0.0)
+    for i in (1, 2):
+        state = jnp.where((lane >= i * HEAD) & (lane < (i + 1) * HEAD), pltpu.roll(parts[i], i * HEAD, 1), state)
+    for i, column in enumerate((*thirds(total), *thirds(top))):
+        state = jnp.where(lane == 96 + i, column, state)
+    state_ref[...] = state.astype(BF16)
     column = lax.broadcasted_iota(jnp.int32, (TILE, TILE), 0)
     for c in range(4):
         first = pl.multiple_of(x_ref[0] * 512 + c * TILE, TILE)
@@ -142,9 +173,12 @@
     bias_ref, refs = refs[0], refs[1:]
     packs, refs = refs[:REP], refs[REP:]
     vs_ref, refs = refs[0], refs[1:]
-    if chunk == CHUNKS - 1:
-        states_ref, refs = refs[0], refs[1:]
-    outs, scratch, kv_ref = refs[:REP], refs[REP], refs[REP + 1]
+    last = chunk == CHUNKS - 1
+    if last:
+        heads_ref, before_ref, refs = refs[0], refs[1], refs[2:]
+        outs, scratch, kv_ref = refs[:REP], refs[REP], refs[REP + 1]
+    else:
+        rows_ref, kv_ref = refs
     rows = []
     for i in range(PER_CHUNK):
         c = chunk * PER_CHUNK + i
@@ -152,33 +186,25 @@
         near = [n[4 * i : 4 * i + 4].reshape(TILE, D) for n in ns]
         source = jnp.concatenate([own, *near, vs_ref[...]], axis=0)
         rows.append(attention_rows(own, source, bias_ref[c * TILE : (c + 1) * TILE, :], packs, kv_ref))
+    if not last:
+        rows_ref[...] = jnp.concatenate(rows, axis=0)
+        return
     w = jnp.concatenate([p[TILE:, :] for p in packs], axis=0)
-    scratch[...] = dot(jnp.concatenate(rows, axis=0), w).T
+    scratch[...] = dot(jnp.concatenate([before_ref[...], *rows], axis=0), w).T
     for d in range(REP):
         first = pl.multiple_of(((x_ref[0] + d) % REP) * WIDTH, WIDTH)
         outs[d][:WIDTH, :] = scratch[pl.ds(first, WIDTH), :].astype(BF16)
-    if chunk == CHUNKS - 1:
-        states = states_ref[...]
-        top = jnp.max(states[:, :, 96:97], axis=0, keepdims=True)
-        joined = jnp.sum(states * jnp.exp2((states[:, :, 96:97] - top) * EXP2_SCALE), axis=0)
-        heads = joined * (1.0 / joined[:, WIDTH : WIDTH + 1])
-        lane = lax.broadcasted_iota(jnp.int32, (G, TILE), 1)
-        heads = jnp.where(lane < HEAD, heads[:G], jnp.where(lane < WIDTH, heads[G:], 0.0))
-        heads = jnp.concatenate([heads, jnp.zeros((G, TILE), jnp.float32)], axis=0)
-        heads = jnp.concatenate([heads, jnp.zeros((2 * G, NODES_CHUNK - TILE), jnp.float32)], axis=1)
-        for d in range(REP):
-            outs[d][WIDTH:, :] = heads.astype(BF16)
+        outs[d][WIDTH:, :TILE] = heads_ref[...]
+        outs[d][WIDTH:, TILE:] = jnp.zeros((2 * G, 3 * TILE), BF16)
 
 
 def assemble_kernel(x_ref, *refs):
-    pieces, refs = refs[: REP * CHUNKS], refs[REP * CHUNKS :]
-    packs, (out_ref, virtual_ref, scratch) = refs[:REP], refs[REP:]
+    pieces, packs, (out_ref, virtual_ref, scratch) = refs[:REP], refs[REP : 2 * REP], refs[2 * REP :]
     total = jnp.zeros((2 * G, D), jnp.float32)
     for d in range(REP):
         first = pl.multiple_of(((x_ref[0] + REP - d) % REP) * 512, 512)
-        for k in range(CHUNKS):
-            out_ref[:, pl.ds(first + k * NODES_CHUNK, NODES_CHUNK)] = pieces[k * REP + d][:WIDTH, :]
-        total = total + dot(pieces[(CHUNKS - 1) * REP + d][WIDTH:, :TILE], packs[d][TILE:, :])
+        out_ref[:, pl.ds(first, 512)] = pieces[d][:WIDTH, :]
+        total = total + dot(pieces[d][WIDTH:, :TILE], packs[d][TILE:, :])
     scratch[...] = total.T
     own = scratch[pl.ds(pl.multiple_of(x_ref[0] * WIDTH, WIDTH), WIDTH), :]
     virtual_ref[...] = own.T[:G, :].astype(BF16)
@@ -211,7 +237,7 @@
             vmem_out((2048, D), BF16),
             vmem_out((D, D), BF16),
             vmem_out((TILE, D), BF16),
-            vmem_out((2 * G, TILE), jnp.float32),
+            vmem_out((2 * G, TILE), BF16),
             vmem_out((512, TILE), jnp.float32),
         ],
         in_specs=[SMEM] + [VMEM] * 7,
@@ -223,8 +249,8 @@
 
     outgoing = pl.pallas_call(
         gather_send_kernel,
-        out_shape=vmem_out((PEERS, QUARTER, D), BF16),
-        in_specs=[SMEM, VMEM, VMEM],
+        out_shape=vmem_out((PEERS, 8, 9 * TILE), BF16),
+        in_specs=[SMEM] + [VMEM] * 3,
         out_specs=VMEM,
         scratch_shapes=[
             pltpu.VMEM((1, TILE), jnp.int32),
@@ -233,39 +259,50 @@
         ],
         compiler_params=params(2),
         name="gather_send",
-    )(x_one, in_vmem(wanted.reshape(PEERS, TILE)), in_vmem(rows_in_vmem.reshape(PEERS, QUARTER, D)))
+    )(x_one, in_vmem(wanted.reshape(PEERS, TILE)), in_vmem(rows_in_vmem.reshape(PEERS, QUARTER, D)), in_vmem(state))
     arrived = lax.all_to_all(outgoing, "nodes", 0, 0, tiled=True)
 
     sends = pl.pallas_call(
         gather_rep_kernel,
-        out_shape=[vmem_out((SLOTS, QUARTER, D), BF16)] * (CHUNKS * REP) + [vmem_out((PEERS, 2 * G, TILE), jnp.float32)],
-        in_specs=[SMEM, SMEM] + [VMEM] * (REP + 1),
-        out_specs=[VMEM] * (CHUNKS * REP + 1),
+        out_shape=[vmem_out((SLOTS, QUARTER, D), BF16)] * (CHUNKS * REP),
+        in_specs=[SMEM, SMEM] + [VMEM] * REP,
+        out_specs=[VMEM] * (CHUNKS * REP),
         compiler_params=params(2),
         name="gather_rep",
-    )(x_one, map_t, in_vmem(arrived), in_vmem(state), *packs[1:])
+    )(x_one, map_t, in_vmem(arrived), *packs[1:])
     pieces = [send_rep(sends[k * REP : k * REP + REP]) for k in range(CHUNKS)]
-    states = lax.all_to_all(sends[-1], "nodes", 0, 0, tiled=True)
-
-    received = []
+    heads = pl.pallas_call(
+        join_virtual_kernel,
+        out_shape=vmem_out((2 * G, TILE), BF16),
+        in_specs=[VMEM],
+        out_specs=VMEM,
+        compiler_params=params(4),
+        name="join_virtual",
+    )(in_vmem(arrived))
+
+    rows = None
     for k in range(CHUNKS):
         last = k == CHUNKS - 1
-        height = WIDTH + (2 * G if last else 0)
         args = [x_one, in_vmem(rows_in_vmem), *map(in_vmem, pieces[k]), in_vmem(bias), *packs, in_vmem(virtual_rows)]
-        args += [in_vmem(states)] if last else []
-        outs = pl.pallas_call(
+        args += [in_vmem(heads), in_vmem(rows)] if last else []
+        if last:
+            out_shape = [vmem_out((WIDTH + 2 * G, 512), BF16)] * REP
+        else:
+            out_shape = vmem_out((NODES_CHUNK, 2 * D), BF16)
+        rows = pl.pallas_call(
             lambda *refs, k=k: attention_kernel(k, *refs),
-            out_shape=[vmem_out((height, NODES_CHUNK), BF16)] * REP,
+            out_shape=out_shape,
             in_specs=[SMEM] + [VMEM] * (len(args) - 1),
-            out_specs=[VMEM] * REP,
-            scratch_shapes=[pltpu.VMEM((D, NODES_CHUNK), jnp.float32), pltpu.VMEM((6 * TILE, 2 * D), BF16)],
+            out_specs=[VMEM] * REP if last else VMEM,
+            scratch_shapes=[pltpu.VMEM((D, 512), jnp.float32)] * last + [pltpu.VMEM((6 * TILE, 2 * D), BF16)],
             compiler_params=params(24),
         )(*args)
-        received += send_rep(outs)
+    received = send_rep(rows)
+    return_shape = [jax.ShapeDtypeStruct((WIDTH, 2048), BF16), jax.ShapeDtypeStruct((G, WIDTH), BF16)]
     node_out, virtual_out = pl.pallas_call(
         assemble_kernel,
-        out_shape=[jax.ShapeDtypeStruct((WIDTH, 2048), BF16), jax.ShapeDtypeStruct((G, WIDTH), BF16)],
-        in_specs=[SMEM] + [VMEM] * (REP * CHUNKS + REP),
+        out_shape=return_shape,
+        in_specs=[SMEM] + [VMEM] * (2 * REP),
         out_specs=[VMEM] * 2,
         scratch_shapes=[pltpu.VMEM((D, 2 * G), jnp.float32)],
         compiler_params=params(4),

time: 106 us -> 98.2 us (0.926)
  starting transfers between devices: 49.8 us -> 40.4 us
    all_to_all x1 -> x0, starting transfers between devices: 6.66 us -> none  [shards(): states = lax.all_to_all(sends[-1], 'nodes', 0, 0, tiled=True)]
    ppermute x15 -> x12, starting transfers between devices: 24.1 us -> 19.1 us  [send_rep(): lax.ppermute(values[d], 'rep', [(i, (i + d) % REP) for i in range(REP)])]
    all_to_all x1, waiting for transfers between devices: 15.5 us -> 18.3 us  [shards(): arrived = lax.all_to_all(outgoing, 'nodes', 0, 0, tiled=True)]
    all_to_all x1, starting transfers between devices: 7.14 us -> 9.54 us  [shards(): arrived = lax.all_to_all(outgoing, 'nodes', 0, 0, tiled=True)]
    all_to_all x1, waiting for transfers between devices: 3.17 us -> 0.78 us  [shards(): lax.all_to_all(wanted_from.reshape(PEERS, 1, TILE), 'nodes', 0, 0, tiled=...]
    unnamed x26 -> x18, local copies, waits for them, and re-layouts: 5.49 us -> 6.52 us
    ppermute x15 -> x12, waiting for transfers between devices: 14.1 us -> 14.5 us  [send_rep(): lax.ppermute(values[d], 'rep', [(i, (i + d) % REP) for i in range(REP)])]
    pallas_call x4 -> x5, Pallas kernels: 12 us -> 11.9 us  [the longest x2 8.6 us: shards(): pl.pallas_call(lambda *refs, k=k: attention_kernel(k, *refs), out_shape=o...]
  transfers between devices with their start and end apart: 18 -> 14, of which waited for: 8 -> 11; matrix products, arithmetic and copies ran while one was open for 0% -> 0% of each run, Pallas kernels for 11% -> 7%
where the time goes in v4:
time: 98.2 us; the launch traced here: 96.8 us
  starting transfers between devices  40.4 us (41%)
  waiting for transfers between devices  33.6 us (34%)
  Pallas kernels  15.5 us (16%)
  local copies, waits for them, and re-layouts  6.52 us (7%)
    ppermute x12, starting transfers between devices, send_rep(): lax.ppermute(values[d], 'rep', [(i, (i + d) % REP) for i in range(REP)])  19.1 us
    all_to_all x1, waiting for transfers between devices, shards(): arrived = lax.all_to_all(outgoing, 'nodes', 0, 0, tiled=True)  18.3 us
    ppermute x12, waiting for transfers between devices, send_rep(): lax.ppermute(values[d], 'rep', [(i, (i + d) % REP) for i in range(REP)])  14.5 us
    all_to_all x1, starting transfers between devices, shards(): lax.all_to_all(wanted_from.reshape(PEERS, 1, TILE), 'nodes', 0, 0, tiled=...  11.8 us
    all_to_all x1, starting transfers between devices, shards(): arrived = lax.all_to_all(outgoing, 'nodes', 0, 0, tiled=True)  9.54 us
    pallas_call x2, Pallas kernels, shards(): pl.pallas_call(lambda *refs, k=k: attention_kernel(k, *refs), out_shape=o...  8.6 us
    unnamed x18, local copies, waits for them, and re-layouts  6.52 us
  transfers between devices with their start and end apart: 14, of which 11 were waited for; matrix products, arithmetic and copies ran while one was open for 0% of the time, Pallas kernels for 7%

profile of v4, /device:TPU:32, one launch (start us, length us, event | category | flops | bytes accessed | tf_op | source)
XLA Modules:
  0.0 96.8 jit_solution(1290496376161563218)
XLA Ops:
  0.6 0.0 copy-start.6
  0.6 0.7 copy-done.6
  1.3 0.7 wanted_rows.1
  2.0 11.8 %all-to-all-start = ((s32[64,1,128]{2,1,0:T(1,128)}), s32[64,1,128]{2,1,0:T(1,128)S(1)}, u32[]{:S(2)}, u32[]{:S(2)}) async-start(s32[64,1,128]{2,1,0:T(1,128)} %bitcast.7), calls=%async_computation | async-start | bytes 65536 | tf_op jit(solution)/shard_map/all_to_all | solution.py:232
  13.8 0.0 copy-start
  13.8 1.2 %copy-done = bf16[2048,256]{1,0:T(8,128)(2,1)S(1)} copy-done((bf16[2048,256]{1,0:T(8,128)(2,1)S(1)}, bf16[2048,256]{1,0:T(8,128)(2,1)}, u32[]{:S(2)}) %copy-start) | copy-done | bytes 1048600
  15.0 0.0 copy-start.1
  15.0 0.9 copy-done.1
  15.9 0.0 copy-start.2
  16.0 0.8 copy-done.2
  16.7 0.0 copy-start.3
  16.7 0.8 copy-done.3
  17.5 0.0 copy-start.4
  17.5 0.8 copy-done.4
  18.2 0.0 copy-start.5
  18.2 0.8 copy-done.5
  19.0 0.0 copy-start.8
  19.0 0.7 copy-done.8
  19.7 1.9 %prepare.1 = (bf16[2048,256]{1,0:T(8,128)(2,1)S(1)}, bf16[256,256]{1,0:T(8,128)(2,1)S(1)}, bf16[128,256]{1,0:T(8,128)(2,1)S(1)}, bf16[8,128]{1,0:T(8,128)(2,1)S(1)}, f32[512,128]{1,0:T(8,128)S(1)}) custom-call(s32[1]{0:T(128)} %bitcast.x_ref.refs_0_, bf16[2048,256]{1,0:T(8,128)(2,1)S(1)} %copy-done, bf16[64,256]{1,0:T(8,128)(2,1)S(1)} %bitcast.15, ...), custom_call_target="tpu_custom_call" | custom-call | tf_op jit(solution)/shard_map/prepare/pallas_call | solution.py:234
  21.6 0.8 all-to-all-done
  22.4 1.8 %gather_send.1 = bf16[64,8,1152]{2,1,0:T(8,128)(2,1)} custom-call(s32[1]{0:T(128)} %bitcast.x_ref.refs_0_, s32[64,128]{1,0:T(8,128)S(1)} %bitcast.13, bf16[64,32,256]{2,1,0:T(8,128)(2,1)S(1)} %bitcast.12, bf16[8,128]{1,0:T(8,128)(2,1)S(1)} %get-tuple-element.22.state_ref), custom_call_target="tpu_custom_call" | custom-call | tf_op jit(solution)/shard_map/gather_send/pallas_call | solution.py:250
  24.2 0.0 copy-start.7
  24.2 9.5 %all-to-all-start.1 = ((bf16[64,8,1152]{2,1,0:T(8,128)(2,1)}), bf16[64,8,1152]{2,1,0:T(8,128)(2,1)S(1)}, u32[]{:S(2)}, u32[]{:S(2)}) async-start(bf16[64,8,1152]{2,1,0:T(8,128)(2,1)} %gather_send.1), calls=%async_computation.1 | async-start | bytes 2359296 | tf_op jit(solution)/shard_map/all_to_all | solution.py:263
  33.7 2.8 %collective-permute-start.2 = (bf16[256,256]{1,0:T(8,128)(2,1)S(1)}, bf16[256,256]{1,0:T(8,128)(2,1)S(1)}, u32[]{:S(2)}, u32[]{:S(2)}) collective-permute-start(bf16[256,256]{1,0:T(8,128)(2,1)S(1)} %get-tuple-element.23.refs_7_.refs_4_), channel_id=1, source_target_pairs={{0,3},{1,0},{2,1},{3,2},{4,7},{5,4},{6,5},{7,6},{8,11},{9,8},{10,9... | collective-permute-start | bytes 393224 | tf_op jit(solution)/shard_map/ppermute | solution.py:215
  36.6 0.8 collective-permute-start.1
  37.4 0.9 collective-permute-start
  38.3 4.2 %collective-permute-done.2.refs_2_.refs_10_.refs_7_ = bf16[256,256]{1,0:T(8,128)(2,1)S(1)} collective-permute-done((bf16[256,256]{1,0:T(8,128)(2,1)S(1)}, bf16[256,256]{1,0:T(8,128)(2,1)S(1)}, u32[]{:S(2)}, u32[]{:S(2)}) %collective-permute-start.2) | collective-permute-done | bytes 131104 | tf_op jit(solution)/shard_map/ppermute | solution.py:215
  42.5 2.0 %collective-permute-done.1.refs_1_.refs_9_.refs_6_ = bf16[256,256]{1,0:T(8,128)(2,1)S(1)} collective-permute-done((bf16[256,256]{1,0:T(8,128)(2,1)S(1)}, bf16[256,256]{1,0:T(8,128)(2,1)S(1)}, u32[]{:S(2)}, u32[]{:S(2)}) %collective-permute-start.1) | collective-permute-done | bytes 131104 | tf_op jit(solution)/shard_map/ppermute | solution.py:215
  44.4 1.7 %collective-permute-done.refs_0_.refs_8_.refs_5_ = bf16[256,256]{1,0:T(8,128)(2,1)S(1)} collective-permute-done((bf16[256,256]{1,0:T(8,128)(2,1)S(1)}, bf16[256,256]{1,0:T(8,128)(2,1)S(1)}, u32[]{:S(2)}, u32[]{:S(2)}) %collective-permute-start) | collective-permute-done | bytes 131104 | tf_op jit(solution)/shard_map/ppermute | solution.py:215
  46.1 18.3 %all-to-all-done.1.arrived_ref = bf16[64,8,1152]{2,1,0:T(8,128)(2,1)S(1)} async-done(((bf16[64,8,1152]{2,1,0:T(8,128)(2,1)}), bf16[64,8,1152]{2,1,0:T(8,128)(2,1)S(1)}, u32[]{:S(2)}, u32[]{:S(2)}) %all-to-all-start.1) | async-done | bytes 1179680 | tf_op jit(solution)/shard_map/all_to_all | solution.py:263
  64.5 0.0 copy-done.7
  64.5 0.9 gather_rep.1
  65.4 1.6 %collective-permute-start.6 = (bf16[8,32,256]{2,1,0:T(8,128)(2,1)S(1)}, bf16[8,32,256]{2,1,0:T(8,128)(2,1)S(1)}, u32[]{:S(2)}, u32[]{:S(2)}) collective-permute-start(bf16[8,32,256]{2,1,0:T(8,128)(2,1)S(1)} %get-tuple-element.31), channel_id=1, source_target_pairs={{0,1},{1,2},{2,3},{3,0},{4,5},{5,6},{6,7},{7,4},{8,9},{9,10},{10,1... | collective-permute-start | bytes 393224 | tf_op jit(solution)/shard_map/ppermute | solution.py:215
  67.0 2.7 %collective-permute-start.7 = (bf16[8,32,256]{2,1,0:T(8,128)(2,1)S(1)}, bf16[8,32,256]{2,1,0:T(8,128)(2,1)S(1)}, u32[]{:S(2)}, u32[]{:S(2)}) collective-permute-start(bf16[8,32,256]{2,1,0:T(8,128)(2,1)S(1)} %get-tuple-element.32), channel_id=1, source_target_pairs={{0,2},{1,3},{2,0},{3,1},{4,6},{5,7},{6,4},{7,5},{8,10},{9,11},{10,... | collective-permute-start | bytes 393224 | tf_op jit(solution)/shard_map/ppermute | solution.py:215
  69.7 1.4 %collective-permute-start.8 = (bf16[8,32,256]{2,1,0:T(8,128)(2,1)S(1)}, bf16[8,32,256]{2,1,0:T(8,128)(2,1)S(1)}, u32[]{:S(2)}, u32[]{:S(2)}) collective-permute-start(bf16[8,32,256]{2,1,0:T(8,128)(2,1)S(1)} %get-tuple-element.33), channel_id=1, source_target_pairs={{0,3},{1,0},{2,1},{3,2},{4,7},{5,4},{6,5},{7,6},{8,11},{9,8},{10,9... | collective-permute-start | bytes 393224 | tf_op jit(solution)/shard_map/ppermute | solution.py:215
  71.1 0.6 collective-permute-start.3
  71.7 0.9 collective-permute-start.4
  72.6 0.0 collective-permute-done.6.refs_3_
  72.6 2.0 %collective-permute-start.5 = (bf16[8,32,256]{2,1,0:T(8,128)(2,1)S(1)}, bf16[8,32,256]{2,1,0:T(8,128)(2,1)S(1)}, u32[]{:S(2)}, u32[]{:S(2)}) collective-permute-start(bf16[8,32,256]{2,1,0:T(8,128)(2,1)S(1)} %get-tuple-element.27), channel_id=1, source_target_pairs={{0,3},{1,0},{2,1},{3,2},{4,7},{5,4},{6,5},{7,6},{8,11},{9,8},{10,9... | collective-permute-start | bytes 393224 | tf_op jit(solution)/shard_map/ppermute | solution.py:215
  74.6 0.5 join_virtual.1.refs_12_
  75.1 1.7 %collective-permute-done.7.refs_4_ = bf16[8,32,256]{2,1,0:T(8,128)(2,1)S(1)} collective-permute-done((bf16[8,32,256]{2,1,0:T(8,128)(2,1)S(1)}, bf16[8,32,256]{2,1,0:T(8,128)(2,1)S(1)}, u32[]{:S(2)}, u32[]{:S(2)}) %collective-permute-start.7) | collective-permute-done | bytes 131104 | tf_op jit(solution)/shard_map/ppermute | solution.py:215
  76.9 0.2 collective-permute-done.8.refs_5_
  77.1 4.2 %shard_map.95.refs_13_ = bf16[256,512]{1,0:T(8,128)(2,1)S(1)} custom-call(s32[1]{0:T(128)} %bitcast.x_ref.refs_0_, bf16[2048,256]{1,0:T(8,128)(2,1)S(1)} %get-tuple-element.21.refs_1_, bf16[8,32,256]{2,1,0:T(8,128)(2,1)S(1)} %get-tuple-element.30.refs_2_, bf16[8,32,256]{2,1,0:T(8,128)(2,1)S(1)} %collective-permute-done.6.refs_3_, ...), custom_call_target="tpu_custom_call" | custom-call | tf_op jit(solution)/shard_map/pallas_call | solution.py:292
  81.3 0.0 collective-permute-done.3.refs_3_
  81.3 0.3 collective-permute-done.4.refs_4_
  81.6 0.0 collective-permute-done.5.refs_5_
  81.6 4.4 %shard_map.96 = (bf16[72,512]{1,0:T(8,128)(2,1)S(1)}, bf16[72,512]{1,0:T(8,128)(2,1)S(1)}, bf16[72,512]{1,0:T(8,128)(2,1)S(1)}, bf16[72,512]{1,0:T(8,128)(2,1)S(1)}) custom-call(s32[1]{0:T(128)} %bitcast.x_ref.refs_0_, bf16[2048,256]{1,0:T(8,128)(2,1)S(1)} %get-tuple-element.21.refs_1_, bf16[8,32,256]{2,1,0:T(8,128)(2,1)S(1)} %get-tuple-element.24.refs_2_, ...), custom_call_target="tpu_custom_call" | custom-call | tf_op jit(solution)/shard_map/pallas_call | solution.py:292
  86.1 1.9 %collective-permute-start.9 = (bf16[72,512]{1,0:T(8,128)(2,1)S(1)}, bf16[72,512]{1,0:T(8,128)(2,1)S(1)}, u32[]{:S(2)}, u32[]{:S(2)}) collective-permute-start(bf16[72,512]{1,0:T(8,128)(2,1)S(1)} %get-tuple-element.35), channel_id=1, source_target_pairs={{0,1},{1,2},{2,3},{3,0},{4,5},{5,6},{6,7},{7,4},{8,9},{9,10},{10,1... | collective-permute-start | bytes 221192 | tf_op jit(solution)/shard_map/ppermute | solution.py:215
  87.9 3.5 %collective-permute-start.10 = (bf16[72,512]{1,0:T(8,128)(2,1)S(1)}, bf16[72,512]{1,0:T(8,128)(2,1)S(1)}, u32[]{:S(2)}, u32[]{:S(2)}) collective-permute-start(bf16[72,512]{1,0:T(8,128)(2,1)S(1)} %get-tuple-element.36), channel_id=1, source_target_pairs={{0,2},{1,3},{2,0},{3,1},{4,6},{5,7},{6,4},{7,5},{8,10},{9,11},{10,... | collective-permute-start | bytes 221192 | tf_op jit(solution)/shard_map/ppermute | solution.py:215
  91.5 0.0 collective-permute-start.11
  91.5 0.9 collective-permute-done.9.refs_1_
  92.3 2.2 %collective-permute-done.10.refs_2_ = bf16[72,512]{1,0:T(8,128)(2,1)S(1)} collective-permute-done((bf16[72,512]{1,0:T(8,128)(2,1)S(1)}, bf16[72,512]{1,0:T(8,128)(2,1)S(1)}, u32[]{:S(2)}, u32[]{:S(2)}) %collective-permute-start.10) | collective-permute-done | bytes 73760 | tf_op jit(solution)/shard_map/ppermute | solution.py:215
  94.6 1.2 %collective-permute-done.11.refs_3_ = bf16[72,512]{1,0:T(8,128)(2,1)S(1)} collective-permute-done((bf16[72,512]{1,0:T(8,128)(2,1)S(1)}, bf16[72,512]{1,0:T(8,128)(2,1)S(1)}, u32[]{:S(2)}, u32[]{:S(2)}) %collective-permute-start.11) | collective-permute-done | bytes 73760 | tf_op jit(solution)/shard_map/ppermute | solution.py:215
  95.8 1.0 %assemble.1 = (bf16[64,2048]{1,0:T(8,128)(2,1)}, bf16[4,64]{1,0:T(4,128)(2,1)}) custom-call(s32[1]{0:T(128)} %bitcast.x_ref.refs_0_, bf16[72,512]{1,0:T(8,128)(2,1)S(1)} %get-tuple-element.34.refs_0_, bf16[72,512]{1,0:T(8,128)(2,1)S(1)} %collective-permute-done.9.refs_1_, bf16[72,512]{1,0:T(8,128)(2,1)S(1)} %collective-permute-done.10.refs_2_, ...), custom_call_target="tpu_custom_call" | custom-call | tf_op jit(solution)/shard_map/assemble/pallas_call | solution.py:302
Async XLA Ops:
  0.6 0.7 copy-start.6
  2.0 20.3 %all-to-all-start = ((s32[64,1,128]{2,1,0:T(1,128)}), s32[64,1,128]{2,1,0:T(1,128)S(1)}, u32[]{:S(2)}, u32[]{:S(2)}) async-start(s32[64,1,128]{2,1,0:T(1,128)} %bitcast.7), calls=%async_computation | async-start | bytes 65536 | tf_op jit(solution)/shard_map/all_to_all | solution.py:232
  13.8 1.2 %copy-start = (bf16[2048,256]{1,0:T(8,128)(2,1)S(1)}, bf16[2048,256]{1,0:T(8,128)(2,1)}, u32[]{:S(2)}) copy-start(bf16[2048,256]{1,0:T(8,128)(2,1)} %feat_in.1) | copy-start | bytes 3145732
  15.0 0.9 copy-start.1
  15.9 0.8 copy-start.2
  16.7 0.8 copy-start.3
  17.5 0.8 copy-start.4
  18.2 0.8 copy-start.5
  19.0 0.7 copy-start.8
  24.2 40.3 %copy-start.7 = (s32[16,4]{0,1:T(4,128)S(1)}, s32[16,4]{0,1:T(4,128)}, u32[]{:S(2)}) copy-start(s32[16,4]{0,1:T(4,128)} %param.14) | copy-start | bytes 772
  24.2 40.3 %all-to-all-start.1 = ((bf16[64,8,1152]{2,1,0:T(8,128)(2,1)}), bf16[64,8,1152]{2,1,0:T(8,128)(2,1)S(1)}, u32[]{:S(2)}, u32[]{:S(2)}) async-start(bf16[64,8,1152]{2,1,0:T(8,128)(2,1)} %gather_send.1), calls=%async_computation.1 | async-start | bytes 2359296 | tf_op jit(solution)/shard_map/all_to_all | solution.py:263
  33.7 8.7 %collective-permute-start.2 = (bf16[256,256]{1,0:T(8,128)(2,1)S(1)}, bf16[256,256]{1,0:T(8,128)(2,1)S(1)}, u32[]{:S(2)}, u32[]{:S(2)}) collective-permute-start(bf16[256,256]{1,0:T(8,128)(2,1)S(1)} %get-tuple-element.23.refs_7_.refs_4_), channel_id=1, source_target_pairs={{0,3},{1,0},{2,1},{3,2},{4,7},{5,4},{6,5},{7,6},{8,11},{9,8},{10,9... | collective-permute-start | bytes 393224 | tf_op jit(solution)/shard_map/ppermute | solution.py:215
  36.6 7.9 %collective-permute-start.1 = (bf16[256,256]{1,0:T(8,128)(2,1)S(1)}, bf16[256,256]{1,0:T(8,128)(2,1)S(1)}, u32[]{:S(2)}, u32[]{:S(2)}) collective-permute-start(bf16[256,256]{1,0:T(8,128)(2,1)S(1)} %get-tuple-element.23.refs_7_.refs_4_), channel_id=1, source_target_pairs={{0,2},{1,3},{2,0},{3,1},{4,6},{5,7},{6,4},{7,5},{8,10},{9,11},{10,... | collective-permute-start | bytes 393224 | tf_op jit(solution)/shard_map/ppermute | solution.py:215
  37.4 8.8 %collective-permute-start = (bf16[256,256]{1,0:T(8,128)(2,1)S(1)}, bf16[256,256]{1,0:T(8,128)(2,1)S(1)}, u32[]{:S(2)}, u32[]{:S(2)}) collective-permute-start(bf16[256,256]{1,0:T(8,128)(2,1)S(1)} %get-tuple-element.23.refs_7_.refs_4_), channel_id=1, source_target_pairs={{0,1},{1,2},{2,3},{3,0},{4,5},{5,6},{6,7},{7,4},{8,9},{9,10},{10,1... | collective-permute-start | bytes 393224 | tf_op jit(solution)/shard_map/ppermute | solution.py:215
  65.4 7.2 %collective-permute-start.6 = (bf16[8,32,256]{2,1,0:T(8,128)(2,1)S(1)}, bf16[8,32,256]{2,1,0:T(8,128)(2,1)S(1)}, u32[]{:S(2)}, u32[]{:S(2)}) collective-permute-start(bf16[8,32,256]{2,1,0:T(8,128)(2,1)S(1)} %get-tuple-element.31), channel_id=1, source_target_pairs={{0,1},{1,2},{2,3},{3,0},{4,5},{5,6},{6,7},{7,4},{8,9},{9,10},{10,1... | collective-permute-start | bytes 393224 | tf_op jit(solution)/shard_map/ppermute | solution.py:215
  67.0 9.9 %collective-permute-start.7 = (bf16[8,32,256]{2,1,0:T(8,128)(2,1)S(1)}, bf16[8,32,256]{2,1,0:T(8,128)(2,1)S(1)}, u32[]{:S(2)}, u32[]{:S(2)}) collective-permute-start(bf16[8,32,256]{2,1,0:T(8,128)(2,1)S(1)} %get-tuple-element.32), channel_id=1, source_target_pairs={{0,2},{1,3},{2,0},{3,1},{4,6},{5,7},{6,4},{7,5},{8,10},{9,11},{10,... | collective-permute-start | bytes 393224 | tf_op jit(solution)/shard_map/ppermute | solution.py:215
  69.7 7.4 %collective-permute-start.8 = (bf16[8,32,256]{2,1,0:T(8,128)(2,1)S(1)}, bf16[8,32,256]{2,1,0:T(8,128)(2,1)S(1)}, u32[]{:S(2)}, u32[]{:S(2)}) collective-permute-start(bf16[8,32,256]{2,1,0:T(8,128)(2,1)S(1)} %get-tuple-element.33), channel_id=1, source_target_pairs={{0,3},{1,0},{2,1},{3,2},{4,7},{5,4},{6,5},{7,6},{8,11},{9,8},{10,9... | collective-permute-start | bytes 393224 | tf_op jit(solution)/shard_map/ppermute | solution.py:215
  71.1 10.1 %collective-permute-start.3 = (bf16[8,32,256]{2,1,0:T(8,128)(2,1)S(1)}, bf16[8,32,256]{2,1,0:T(8,128)(2,1)S(1)}, u32[]{:S(2)}, u32[]{:S(2)}) collective-permute-start(bf16[8,32,256]{2,1,0:T(8,128)(2,1)S(1)} %get-tuple-element.25), channel_id=1, source_target_pairs={{0,1},{1,2},{2,3},{3,0},{4,5},{5,6},{6,7},{7,4},{8,9},{9,10},{10,1... | collective-permute-start | bytes 393224 | tf_op jit(solution)/shard_map/ppermute | solution.py:215
  71.7 9.9 %collective-permute-start.4 = (bf16[8,32,256]{2,1,0:T(8,128)(2,1)S(1)}, bf16[8,32,256]{2,1,0:T(8,128)(2,1)S(1)}, u32[]{:S(2)}, u32[]{:S(2)}) collective-permute-start(bf16[8,32,256]{2,1,0:T(8,128)(2,1)S(1)} %get-tuple-element.26), channel_id=1, source_target_pairs={{0,2},{1,3},{2,0},{3,1},{4,6},{5,7},{6,4},{7,5},{8,10},{9,11},{10,... | collective-permute-start | bytes 393224 | tf_op jit(solution)/shard_map/ppermute | solution.py:215
  72.6 9.0 %collective-permute-start.5 = (bf16[8,32,256]{2,1,0:T(8,128)(2,1)S(1)}, bf16[8,32,256]{2,1,0:T(8,128)(2,1)S(1)}, u32[]{:S(2)}, u32[]{:S(2)}) collective-permute-start(bf16[8,32,256]{2,1,0:T(8,128)(2,1)S(1)} %get-tuple-element.27), channel_id=1, source_target_pairs={{0,3},{1,0},{2,1},{3,2},{4,7},{5,4},{6,5},{7,6},{8,11},{9,8},{10,9... | collective-permute-start | bytes 393224 | tf_op jit(solution)/shard_map/ppermute | solution.py:215
  86.1 6.3 %collective-permute-start.9 = (bf16[72,512]{1,0:T(8,128)(2,1)S(1)}, bf16[72,512]{1,0:T(8,128)(2,1)S(1)}, u32[]{:S(2)}, u32[]{:S(2)}) collective-permute-start(bf16[72,512]{1,0:T(8,128)(2,1)S(1)} %get-tuple-element.35), channel_id=1, source_target_pairs={{0,1},{1,2},{2,3},{3,0},{4,5},{5,6},{6,7},{7,4},{8,9},{9,10},{10,1... | collective-permute-start | bytes 221192 | tf_op jit(solution)/shard_map/ppermute | solution.py:215
  87.9 6.7 %collective-permute-start.10 = (bf16[72,512]{1,0:T(8,128)(2,1)S(1)}, bf16[72,512]{1,0:T(8,128)(2,1)S(1)}, u32[]{:S(2)}, u32[]{:S(2)}) collective-permute-start(bf16[72,512]{1,0:T(8,128)(2,1)S(1)} %get-tuple-element.36), channel_id=1, source_target_pairs={{0,2},{1,3},{2,0},{3,1},{4,6},{5,7},{6,4},{7,5},{8,10},{9,11},{10,... | collective-permute-start | bytes 221192 | tf_op jit(solution)/shard_map/ppermute | solution.py:215
  91.5 4.4 %collective-permute-start.11 = (bf16[72,512]{1,0:T(8,128)(2,1)S(1)}, bf16[72,512]{1,0:T(8,128)(2,1)S(1)}, u32[]{:S(2)}, u32[]{:S(2)}) collective-permute-start(bf16[72,512]{1,0:T(8,128)(2,1)S(1)} %get-tuple-element.37), channel_id=1, source_target_pairs={{0,3},{1,0},{2,1},{3,2},{4,7},{5,4},{6,5},{7,6},{8,11},{9,8},{10,9... | collective-permute-start | bytes 221192 | tf_op jit(solution)/shard_map/ppermute | solution.py:215

commit v5 on v4

v5 whole, which is shorter than its diff:
```python
import math

import jax
import jax.numpy as jnp
from jax import lax
from jax.experimental import pallas as pl
from jax.experimental.pallas import tpu as pltpu
from jax.sharding import PartitionSpec as P


D = 256
H = 8
TILE = 128
G = 4
HEAD = D // H
REP = 4
PEERS = 64
WIDTH = D // REP
QUARTER = TILE // REP
SCORE_SCALE = 1.0 / math.sqrt(HEAD)
EXP2_SCALE = SCORE_SCALE * math.log2(math.e)
NEG = -1e30
NT = (((1,), (1,)), ((), ()))
NN = (((1,), (0,)), ((), ()))

SMEM = pl.BlockSpec(memory_space=pltpu.SMEM)
VMEM = pl.BlockSpec(memory_space=pltpu.VMEM)
CHUNKS = ((0, 1, 2), (3,))
KEYS = 5 * TILE + 16
PIECES = 4
BF16 = jnp.bfloat16


def dot(a, b, dims=NN, precision=None):
    return lax.dot_general(a, b, dims, precision=precision, preferred_element_type=jnp.float32)


def in_vmem(value):
    return pltpu.with_memory_space_constraint(value, pltpu.VMEM)


def in_hbm(value):
    return pltpu.with_memory_space_constraint(value, pltpu.HBM)


def vmem_out(shape, dtype):
    return pltpu.VMEM(shape, dtype)


def params(mib):
    return pltpu.CompilerParams(vmem_limit_bytes=mib * 1024 * 1024)


def wanted_rows_kernel(map_ref, out_ref):
    blocks = map_ref[...]
    peer = lax.broadcasted_iota(jnp.int32, (PEERS, 16), 0)
    found = jnp.zeros((PEERS, 16), jnp.int32)
    for j in range(4):
        row = blocks[j : j + 1, :]
        found = found + jnp.where(peer == row // 16, row % 16, 0)
    out_ref[...] = jnp.broadcast_to(jnp.sum(found, axis=1, keepdims=True), (PEERS, TILE))


def gather_send_kernel(want_ref, feat_ref, state_ref, out_ref, row_ref, want_smem, sem):
    lane = lax.broadcasted_iota(jnp.int32, (PEERS, TILE), 1)
    peer = lax.broadcasted_iota(jnp.int32, (PEERS, TILE), 0)
    row_ref[...] = jnp.sum(jnp.where(lane == peer, want_ref[...], 0), axis=0, keepdims=True)
    copy = pltpu.make_async_copy(row_ref, want_smem, sem)
    copy.start()
    copy.wait()
    state = state_ref[...]
    for e in range(PEERS):
        rows = feat_ref[want_smem[0, e] * REP + lax.axis_index("rep")]
        for t in range(8):
            out_ref[e, :, t * TILE : (t + 1) * TILE] = rows[t // 2 * 8 : t // 2 * 8 + 8, t % 2 * TILE : (t % 2 + 1) * TILE]
        out_ref[e, :, 8 * TILE :] = state


def gather_rep_kernel(map_ref, arrived_ref, *refs):
    outs = refs[REP - 1 :]
    for k, blocks in enumerate(CHUNKS):
        for d in range(REP):
            column = ((lax.axis_index("rep") + d) % REP) * 4 + blocks[0]
            for j in range(4 * len(blocks)):
                owner = map_ref[j % 4, column + j // 4] // 16
                for t in range(8):
                    piece = arrived_ref[owner, :, t * TILE : (t + 1) * TILE]
                    outs[k * REP + d][j, t // 2 * 8 : t // 2 * 8 + 8, t % 2 * TILE : (t % 2 + 1) * TILE] = piece


def thirds(value):
    high = value.astype(BF16).astype(jnp.float32)
    middle = (value - high).astype(BF16).astype(jnp.float32)
    return high, middle, value - high - middle


def join_virtual_kernel(arrived_ref, heads_ref):
    parts = arrived_ref[:, :, 8 * TILE :].astype(jnp.float32)
    flat = parts.reshape(PEERS * 2 * G, TILE)
    weighted = (flat + pltpu.roll(flat, TILE - HEAD, 1) + pltpu.roll(flat, TILE - 2 * HEAD, 1)).reshape(parts.shape)
    total = parts[:, :, 96:97] + parts[:, :, 97:98] + parts[:, :, 98:99]
    top = parts[:, :, 99:100] + parts[:, :, 100:101] + parts[:, :, 101:102]
    scale = jnp.exp2((top - jnp.max(top, axis=0, keepdims=True)) * EXP2_SCALE)
    heads = jnp.sum(weighted * scale, axis=0) * (1.0 / jnp.sum(total * scale, axis=0))
    lane = lax.broadcasted_iota(jnp.int32, (2 * G, TILE), 1)
    heads = jnp.where(lane < HEAD, heads, 0.0)
    moved = pltpu.roll(heads, HEAD, 1)
    heads_ref[...] = jnp.concatenate([heads[:G] + moved[G:], jnp.zeros((G, TILE), jnp.float32)], axis=0).astype(BF16)


def prepare_kernel(
    feat_in, value_in, key_in, out_in, query_in, vs_ref, feat_ref, pack_ref, virtual_ref, state_ref, sems
):
    copies = [
        pltpu.make_async_copy(part, pack_ref.at[i * WIDTH : (i + 1) * WIDTH], sems.at[i])
        for i, part in enumerate((value_in, key_in, out_in, query_in))
    ]
    size = 2048 // PIECES
    for i in range(PIECES):
        rows = slice(i * size, (i + 1) * size)
        copies.append(pltpu.make_async_copy(feat_in.at[rows], feat_ref.at[rows], sems.at[4 + i]))
    for copy in copies:
        copy.start()
    vs = vs_ref[...]
    virtual_ref[...] = jnp.concatenate([vs, jnp.zeros((TILE - G, D), BF16)], axis=0)
    for copy in copies[:4]:
        copy.wait()
    q = dot(jnp.concatenate([vs, vs], axis=0), pack_ref[TILE:, :], NT)
    lane = lax.broadcasted_iota(jnp.int32, (2 * G, TILE), 1)
    row = lax.broadcasted_iota(jnp.int32, (2 * G, TILE), 0)
    first = WIDTH + HEAD * (row // G)
    q = jnp.where((lane >= first) & (lane < first + HEAD), q, 0.0).astype(BF16)
    weights = pack_ref[:TILE, :]
    kv, s = [], []
    for i in range(PIECES):
        copies[4 + i].wait()
        kv.append(dot(feat_ref[i * size : (i + 1) * size, :], weights, NT).astype(BF16))
        s.append(dot(q, kv[i], NT))
    s = jnp.concatenate(s, axis=1)
    top = jnp.max(s, axis=1, keepdims=True)
    p = jnp.exp2((s - top) * EXP2_SCALE)
    total = jnp.sum(p, axis=1, keepdims=True)
    w = dot(jnp.concatenate(thirds(p), axis=0).astype(BF16), jnp.concatenate(kv, axis=0))
    w = w[: 2 * G] + w[2 * G : 4 * G] + w[4 * G :]
    w = jnp.where(row < G, w, pltpu.roll(w, TILE - HEAD, 1))
    parts = thirds(w)
    state = jnp.where(lane < HEAD, parts[0], 0.0)
    for i in (1, 2):
        state = jnp.where((lane >= i * HEAD) & (lane < (i + 1) * HEAD), pltpu.roll(parts[i], i * HEAD, 1), state)
    for i, column in enumerate((*thirds(total), *thirds(top))):
        state = jnp.where(lane == 96 + i, column, state)
    state_ref[...] = state.astype(BF16)


def masks_kernel(links_ref, bias_ref):
    position = lax.broadcasted_iota(jnp.int32, (TILE, TILE), 0)
    for c in range(4):
        first = pl.multiple_of(lax.axis_index("rep") * 512 + c * TILE, TILE)
        links = links_ref[:, pl.ds(first, TILE)]
        linked = position == links[0:1, :]
        for n in range(1, 16):
            linked = linked | (position == links[n : n + 1, :])
        bias_ref[:, c * TILE : (c + 1) * TILE] = jnp.where(linked, 0.0, NEG)


def attention(blocks, feat_ref, ns, bias_ref, packs, vs_ref, key_ref, value_ref, score_ref, weight_ref, query_ref):
    lane = lax.broadcasted_iota(jnp.int32, (TILE, TILE), 1)
    row = lax.broadcasted_iota(jnp.int32, (16, 2 * TILE), 0)
    w_value = jnp.concatenate([p[:WIDTH, :] for p in packs], axis=0)
    w_key = jnp.concatenate([p[WIDTH : 2 * WIDTH, :] for p in packs], axis=0)
    w_query = jnp.concatenate([p[3 * WIDTH :, :] for p in packs], axis=0)
    for b in range(2):
        weight_ref[b, KEYS:, :] = jnp.zeros((6 * TILE - KEYS, 2 * TILE), BF16)

    def project(i):
        first = pl.multiple_of(lax.axis_index("rep") * 512 + blocks[i] * TILE, TILE)
        own = feat_ref[pl.ds(first, TILE), :]
        near = [n[4 * i : 4 * i + 4].reshape(TILE, D) for n in ns]
        key_ref[i] = dot(jnp.concatenate([own, *near, vs_ref[:16, :]], axis=0), w_key, NT).astype(BF16)
        value_ref[i] = dot(w_value, jnp.concatenate([own, *near, vs_ref[...]], axis=0), NT).astype(BF16)
        q = dot(own, w_query, NT)
        for pair in range(4):
            part = q[:, pair // 2 * TILE : (pair // 2 + 1) * TILE]
            for k in range(2):
                low = (2 * pair + k) % 4 * HEAD
                masked = jnp.where((lane >= low) & (lane < low + HEAD), part, 0.0).astype(BF16)
                query_ref[i, pair, k * TILE : (k + 1) * TILE, :] = masked

    def score(n):
        i, pair = divmod(n, 4)
        s = dot(key_ref[i, :, pair // 2 * TILE : (pair // 2 + 1) * TILE], query_ref[i, pair], NT)
        bias = bias_ref[:, blocks[i] * TILE : (blocks[i] + 1) * TILE]
        bias = jnp.concatenate([bias, bias], axis=1)
        near, far = s[:TILE] + bias, jnp.where(row < G, s[5 * TILE :], NEG)
        score_ref[n % 2] = jnp.concatenate([near, s[TILE : 5 * TILE], far], axis=0)

    def weigh(n):
        s = score_ref[n % 2]
        p = jnp.exp2((s - jnp.max(s, axis=0, keepdims=True)) * EXP2_SCALE)
        weight_ref[n % 2, :KEYS, :] = p.astype(BF16)
        return 1.0 / jnp.sum(p, axis=0, keepdims=True)

    def blend(n, scale):
        i, pair = divmod(n, 4)
        o = dot(value_ref[i, pair * WIDTH : (pair + 1) * WIDTH, :], weight_ref[n % 2]) * scale
        return jnp.concatenate([o[:HEAD, :TILE], o[HEAD:, TILE:]], axis=0)

    project(0)
    score(0)
    parts, scale = [], None
    for n in range(4 * len(blocks)):
        if n % 4 == 1 and n // 4 + 1 < len(blocks):
            project(n // 4 + 1)
        if n + 1 < 4 * len(blocks):
            score(n + 1)
        if n:
            parts.append(blend(n - 1, scale))
        scale = weigh(n)
    parts.append(blend(4 * len(blocks) - 1, scale))
    heads = [jnp.concatenate(parts[4 * i : 4 * i + 4], axis=0) for i in range(len(blocks))]
    w_out = jnp.concatenate([p[2 * WIDTH : 3 * WIDTH, :] for p in packs], axis=0)
    return dot(w_out, jnp.concatenate(heads, axis=1).astype(BF16), (((0,), (0,)), ((), ()))).astype(BF16)


def attention_kernel(chunk, feat_ref, *refs):
    ns, refs = refs[:REP], refs[REP:]
    bias_ref, refs = refs[0], refs[1:]
    packs, refs = refs[:REP], refs[REP:]
    vs_ref, refs = refs[0], refs[1:]
    refs, scratch = refs[:-5], refs[-5:]
    out = attention(CHUNKS[chunk], feat_ref, ns, bias_ref, packs, vs_ref, *scratch)
    if chunk == 0:
        refs[0][...] = out
        return
    heads_ref, before_ref, *outs, own_ref = refs
    own_ref[...] = out
    done = before_ref.shape[1]
    for d in range(REP):
        first = pl.multiple_of(((lax.axis_index("rep") + d) % REP) * WIDTH, WIDTH)
        outs[d][:WIDTH, :done] = before_ref[pl.ds(first, WIDTH), :]
        outs[d][:WIDTH, done:] = own_ref[pl.ds(first, WIDTH), :]
        outs[d][WIDTH:, :TILE] = heads_ref[...]
        outs[d][WIDTH:, TILE:] = jnp.zeros((2 * G, 3 * TILE), BF16)


def assemble_kernel(*refs):
    pieces, packs, (out_ref, virtual_ref, scratch) = refs[:REP], refs[REP : 2 * REP], refs[2 * REP :]
    total = jnp.zeros((2 * G, D), jnp.float32)
    for d in range(REP):
        first = pl.multiple_of(((lax.axis_index("rep") + REP - d) % REP) * 512, 512)
        out_ref[:, pl.ds(first, 512)] = pieces[d][:WIDTH, :]
        total = total + dot(pieces[d][WIDTH:, :TILE], packs[d][TILE:, :])
    scratch[...] = total.T
    own = scratch[pl.ds(pl.multiple_of(lax.axis_index("rep") * WIDTH, WIDTH), WIDTH), :]
    virtual_ref[...] = own.T[:G, :].astype(BF16)


def send_rep(values):
    return [values[0]] + [
        lax.ppermute(values[d], "rep", [(i, (i + d) % REP) for i in range(REP)]) for d in range(1, REP)
    ]


def shards(features, virtual_state, w_query, w_key, w_value, w_out, tile_map, local_nbr):
    map_t = tile_map.T

    wanted_from = pl.pallas_call(
        wanted_rows_kernel,
        out_shape=vmem_out((PEERS, TILE), jnp.int32),
        in_specs=[VMEM],
        out_specs=VMEM,
        compiler_params=params(2),
        name="wanted_rows",
    )(in_vmem(map_t))
    wanted = lax.all_to_all(wanted_from.reshape(PEERS, 1, TILE), "nodes", 0, 0, tiled=True)

    rows_in_vmem, pack, virtual_rows, state = pl.pallas_call(
        prepare_kernel,
        out_shape=[
            vmem_out((2048, D), BF16),
            vmem_out((D, D), BF16),
            vmem_out((TILE, D), BF16),
            vmem_out((2 * G, TILE), BF16),
        ],
        in_specs=[pl.BlockSpec(memory_space=pl.ANY)] * 5 + [VMEM],
        out_specs=[VMEM] * 4,
        scratch_shapes=[pltpu.SemaphoreType.DMA((4 + PIECES,))],
        compiler_params=params(16),
        name="prepare",
    )(*map(in_hbm, (features, w_value.T, w_key.T, w_out, w_query.T)), virtual_state)
    bias = pl.pallas_call(
        masks_kernel,
        out_shape=vmem_out((TILE, 512), jnp.float32),
        in_specs=[VMEM],
        out_specs=VMEM,
        compiler_params=params(2),
        name="masks",
    )(local_nbr.T)
    packs = [in_vmem(p) for p in send_rep([pack] * REP)]

    outgoing = pl.pallas_call(
        gather_send_kernel,
        out_shape=vmem_out((PEERS, 8, 9 * TILE), BF16),
        in_specs=[VMEM] * 3,
        out_specs=VMEM,
        scratch_shapes=[
            pltpu.VMEM((1, TILE), jnp.int32),
            pltpu.SMEM((1, TILE), jnp.int32),
            pltpu.SemaphoreType.DMA,
        ],
        compiler_params=params(2),
        name="gather_send",
    )(in_vmem(wanted.reshape(PEERS, TILE)), in_vmem(rows_in_vmem.reshape(PEERS, QUARTER, D)), in_vmem(state))
    arrived = lax.all_to_all(outgoing, "nodes", 0, 0, tiled=True)

    sends = pl.pallas_call(
        gather_rep_kernel,
        out_shape=[vmem_out((4 * len(blocks), QUARTER, D), BF16) for blocks in CHUNKS for _ in range(REP)],
        in_specs=[SMEM] + [VMEM] * REP,
        out_specs=[VMEM] * (len(CHUNKS) * REP),
        compiler_params=params(2),
        name="gather_rep",
    )(map_t, in_vmem(arrived), *packs[1:])
    pieces = [send_rep(sends[k * REP : k * REP + REP]) for k in range(len(CHUNKS))]
    heads = pl.pallas_call(
        join_virtual_kernel,
        out_shape=vmem_out((2 * G, TILE), BF16),
        in_specs=[VMEM],
        out_specs=VMEM,
        compiler_params=params(4),
        name="join_virtual",
    )(in_vmem(arrived))

    rows = None
    for k, blocks in enumerate(CHUNKS):
        last = k == len(CHUNKS) - 1
        args = [in_vmem(rows_in_vmem), *map(in_vmem, pieces[k]), in_vmem(bias), *packs, in_vmem(virtual_rows)]
        args += [in_vmem(heads), in_vmem(rows)] if last else []
        count = len(blocks)
        rows = pl.pallas_call(
            lambda *refs, k=k: attention_kernel(k, *refs),
            out_shape=[vmem_out((WIDTH + 2 * G, 512), BF16)] * REP if last else vmem_out((D, count * TILE), BF16),
            in_specs=[VMEM] * len(args),
            out_specs=[VMEM] * REP if last else VMEM,
            scratch_shapes=[pltpu.VMEM((D, TILE), BF16)] * last
            + [
                pltpu.VMEM((count, KEYS, D), BF16),
                pltpu.VMEM((count, D, 6 * TILE), BF16),
                pltpu.VMEM((2, KEYS, 2 * TILE), jnp.float32),
                pltpu.VMEM((2, 6 * TILE, 2 * TILE), BF16),
                pltpu.VMEM((count, 4, 2 * TILE, TILE), BF16),
            ],
            compiler_params=params(24),
        )(*args)
    received = send_rep(rows)
    return_shape = [jax.ShapeDtypeStruct((WIDTH, 2048), BF16), jax.ShapeDtypeStruct((G, WIDTH), BF16)]
    node_out, virtual_out = pl.pallas_call(
        assemble_kernel,
        out_shape=return_shape,
        in_specs=[VMEM] * (2 * REP),
        out_specs=[VMEM] * 2,
        scratch_shapes=[pltpu.VMEM((D, 2 * G), jnp.float32)],
        compiler_params=params(4),
        name="assemble",
    )(*map(in_vmem, received), *packs)
    return node_out.T, virtual_out


def solution(mesh):
    in_specs = (
        P("nodes", None),
        P(),
        P(None, "rep"),
        P(None, "rep"),
        P(None, "rep"),
        P("rep", None),
        P("nodes", None),
        P("nodes", None),
    )
    out_specs = (P("nodes", "rep"), P(None, "rep"))
    return jax.shard_map(shards, mesh=mesh, in_specs=in_specs, out_specs=out_specs, check_vma=False)
```

time: 98.2 us -> 91.8 us (0.935)
  local copies, waits for them, and re-layouts: 6.52 us -> 1.37 us
  waiting for transfers between devices: 33.6 us -> 36.1 us
  starting transfers between devices: 40.4 us -> 38.2 us
  Pallas kernels: 15.5 us -> 14.4 us
    unnamed x18 -> x8, local copies, waits for them, and re-layouts: 6.52 us -> 1.37 us
    all_to_all x1, starting transfers between devices: 9.54 us -> 5.6 us  [shards(): arrived = lax.all_to_all(outgoing, 'nodes', 0, 0, tiled=True)]
    all_to_all x1, waiting for transfers between devices: 0.78 us -> 4.72 us  [shards(): lax.all_to_all(wanted_from.reshape(PEERS, 1, TILE), 'nodes', 0, 0, tiled=...]
    ppermute x12, waiting for transfers between devices: 14.5 us -> 11.2 us  [send_rep(): lax.ppermute(values[d], 'rep', [(i, (i + d) % REP) for i in range(REP)])]
    pallas_call x4 -> x5, Pallas kernels: 10.5 us -> 8.24 us  [the longest x2 5.86 us: shards(): pl.pallas_call(lambda *refs, k=k: attention_kernel(k, *refs), out_shape=[...]
    all_to_all x1, waiting for transfers between devices: 18.3 us -> 20.2 us  [shards(): arrived = lax.all_to_all(outgoing, 'nodes', 0, 0, tiled=True)]
    ppermute x12, starting transfers between devices: 19.1 us -> 20.8 us  [send_rep(): lax.ppermute(values[d], 'rep', [(i, (i + d) % REP) for i in range(REP)])]
    pallas_call x1, Pallas kernels: 1.94 us -> 3.16 us  [shards(): pl.pallas_call(prepare_kernel, out_shape=[vmem_out((2048, D), BF16), vmem...]
  transfers between devices with their start and end apart: 14 -> 14, of which waited for: 11 -> 9; matrix products, arithmetic and copies ran while one was open for 0% -> 0% of each run, Pallas kernels for 7% -> 9%
where the time goes in v5:
time: 91.8 us; the launch traced here: 90.8 us
  starting transfers between devices  38.2 us (42%)
  waiting for transfers between devices  36.1 us (39%)
  Pallas kernels  14.4 us (16%)
  local copies, waits for them, and re-layouts  1.37 us (1%)
    ppermute x12, starting transfers between devices, send_rep(): lax.ppermute(values[d], 'rep', [(i, (i + d) % REP) for i in range(REP)])  20.8 us
    all_to_all x1, waiting for transfers between devices, shards(): arrived = lax.all_to_all(outgoing, 'nodes', 0, 0, tiled=True)  20.2 us
    all_to_all x1, starting transfers between devices, shards(): lax.all_to_all(wanted_from.reshape(PEERS, 1, TILE), 'nodes', 0, 0, tiled=...  11.8 us
    ppermute x12, waiting for transfers between devices, send_rep(): lax.ppermute(values[d], 'rep', [(i, (i + d) % REP) for i in range(REP)])  11.2 us
    pallas_call x2, Pallas kernels, shards(): pl.pallas_call(lambda *refs, k=k: attention_kernel(k, *refs), out_shape=[...  5.86 us
    all_to_all x1, starting transfers between devices, shards(): arrived = lax.all_to_all(outgoing, 'nodes', 0, 0, tiled=True)  5.6 us
    all_to_all x1, waiting for transfers between devices, shards(): lax.all_to_all(wanted_from.reshape(PEERS, 1, TILE), 'nodes', 0, 0, tiled=...  4.72 us
    pallas_call x1, Pallas kernels, shards(): pl.pallas_call(prepare_kernel, out_shape=[vmem_out((2048, D), BF16), vmem...  3.16 us
  transfers between devices with their start and end apart: 14, of which 9 were waited for; matrix products, arithmetic and copies ran while one was open for 0% of the time, Pallas kernels for 9%

profile of v5, /device:TPU:32, one launch (start us, length us, event | category | flops | bytes accessed | tf_op | source)
XLA Modules:
  0.0 90.8 jit_solution(13248562426701593177)
XLA Ops:
  0.6 0.0 copy-start.1
  0.6 0.7 copy-done.1
  1.3 0.7 wanted_rows.1
  2.0 11.8 %all-to-all-start = ((s32[64,1,128]{2,1,0:T(1,128)}), s32[64,1,128]{2,1,0:T(1,128)S(1)}, u32[]{:S(2)}, u32[]{:S(2)}) async-start(s32[64,1,128]{2,1,0:T(1,128)} %bitcast.5), calls=%async_computation | async-start | bytes 65536 | tf_op jit(solution)/shard_map/all_to_all | solution.py:275
  13.8 0.0 copy-start.3
  13.8 0.7 copy-done.3
  14.5 3.2 %prepare.1 = (bf16[2048,256]{1,0:T(8,128)(2,1)S(1)}, bf16[256,256]{1,0:T(8,128)(2,1)S(1)}, bf16[128,256]{1,0:T(8,128)(2,1)S(1)}, bf16[8,128]{1,0:T(8,128)(2,1)S(1)}) custom-call(bf16[2048,256]{1,0:T(8,128)(2,1)} %feat_in.1, bf16[64,256]{1,0:T(8,128)(2,1)} %bitcast.16, bf16[64,256]{1,0:T(8,128)(2,1)} %bitcast.17, bf16[64,256]{1,0:T(8,128)(2,1)} %out_in.1, ...), custom_call_target="tpu_custom_call" | custom-call | tf_op jit(solution)/shard_map/prepare/pallas_call | solution.py:277
  17.7 4.7 %all-to-all-done = s32[64,1,128]{2,1,0:T(1,128)S(1)} async-done(((s32[64,1,128]{2,1,0:T(1,128)}), s32[64,1,128]{2,1,0:T(1,128)S(1)}, u32[]{:S(2)}, u32[]{:S(2)}) %all-to-all-start) | async-done | bytes 32800 | tf_op jit(solution)/shard_map/all_to_all | solution.py:275
  22.4 1.8 %gather_send.1 = bf16[64,8,1152]{2,1,0:T(8,128)(2,1)} custom-call(s32[64,128]{1,0:T(8,128)S(1)} %bitcast.12, bf16[64,32,256]{2,1,0:T(8,128)(2,1)S(1)} %bitcast.11, bf16[8,128]{1,0:T(8,128)(2,1)S(1)} %get-tuple-element.21.state_ref), custom_call_target="tpu_custom_call" | custom-call | tf_op jit(solution)/shard_map/gather_send/pallas_call | solution.py:301
  24.2 0.0 copy-start.2
  24.2 5.6 %all-to-all-start.1 = ((bf16[64,8,1152]{2,1,0:T(8,128)(2,1)}), bf16[64,8,1152]{2,1,0:T(8,128)(2,1)S(1)}, u32[]{:S(2)}, u32[]{:S(2)}) async-start(bf16[64,8,1152]{2,1,0:T(8,128)(2,1)} %gather_send.1), calls=%async_computation.1 | async-start | bytes 2359296 | tf_op jit(solution)/shard_map/all_to_all | solution.py:314
  29.8 0.0 copy-start
  29.8 1.6 %collective-permute-start = (bf16[256,256]{1,0:T(8,128)(2,1)S(1)}, bf16[256,256]{1,0:T(8,128)(2,1)S(1)}, u32[]{:S(2)}, u32[]{:S(2)}) collective-permute-start(bf16[256,256]{1,0:T(8,128)(2,1)S(1)} %get-tuple-element.22.refs_6_.refs_4_), channel_id=1, source_target_pairs={{0,1},{1,2},{2,3},{3,0},{4,5},{5,6},{6,7},{7,4},{8,9},{9,10},{10,1... | collective-permute-start | bytes 393224 | tf_op jit(solution)/shard_map/ppermute | solution.py:260
  31.4 2.7 %collective-permute-start.1 = (bf16[256,256]{1,0:T(8,128)(2,1)S(1)}, bf16[256,256]{1,0:T(8,128)(2,1)S(1)}, u32[]{:S(2)}, u32[]{:S(2)}) collective-permute-start(bf16[256,256]{1,0:T(8,128)(2,1)S(1)} %get-tuple-element.22.refs_6_.refs_4_), channel_id=1, source_target_pairs={{0,2},{1,3},{2,0},{3,1},{4,6},{5,7},{6,4},{7,5},{8,10},{9,11},{10,... | collective-permute-start | bytes 393224 | tf_op jit(solution)/shard_map/ppermute | solution.py:260
  34.1 1.4 %collective-permute-start.2 = (bf16[256,256]{1,0:T(8,128)(2,1)S(1)}, bf16[256,256]{1,0:T(8,128)(2,1)S(1)}, u32[]{:S(2)}, u32[]{:S(2)}) collective-permute-start(bf16[256,256]{1,0:T(8,128)(2,1)S(1)} %get-tuple-element.22.refs_6_.refs_4_), channel_id=1, source_target_pairs={{0,3},{1,0},{2,1},{3,2},{4,7},{5,4},{6,5},{7,6},{8,11},{9,8},{10,9... | collective-permute-start | bytes 393224 | tf_op jit(solution)/shard_map/ppermute | solution.py:260
  35.5 1.1 %collective-permute-done.refs_0_.refs_7_.refs_5_ = bf16[256,256]{1,0:T(8,128)(2,1)S(1)} collective-permute-done((bf16[256,256]{1,0:T(8,128)(2,1)S(1)}, bf16[256,256]{1,0:T(8,128)(2,1)S(1)}, u32[]{:S(2)}, u32[]{:S(2)}) %collective-permute-start) | collective-permute-done | bytes 131104 | tf_op jit(solution)/shard_map/ppermute | solution.py:260
  36.6 3.8 %collective-permute-done.1.refs_1_.refs_8_.refs_6_ = bf16[256,256]{1,0:T(8,128)(2,1)S(1)} collective-permute-done((bf16[256,256]{1,0:T(8,128)(2,1)S(1)}, bf16[256,256]{1,0:T(8,128)(2,1)S(1)}, u32[]{:S(2)}, u32[]{:S(2)}) %collective-permute-start.1) | collective-permute-done | bytes 131104 | tf_op jit(solution)/shard_map/ppermute | solution.py:260
  40.4 0.0 collective-permute-done.2.refs_2_.refs_9_.refs_7_
  40.4 20.2 %all-to-all-done.1.arrived_ref = bf16[64,8,1152]{2,1,0:T(8,128)(2,1)S(1)} async-done(((bf16[64,8,1152]{2,1,0:T(8,128)(2,1)}), bf16[64,8,1152]{2,1,0:T(8,128)(2,1)S(1)}, u32[]{:S(2)}, u32[]{:S(2)}) %all-to-all-start.1) | async-done | bytes 1179680 | tf_op jit(solution)/shard_map/all_to_all | solution.py:314
  60.5 0.0 copy-done.2
  60.5 1.0 %gather_rep.1 = (bf16[12,32,256]{2,1,0:T(8,128)(2,1)S(1)}, bf16[12,32,256]{2,1,0:T(8,128)(2,1)S(1)}, bf16[12,32,256]{2,1,0:T(8,128)(2,1)S(1)}, bf16[12,32,256]{2...) custom-call(s32[4,16]{1,0:T(4,128)S(1)} %bitcast.15, ...), custom_call_target="tpu_custom_call" | custom-call | tf_op jit(solution)/shard_map/gather_rep/pallas_call | solution.py:316
  61.5 1.6 %collective-permute-start.6 = (bf16[12,32,256]{2,1,0:T(8,128)(2,1)S(1)}, bf16[12,32,256]{2,1,0:T(8,128)(2,1)S(1)}, u32[]{:S(2)}, u32[]{:S(2)}) collective-permute-start(bf16[12,32,256]{2,1,0:T(8,128)(2,1)S(1)} %get-tuple-element.29), channel_id=1, source_target_pairs={{0,1},{1,2},{2,3},{3,0},{4,5},{5,6},{6,7},{7,4},{8,9},{9,10},{10,1... | collective-permute-start | bytes 589832 | tf_op jit(solution)/shard_map/ppermute | solution.py:260
  63.1 2.7 %collective-permute-start.7 = (bf16[12,32,256]{2,1,0:T(8,128)(2,1)S(1)}, bf16[12,32,256]{2,1,0:T(8,128)(2,1)S(1)}, u32[]{:S(2)}, u32[]{:S(2)}) collective-permute-start(bf16[12,32,256]{2,1,0:T(8,128)(2,1)S(1)} %get-tuple-element.30), channel_id=1, source_target_pairs={{0,2},{1,3},{2,0},{3,1},{4,6},{5,7},{6,4},{7,5},{8,10},{9,11},{10,... | collective-permute-start | bytes 589832 | tf_op jit(solution)/shard_map/ppermute | solution.py:260
  65.8 1.4 %collective-permute-start.8 = (bf16[12,32,256]{2,1,0:T(8,128)(2,1)S(1)}, bf16[12,32,256]{2,1,0:T(8,128)(2,1)S(1)}, u32[]{:S(2)}, u32[]{:S(2)}) collective-permute-start(bf16[12,32,256]{2,1,0:T(8,128)(2,1)S(1)} %get-tuple-element.31), channel_id=1, source_target_pairs={{0,3},{1,0},{2,1},{3,2},{4,7},{5,4},{6,5},{7,6},{8,11},{9,8},{10,9... | collective-permute-start | bytes 589832 | tf_op jit(solution)/shard_map/ppermute | solution.py:260
  67.2 0.6 collective-permute-start.3
  67.8 0.9 collective-permute-start.4
  68.7 1.1 %collective-permute-done.6.refs_2_ = bf16[12,32,256]{2,1,0:T(8,128)(2,1)S(1)} collective-permute-done((bf16[12,32,256]{2,1,0:T(8,128)(2,1)S(1)}, bf16[12,32,256]{2,1,0:T(8,128)(2,1)S(1)}, u32[]{:S(2)}, u32[]{:S(2)}) %collective-permute-start.6) | collective-permute-done | bytes 196640 | tf_op jit(solution)/shard_map/ppermute | solution.py:260
  69.8 2.3 %collective-permute-start.5 = (bf16[4,32,256]{2,1,0:T(8,128)(2,1)S(1)}, bf16[4,32,256]{2,1,0:T(8,128)(2,1)S(1)}, u32[]{:S(2)}, u32[]{:S(2)}) collective-permute-start(bf16[4,32,256]{2,1,0:T(8,128)(2,1)S(1)} %get-tuple-element.26), channel_id=1, source_target_pairs={{0,3},{1,0},{2,1},{3,2},{4,7},{5,4},{6,5},{7,6},{8,11},{9,8},{10,9... | collective-permute-start | bytes 196616 | tf_op jit(solution)/shard_map/ppermute | solution.py:260
  72.1 0.0 copy-done
  72.1 0.5 masks.1.refs_5_
  72.6 0.5 join_virtual.1.refs_11_
  73.2 2.6 %collective-permute-done.7.refs_3_ = bf16[12,32,256]{2,1,0:T(8,128)(2,1)S(1)} collective-permute-done((bf16[12,32,256]{2,1,0:T(8,128)(2,1)S(1)}, bf16[12,32,256]{2,1,0:T(8,128)(2,1)S(1)}, u32[]{:S(2)}, u32[]{:S(2)}) %collective-permute-start.7) | collective-permute-done | bytes 196640 | tf_op jit(solution)/shard_map/ppermute | solution.py:260
  75.8 0.0 collective-permute-done.8.refs_4_
  75.8 3.9 %shard_map.95.refs_12_ = bf16[256,384]{1,0:T(8,128)(2,1)S(1)} custom-call(bf16[2048,256]{1,0:T(8,128)(2,1)S(1)} %get-tuple-element.20.refs_0_, bf16[12,32,256]{2,1,0:T(8,128)(2,1)S(1)} %get-tuple-element.28.refs_1_, bf16[12,32,256]{2,1,0:T(8,128)(2,1)S(1)} %collective-permute-done.6.refs_2_, bf16[12,32,256]{2,1,0:T(8,128)(2,1)S(1)} %collective-permute-done.7.refs_3_, ...), custom_call_target="tpu_custom_call" | custom-call | tf_op jit(solution)/shard_map/pallas_call | solution.py:340
  79.8 0.0 collective-permute-done.3.refs_2_
  79.8 0.0 collective-permute-done.4.refs_3_
  79.8 0.0 collective-permute-done.5.refs_4_
  79.8 1.9 %shard_map.96 = (bf16[72,512]{1,0:T(8,128)(2,1)S(1)}, bf16[72,512]{1,0:T(8,128)(2,1)S(1)}, bf16[72,512]{1,0:T(8,128)(2,1)S(1)}, bf16[72,512]{1,0:T(8,128)(2,1)S(1)}) custom-call(bf16[2048,256]{1,0:T(8,128)(2,1)S(1)} %get-tuple-element.20.refs_0_, bf16[4,32,256]{2,1,0:T(8,128)(2,1)S(1)} %get-tuple-element.23.refs_1_, ...), custom_call_target="tpu_custom_call" | custom-call | tf_op jit(solution)/shard_map/pallas_call | solution.py:340
  81.7 2.0 %collective-permute-start.9 = (bf16[72,512]{1,0:T(8,128)(2,1)S(1)}, bf16[72,512]{1,0:T(8,128)(2,1)S(1)}, u32[]{:S(2)}, u32[]{:S(2)}) collective-permute-start(bf16[72,512]{1,0:T(8,128)(2,1)S(1)} %get-tuple-element.33), channel_id=1, source_target_pairs={{0,1},{1,2},{2,3},{3,0},{4,5},{5,6},{6,7},{7,4},{8,9},{9,10},{10,1... | collective-permute-start | bytes 221192 | tf_op jit(solution)/shard_map/ppermute | solution.py:260
  83.7 1.8 %collective-permute-start.10 = (bf16[72,512]{1,0:T(8,128)(2,1)S(1)}, bf16[72,512]{1,0:T(8,128)(2,1)S(1)}, u32[]{:S(2)}, u32[]{:S(2)}) collective-permute-start(bf16[72,512]{1,0:T(8,128)(2,1)S(1)} %get-tuple-element.34), channel_id=1, source_target_pairs={{0,2},{1,3},{2,0},{3,1},{4,6},{5,7},{6,4},{7,5},{8,10},{9,11},{10,... | collective-permute-start | bytes 221192 | tf_op jit(solution)/shard_map/ppermute | solution.py:260
  85.5 1.7 %collective-permute-start.11 = (bf16[72,512]{1,0:T(8,128)(2,1)S(1)}, bf16[72,512]{1,0:T(8,128)(2,1)S(1)}, u32[]{:S(2)}, u32[]{:S(2)}) collective-permute-start(bf16[72,512]{1,0:T(8,128)(2,1)S(1)} %get-tuple-element.35), channel_id=1, source_target_pairs={{0,3},{1,0},{2,1},{3,2},{4,7},{5,4},{6,5},{7,6},{8,11},{9,8},{10,9... | collective-permute-start | bytes 221192 | tf_op jit(solution)/shard_map/ppermute | solution.py:260
  87.3 0.9 collective-permute-done.9.refs_1_
  88.2 1.4 %collective-permute-done.10.refs_2_ = bf16[72,512]{1,0:T(8,128)(2,1)S(1)} collective-permute-done((bf16[72,512]{1,0:T(8,128)(2,1)S(1)}, bf16[72,512]{1,0:T(8,128)(2,1)S(1)}, u32[]{:S(2)}, u32[]{:S(2)}) %collective-permute-start.10) | collective-permute-done | bytes 73760 | tf_op jit(solution)/shard_map/ppermute | solution.py:260
  89.6 0.3 collective-permute-done.11.refs_3_
  89.9 0.9 %assemble.1 = (bf16[64,2048]{1,0:T(8,128)(2,1)}, bf16[4,64]{1,0:T(4,128)(2,1)}) custom-call(bf16[72,512]{1,0:T(8,128)(2,1)S(1)} %get-tuple-element.32.refs_0_, bf16[72,512]{1,0:T(8,128)(2,1)S(1)} %collective-permute-done.9.refs_1_, bf16[72,512]{1,0:T(8,128)(2,1)S(1)} %collective-permute-done.10.refs_2_, bf16[72,512]{1,0:T(8,128)(2,1)S(1)} %collective-permute-done.11.refs_3_, ...), custom_call_target="tpu_custom_call" | custom-call | tf_op jit(solution)/shard_map/assemble/pallas_call | solution.py:357
Async XLA Ops:
  0.6 0.7 copy-start.1
  2.0 20.3 %all-to-all-start = ((s32[64,1,128]{2,1,0:T(1,128)}), s32[64,1,128]{2,1,0:T(1,128)S(1)}, u32[]{:S(2)}, u32[]{:S(2)}) async-start(s32[64,1,128]{2,1,0:T(1,128)} %bitcast.5), calls=%async_computation | async-start | bytes 65536 | tf_op jit(solution)/shard_map/all_to_all | solution.py:275
  13.8 0.7 copy-start.3
  24.2 36.4 %copy-start.2 = (s32[16,4]{0,1:T(4,128)S(1)}, s32[16,4]{0,1:T(4,128)}, u32[]{:S(2)}) copy-start(s32[16,4]{0,1:T(4,128)} %param.14) | copy-start | bytes 772
  24.2 36.4 %all-to-all-start.1 = ((bf16[64,8,1152]{2,1,0:T(8,128)(2,1)}), bf16[64,8,1152]{2,1,0:T(8,128)(2,1)S(1)}, u32[]{:S(2)}, u32[]{:S(2)}) async-start(bf16[64,8,1152]{2,1,0:T(8,128)(2,1)} %gather_send.1), calls=%async_computation.1 | async-start | bytes 2359296 | tf_op jit(solution)/shard_map/all_to_all | solution.py:314
  29.8 42.3 %copy-start = (s32[2048,16]{0,1:T(8,128)S(1)}, s32[2048,16]{0,1:T(8,128)}, u32[]{:S(2)}) copy-start(s32[2048,16]{0,1:T(8,128)} %param.15) | copy-start | bytes 393220
  29.8 6.8 %collective-permute-start = (bf16[256,256]{1,0:T(8,128)(2,1)S(1)}, bf16[256,256]{1,0:T(8,128)(2,1)S(1)}, u32[]{:S(2)}, u32[]{:S(2)}) collective-permute-start(bf16[256,256]{1,0:T(8,128)(2,1)S(1)} %get-tuple-element.22.refs_6_.refs_4_), channel_id=1, source_target_pairs={{0,1},{1,2},{2,3},{3,0},{4,5},{5,6},{6,7},{7,4},{8,9},{9,10},{10,1... | collective-permute-start | bytes 393224 | tf_op jit(solution)/shard_map/ppermute | solution.py:260
  31.4 9.0 %collective-permute-start.1 = (bf16[256,256]{1,0:T(8,128)(2,1)S(1)}, bf16[256,256]{1,0:T(8,128)(2,1)S(1)}, u32[]{:S(2)}, u32[]{:S(2)}) collective-permute-start(bf16[256,256]{1,0:T(8,128)(2,1)S(1)} %get-tuple-element.22.refs_6_.refs_4_), channel_id=1, source_target_pairs={{0,2},{1,3},{2,0},{3,1},{4,6},{5,7},{6,4},{7,5},{8,10},{9,11},{10,... | collective-permute-start | bytes 393224 | tf_op jit(solution)/shard_map/ppermute | solution.py:260
  34.1 6.3 %collective-permute-start.2 = (bf16[256,256]{1,0:T(8,128)(2,1)S(1)}, bf16[256,256]{1,0:T(8,128)(2,1)S(1)}, u32[]{:S(2)}, u32[]{:S(2)}) collective-permute-start(bf16[256,256]{1,0:T(8,128)(2,1)S(1)} %get-tuple-element.22.refs_6_.refs_4_), channel_id=1, source_target_pairs={{0,3},{1,0},{2,1},{3,2},{4,7},{5,4},{6,5},{7,6},{8,11},{9,8},{10,9... | collective-permute-start | bytes 393224 | tf_op jit(solution)/shard_map/ppermute | solution.py:260
  61.5 8.3 %collective-permute-start.6 = (bf16[12,32,256]{2,1,0:T(8,128)(2,1)S(1)}, bf16[12,32,256]{2,1,0:T(8,128)(2,1)S(1)}, u32[]{:S(2)}, u32[]{:S(2)}) collective-permute-start(bf16[12,32,256]{2,1,0:T(8,128)(2,1)S(1)} %get-tuple-element.29), channel_id=1, source_target_pairs={{0,1},{1,2},{2,3},{3,0},{4,5},{5,6},{6,7},{7,4},{8,9},{9,10},{10,1... | collective-permute-start | bytes 589832 | tf_op jit(solution)/shard_map/ppermute | solution.py:260
  63.1 12.7 %collective-permute-start.7 = (bf16[12,32,256]{2,1,0:T(8,128)(2,1)S(1)}, bf16[12,32,256]{2,1,0:T(8,128)(2,1)S(1)}, u32[]{:S(2)}, u32[]{:S(2)}) collective-permute-start(bf16[12,32,256]{2,1,0:T(8,128)(2,1)S(1)} %get-tuple-element.30), channel_id=1, source_target_pairs={{0,2},{1,3},{2,0},{3,1},{4,6},{5,7},{6,4},{7,5},{8,10},{9,11},{10,... | collective-permute-start | bytes 589832 | tf_op jit(solution)/shard_map/ppermute | solution.py:260
  65.8 10.0 %collective-permute-start.8 = (bf16[12,32,256]{2,1,0:T(8,128)(2,1)S(1)}, bf16[12,32,256]{2,1,0:T(8,128)(2,1)S(1)}, u32[]{:S(2)}, u32[]{:S(2)}) collective-permute-start(bf16[12,32,256]{2,1,0:T(8,128)(2,1)S(1)} %get-tuple-element.31), channel_id=1, source_target_pairs={{0,3},{1,0},{2,1},{3,2},{4,7},{5,4},{6,5},{7,6},{8,11},{9,8},{10,9... | collective-permute-start | bytes 589832 | tf_op jit(solution)/shard_map/ppermute | solution.py:260
  67.2 12.5 %collective-permute-start.3 = (bf16[4,32,256]{2,1,0:T(8,128)(2,1)S(1)}, bf16[4,32,256]{2,1,0:T(8,128)(2,1)S(1)}, u32[]{:S(2)}, u32[]{:S(2)}) collective-permute-start(bf16[4,32,256]{2,1,0:T(8,128)(2,1)S(1)} %get-tuple-element.24), channel_id=1, source_target_pairs={{0,1},{1,2},{2,3},{3,0},{4,5},{5,6},{6,7},{7,4},{8,9},{9,10},{10,1... | collective-permute-start | bytes 196616 | tf_op jit(solution)/shard_map/ppermute | solution.py:260
  67.8 12.0 %collective-permute-start.4 = (bf16[4,32,256]{2,1,0:T(8,128)(2,1)S(1)}, bf16[4,32,256]{2,1,0:T(8,128)(2,1)S(1)}, u32[]{:S(2)}, u32[]{:S(2)}) collective-permute-start(bf16[4,32,256]{2,1,0:T(8,128)(2,1)S(1)} %get-tuple-element.25), channel_id=1, source_target_pairs={{0,2},{1,3},{2,0},{3,1},{4,6},{5,7},{6,4},{7,5},{8,10},{9,11},{10,... | collective-permute-start | bytes 196616 | tf_op jit(solution)/shard_map/ppermute | solution.py:260
  69.8 10.0 %collective-permute-start.5 = (bf16[4,32,256]{2,1,0:T(8,128)(2,1)S(1)}, bf16[4,32,256]{2,1,0:T(8,128)(2,1)S(1)}, u32[]{:S(2)}, u32[]{:S(2)}) collective-permute-start(bf16[4,32,256]{2,1,0:T(8,128)(2,1)S(1)} %get-tuple-element.26), channel_id=1, source_target_pairs={{0,3},{1,0},{2,1},{3,2},{4,7},{5,4},{6,5},{7,6},{8,11},{9,8},{10,9... | collective-permute-start | bytes 196616 | tf_op jit(solution)/shard_map/ppermute | solution.py:260
  81.7 6.4 %collective-permute-start.9 = (bf16[72,512]{1,0:T(8,128)(2,1)S(1)}, bf16[72,512]{1,0:T(8,128)(2,1)S(1)}, u32[]{:S(2)}, u32[]{:S(2)}) collective-permute-start(bf16[72,512]{1,0:T(8,128)(2,1)S(1)} %get-tuple-element.33), channel_id=1, source_target_pairs={{0,1},{1,2},{2,3},{3,0},{4,5},{5,6},{6,7},{7,4},{8,9},{9,10},{10,1... | collective-permute-start | bytes 221192 | tf_op jit(solution)/shard_map/ppermute | solution.py:260
  83.7 5.9 %collective-permute-start.10 = (bf16[72,512]{1,0:T(8,128)(2,1)S(1)}, bf16[72,512]{1,0:T(8,128)(2,1)S(1)}, u32[]{:S(2)}, u32[]{:S(2)}) collective-permute-start(bf16[72,512]{1,0:T(8,128)(2,1)S(1)} %get-tuple-element.34), channel_id=1, source_target_pairs={{0,2},{1,3},{2,0},{3,1},{4,6},{5,7},{6,4},{7,5},{8,10},{9,11},{10,... | collective-permute-start | bytes 221192 | tf_op jit(solution)/shard_map/ppermute | solution.py:260
  85.5 4.4 %collective-permute-start.11 = (bf16[72,512]{1,0:T(8,128)(2,1)S(1)}, bf16[72,512]{1,0:T(8,128)(2,1)S(1)}, u32[]{:S(2)}, u32[]{:S(2)}) collective-permute-start(bf16[72,512]{1,0:T(8,128)(2,1)S(1)} %get-tuple-element.35), channel_id=1, source_target_pairs={{0,3},{1,0},{2,1},{3,2},{4,7},{5,4},{6,5},{7,6},{8,11},{9,8},{10,9... | collective-permute-start | bytes 221192 | tf_op jit(solution)/shard_map/ppermute | solution.py:260

commit v6 on v5

--- a/solution.py
+++ b/solution.py
@@ -25,8 +25,9 @@
 
 SMEM = pl.BlockSpec(memory_space=pltpu.SMEM)
 VMEM = pl.BlockSpec(memory_space=pltpu.VMEM)
-CHUNKS = ((0, 1, 2), (3,))
-KEYS = 5 * TILE + 16
+CHUNKS = ((0, 1), (2, 3))
+NEAR = 4 * TILE
+OWN = TILE + 16
 PIECES = 4
 BF16 = jnp.bfloat16
 
@@ -61,16 +62,10 @@
     out_ref[...] = jnp.broadcast_to(jnp.sum(found, axis=1, keepdims=True), (PEERS, TILE))
 
 
-def gather_send_kernel(want_ref, feat_ref, state_ref, out_ref, row_ref, want_smem, sem):
-    lane = lax.broadcasted_iota(jnp.int32, (PEERS, TILE), 1)
-    peer = lax.broadcasted_iota(jnp.int32, (PEERS, TILE), 0)
-    row_ref[...] = jnp.sum(jnp.where(lane == peer, want_ref[...], 0), axis=0, keepdims=True)
-    copy = pltpu.make_async_copy(row_ref, want_smem, sem)
-    copy.start()
-    copy.wait()
+def gather_send_kernel(want_ref, feat_ref, state_ref, out_ref):
     state = state_ref[...]
     for e in range(PEERS):
-        rows = feat_ref[want_smem[0, e] * REP + lax.axis_index("rep")]
+        rows = feat_ref[want_ref[e : e + 1, :][0, 0] * REP + lax.axis_index("rep")]
         for t in range(8):
             out_ref[e, :, t * TILE : (t + 1) * TILE] = rows[t // 2 * 8 : t // 2 * 8 + 8, t % 2 * TILE : (t % 2 + 1) * TILE]
         out_ref[e, :, 8 * TILE :] = state
@@ -152,57 +147,70 @@
     state_ref[...] = state.astype(BF16)
 
 
-def masks_kernel(links_ref, bias_ref):
+def own_part_kernel(feat_ref, links_ref, vs_ref, *refs):
+    packs, (query_ref, score_ref, value_ref, w_out_ref) = refs[:REP], refs[REP:]
+    lane = lax.broadcasted_iota(jnp.int32, (TILE, TILE), 1)
+    row = lax.broadcasted_iota(jnp.int32, (16, 2 * TILE), 0)
     position = lax.broadcasted_iota(jnp.int32, (TILE, TILE), 0)
+    w_value = jnp.concatenate([p[:WIDTH, :] for p in packs], axis=0)
+    w_key = jnp.concatenate([p[WIDTH : 2 * WIDTH, :] for p in packs], axis=0)
+    w_query = jnp.concatenate([p[3 * WIDTH :, :] for p in packs], axis=0)
+    w_out = jnp.concatenate([p[2 * WIDTH : 3 * WIDTH, :] for p in packs], axis=0)
+    w_out_ref[...] = w_out.astype(jnp.float32).T.astype(BF16)
     for c in range(4):
         first = pl.multiple_of(lax.axis_index("rep") * 512 + c * TILE, TILE)
         links = links_ref[:, pl.ds(first, TILE)]
         linked = position == links[0:1, :]
         for n in range(1, 16):
             linked = linked | (position == links[n : n + 1, :])
-        bias_ref[:, c * TILE : (c + 1) * TILE] = jnp.where(linked, 0.0, NEG)
-
-
-def attention(blocks, feat_ref, ns, bias_ref, packs, vs_ref, key_ref, value_ref, score_ref, weight_ref, query_ref):
-    lane = lax.broadcasted_iota(jnp.int32, (TILE, TILE), 1)
-    row = lax.broadcasted_iota(jnp.int32, (16, 2 * TILE), 0)
+        bias = jnp.where(linked, 0.0, NEG)
+        bias = jnp.concatenate([bias, bias], axis=1)
+        own = feat_ref[pl.ds(first, TILE), :]
+        keys = dot(jnp.concatenate([own, vs_ref[:16, :]], axis=0), w_key, NT).astype(BF16)
+        value_ref[c] = dot(w_value, jnp.concatenate([own, vs_ref[...]], axis=0), NT).astype(BF16)
+        q = dot(own, w_query, NT)
+        for pair in range(4):
+            part = slice(pair // 2 * TILE, (pair // 2 + 1) * TILE)
+            for k in range(2):
+                low = (2 * pair + k) % 4 * HEAD
+                masked = jnp.where((lane >= low) & (lane < low + HEAD), q[:, part], 0.0).astype(BF16)
+                query_ref[c, pair, k * TILE : (k + 1) * TILE, :] = masked
+            s = dot(keys[:, part], query_ref[c, pair], NT)
+            score_ref[c, pair] = jnp.concatenate([s[:TILE] + bias, jnp.where(row < G, s[TILE:], NEG)], axis=0)
+
+
+def attention(blocks, ns, own, packs, key_ref, value_ref, score_ref, weight_ref):
+    query_ref, own_score_ref, own_value_ref, w_out_ref = own
     w_value = jnp.concatenate([p[:WIDTH, :] for p in packs], axis=0)
     w_key = jnp.concatenate([p[WIDTH : 2 * WIDTH, :] for p in packs], axis=0)
-    w_query = jnp.concatenate([p[3 * WIDTH :, :] for p in packs], axis=0)
     for b in range(2):
-        weight_ref[b, KEYS:, :] = jnp.zeros((6 * TILE - KEYS, 2 * TILE), BF16)
+        weight_ref[b, OWN : 2 * TILE, :] = jnp.zeros((2 * TILE - OWN, 2 * TILE), BF16)
 
     def project(i):
-        first = pl.multiple_of(lax.axis_index("rep") * 512 + blocks[i] * TILE, TILE)
-        own = feat_ref[pl.ds(first, TILE), :]
-        near = [n[4 * i : 4 * i + 4].reshape(TILE, D) for n in ns]
-        key_ref[i] = dot(jnp.concatenate([own, *near, vs_ref[:16, :]], axis=0), w_key, NT).astype(BF16)
-        value_ref[i] = dot(w_value, jnp.concatenate([own, *near, vs_ref[...]], axis=0), NT).astype(BF16)
-        q = dot(own, w_query, NT)
-        for pair in range(4):
-            part = q[:, pair // 2 * TILE : (pair // 2 + 1) * TILE]
-            for k in range(2):
-                low = (2 * pair + k) % 4 * HEAD
-                masked = jnp.where((lane >= low) & (lane < low + HEAD), part, 0.0).astype(BF16)
-                query_ref[i, pair, k * TILE : (k + 1) * TILE, :] = masked
+        near = jnp.concatenate([n[4 * i : 4 * i + 4].reshape(TILE, D) for n in ns], axis=0)
+        key_ref[i] = dot(near, w_key, NT).astype(BF16)
+        value_ref[i] = dot(w_value, near, NT).astype(BF16)
 
     def score(n):
         i, pair = divmod(n, 4)
-        s = dot(key_ref[i, :, pair // 2 * TILE : (pair // 2 + 1) * TILE], query_ref[i, pair], NT)
-        bias = bias_ref[:, blocks[i] * TILE : (blocks[i] + 1) * TILE]
-        bias = jnp.concatenate([bias, bias], axis=1)
-        near, far = s[:TILE] + bias, jnp.where(row < G, s[5 * TILE :], NEG)
-        score_ref[n % 2] = jnp.concatenate([near, s[TILE : 5 * TILE], far], axis=0)
+        keys = key_ref[i, :, pair // 2 * TILE : (pair // 2 + 1) * TILE]
+        score_ref[n % 2] = dot(keys, query_ref[blocks[i], pair], NT)
 
     def weigh(n):
-        s = score_ref[n % 2]
-        p = jnp.exp2((s - jnp.max(s, axis=0, keepdims=True)) * EXP2_SCALE)
-        weight_ref[n % 2, :KEYS, :] = p.astype(BF16)
-        return 1.0 / jnp.sum(p, axis=0, keepdims=True)
+        i, pair = divmod(n, 4)
+        s, own_s = score_ref[n % 2], own_score_ref[blocks[i], pair]
+        top = jnp.maximum(jnp.max(s, axis=0, keepdims=True), jnp.max(own_s, axis=0, keepdims=True))
+        p = jnp.exp2((s - top) * EXP2_SCALE)
+        own_p = jnp.exp2((own_s - top) * EXP2_SCALE)
+        weight_ref[n % 2, :OWN, :] = own_p.astype(BF16)
+        weight_ref[n % 2, 2 * TILE :, :] = p.astype(BF16)
+        return 1.0 / (jnp.sum(p, axis=0, keepdims=True) + jnp.sum(own_p, axis=0, keepdims=True))
 
     def blend(n, scale):
         i, pair = divmod(n, 4)
-        o = dot(value_ref[i, pair * WIDTH : (pair + 1) * WIDTH, :], weight_ref[n % 2]) * scale
+        rows = slice(pair * WIDTH, (pair + 1) * WIDTH)
+        values = jnp.concatenate([own_value_ref[blocks[i], rows, :], value_ref[i, rows, :]], axis=1)
+        o = dot(values, weight_ref[n % 2]) * scale
         return jnp.concatenate([o[:HEAD, :TILE], o[HEAD:, TILE:]], axis=0)
 
     project(0)
@@ -218,17 +226,13 @@
         scale = weigh(n)
     parts.append(blend(4 * len(blocks) - 1, scale))
     heads = [jnp.concatenate(parts[4 * i : 4 * i + 4], axis=0) for i in range(len(blocks))]
-    w_out = jnp.concatenate([p[2 * WIDTH : 3 * WIDTH, :] for p in packs], axis=0)
-    return dot(w_out, jnp.concatenate(heads, axis=1).astype(BF16), (((0,), (0,)), ((), ()))).astype(BF16)
-
-
-def attention_kernel(chunk, feat_ref, *refs):
-    ns, refs = refs[:REP], refs[REP:]
-    bias_ref, refs = refs[0], refs[1:]
-    packs, refs = refs[:REP], refs[REP:]
-    vs_ref, refs = refs[0], refs[1:]
-    refs, scratch = refs[:-5], refs[-5:]
-    out = attention(CHUNKS[chunk], feat_ref, ns, bias_ref, packs, vs_ref, *scratch)
+    return dot(w_out_ref[...], jnp.concatenate(heads, axis=1).astype(BF16)).astype(BF16)
+
+
+def attention_kernel(chunk, *refs):
+    ns, own, packs, refs = refs[:REP], refs[REP : 2 * REP], refs[2 * REP : 3 * REP], refs[3 * REP :]
+    refs, scratch = refs[:-4], refs[-4:]
+    out = attention(CHUNKS[chunk], ns, own, packs, *scratch)
     if chunk == 0:
         refs[0][...] = out
         return
@@ -288,26 +292,27 @@
         compiler_params=params(16),
         name="prepare",
     )(*map(in_hbm, (features, w_value.T, w_key.T, w_out, w_query.T)), virtual_state)
-    bias = pl.pallas_call(
-        masks_kernel,
-        out_shape=vmem_out((TILE, 512), jnp.float32),
-        in_specs=[VMEM],
-        out_specs=VMEM,
-        compiler_params=params(2),
-        name="masks",
-    )(local_nbr.T)
     packs = [in_vmem(p) for p in send_rep([pack] * REP)]
+
+    own = pl.pallas_call(
+        own_part_kernel,
+        out_shape=[
+            vmem_out((4, 4, 2 * TILE, TILE), BF16),
+            vmem_out((4, 4, OWN, 2 * TILE), jnp.float32),
+            vmem_out((4, D, 2 * TILE), BF16),
+            vmem_out((D, D), BF16),
+        ],
+        in_specs=[VMEM] * (3 + REP),
+        out_specs=[VMEM] * 4,
+        compiler_params=params(16),
+        name="own_part",
+    )(in_vmem(rows_in_vmem), local_nbr.T, in_vmem(virtual_rows), *packs)
 
     outgoing = pl.pallas_call(
         gather_send_kernel,
         out_shape=vmem_out((PEERS, 8, 9 * TILE), BF16),
         in_specs=[VMEM] * 3,
         out_specs=VMEM,
-        scratch_shapes=[
-            pltpu.VMEM((1, TILE), jnp.int32),
-            pltpu.SMEM((1, TILE), jnp.int32),
-            pltpu.SemaphoreType.DMA,
-        ],
         compiler_params=params(2),
         name="gather_send",
     )(in_vmem(wanted.reshape(PEERS, TILE)), in_vmem(rows_in_vmem.reshape(PEERS, QUARTER, D)), in_vmem(state))
@@ -334,7 +339,7 @@
     rows = None
     for k, blocks in enumerate(CHUNKS):
         last = k == len(CHUNKS) - 1
-        args = [in_vmem(rows_in_vmem), *map(in_vmem, pieces[k]), in_vmem(bias), *packs, in_vmem(virtual_rows)]
+        args = [*map(in_vmem, (*pieces[k], *own)), *packs]
         args += [in_vmem(heads), in_vmem(rows)] if last else []
         count = len(blocks)
         rows = pl.pallas_call(
@@ -342,13 +347,12 @@
             out_shape=[vmem_out((WIDTH + 2 * G, 512), BF16)] * REP if last else vmem_out((D, count * TILE), BF16),
             in_specs=[VMEM] * len(args),
             out_specs=[VMEM] * REP if last else VMEM,
-            scratch_shapes=[pltpu.VMEM((D, TILE), BF16)] * last
+            scratch_shapes=[pltpu.VMEM((D, count * TILE), BF16)] * last
             + [
-                pltpu.VMEM((count, KEYS, D), BF16),
-                pltpu.VMEM((count, D, 6 * TILE), BF16),
-                pltpu.VMEM((2, KEYS, 2 * TILE), jnp.float32),
-                pltpu.VMEM((2, 6 * TILE, 2 * TILE), BF16),
-                pltpu.VMEM((count, 4, 2 * TILE, TILE), BF16),
+                pltpu.VMEM((count, NEAR, D), BF16),
+                pltpu.VMEM((count, D, NEAR), BF16),
+                pltpu.VMEM((2, NEAR, 2 * TILE), jnp.float32),
+                pltpu.VMEM((2, 2 * TILE + NEAR, 2 * TILE), BF16),
             ],
             compiler_params=params(24),
         )(*args)

time: 91.8 us -> 89.8 us (0.978)
  starting transfers between devices: 38.2 us -> 36.6 us
    all_to_all x1, waiting for transfers between devices: 20.2 us -> 18.4 us  [shards(): arrived = lax.all_to_all(outgoing, 'nodes', 0, 0, tiled=True)]
    ppermute x12, waiting for transfers between devices: 11.2 us -> 13 us  [send_rep(): lax.ppermute(values[d], 'rep', [(i, (i + d) % REP) for i in range(REP)])]
    ppermute x12, starting transfers between devices: 20.8 us -> 19.1 us  [send_rep(): lax.ppermute(values[d], 'rep', [(i, (i + d) % REP) for i in range(REP)])]
    pallas_call x1, Pallas kernels: 0.51 us -> 1.75 us  [shards(): pl.pallas_call(own_part_kernel, out_shape=[vmem_out((4, 4, 2 * TILE, TILE...]
  transfers between devices with their start and end apart: 14 -> 14, of which waited for: 9 -> 10; matrix products, arithmetic and copies ran while one was open for 0% -> 0% of each run, Pallas kernels for 9% -> 9%
where the time goes in v6:
time: 89.8 us; the launch traced here: 88.9 us
  starting transfers between devices  36.6 us (41%)
  waiting for transfers between devices  36.1 us (40%)
  Pallas kernels  14.2 us (16%)
  local copies, waits for them, and re-layouts  1.36 us (2%)
    ppermute x12, starting transfers between devices, send_rep(): lax.ppermute(values[d], 'rep', [(i, (i + d) % REP) for i in range(REP)])  19.1 us
    all_to_all x1, waiting for transfers between devices, shards(): arrived = lax.all_to_all(outgoing, 'nodes', 0, 0, tiled=True)  18.4 us
    ppermute x12, waiting for transfers between devices, send_rep(): lax.ppermute(values[d], 'rep', [(i, (i + d) % REP) for i in range(REP)])  13 us
    all_to_all x1, starting transfers between devices, shards(): lax.all_to_all(wanted_from.reshape(PEERS, 1, TILE), 'nodes', 0, 0, tiled=...  11.8 us
    all_to_all x1, starting transfers between devices, shards(): arrived = lax.all_to_all(outgoing, 'nodes', 0, 0, tiled=True)  5.72 us
    pallas_call x2, Pallas kernels, shards(): pl.pallas_call(lambda *refs, k=k: attention_kernel(k, *refs), out_shape=[...  4.98 us
    all_to_all x1, waiting for transfers between devices, shards(): lax.all_to_all(wanted_from.reshape(PEERS, 1, TILE), 'nodes', 0, 0, tiled=...  4.72 us
    pallas_call x1, Pallas kernels, shards(): pl.pallas_call(prepare_kernel, out_shape=[vmem_out((2048, D), BF16), vmem...  3.16 us
  transfers between devices with their start and end apart: 14, of which 10 were waited for; matrix products, arithmetic and copies ran while one was open for 0% of the time, Pallas kernels for 9%

profile of v6, /device:TPU:32, one launch (start us, length us, event | category | flops | bytes accessed | tf_op | source)
XLA Modules:
  0.0 88.9 jit_solution(12812270517747666331)
XLA Ops:
  0.6 0.0 copy-start.1
  0.6 0.7 copy-done.1
  1.3 0.7 wanted_rows.1
  2.0 11.8 %all-to-all-start = ((s32[64,1,128]{2,1,0:T(1,128)}), s32[64,1,128]{2,1,0:T(1,128)S(1)}, u32[]{:S(2)}, u32[]{:S(2)}) async-start(s32[64,1,128]{2,1,0:T(1,128)} %bitcast.2), calls=%async_computation | async-start | bytes 65536 | tf_op jit(solution)/shard_map/all_to_all | solution.py:279
  13.8 0.0 copy-start.3
  13.8 0.7 copy-done.3
  14.5 3.2 %prepare.1 = (bf16[2048,256]{1,0:T(8,128)(2,1)S(1)}, bf16[256,256]{1,0:T(8,128)(2,1)S(1)}, bf16[128,256]{1,0:T(8,128)(2,1)S(1)}, bf16[8,128]{1,0:T(8,128)(2,1)S(1)}) custom-call(bf16[2048,256]{1,0:T(8,128)(2,1)} %feat_in.1, bf16[64,256]{1,0:T(8,128)(2,1)} %bitcast.16, bf16[64,256]{1,0:T(8,128)(2,1)} %bitcast.17, bf16[64,256]{1,0:T(8,128)(2,1)} %out_in.1, ...), custom_call_target="tpu_custom_call" | custom-call | tf_op jit(solution)/shard_map/prepare/pallas_call | solution.py:281
  17.7 4.7 %all-to-all-done = s32[64,1,128]{2,1,0:T(1,128)S(1)} async-done(((s32[64,1,128]{2,1,0:T(1,128)}), s32[64,1,128]{2,1,0:T(1,128)S(1)}, u32[]{:S(2)}, u32[]{:S(2)}) %all-to-all-start) | async-done | bytes 32800 | tf_op jit(solution)/shard_map/all_to_all | solution.py:279
  22.4 1.2 %gather_send.1 = bf16[64,8,1152]{2,1,0:T(8,128)(2,1)} custom-call(s32[64,128]{1,0:T(8,128)S(1)} %bitcast.12, bf16[64,32,256]{2,1,0:T(8,128)(2,1)S(1)} %bitcast.11, bf16[8,128]{1,0:T(8,128)(2,1)S(1)} %get-tuple-element.25.state_ref), custom_call_target="tpu_custom_call" | custom-call | tf_op jit(solution)/shard_map/gather_send/pallas_call | solution.py:311
  23.6 0.0 copy-start.2
  23.6 5.7 %all-to-all-start.1 = ((bf16[64,8,1152]{2,1,0:T(8,128)(2,1)}), bf16[64,8,1152]{2,1,0:T(8,128)(2,1)S(1)}, u32[]{:S(2)}, u32[]{:S(2)}) async-start(bf16[64,8,1152]{2,1,0:T(8,128)(2,1)} %gather_send.1), calls=%async_computation.1 | async-start | bytes 2359296 | tf_op jit(solution)/shard_map/all_to_all | solution.py:319
  29.3 0.0 copy-start
  29.3 2.8 %collective-permute-start.2 = (bf16[256,256]{1,0:T(8,128)(2,1)S(1)}, bf16[256,256]{1,0:T(8,128)(2,1)S(1)}, u32[]{:S(2)}, u32[]{:S(2)}) collective-permute-start(bf16[256,256]{1,0:T(8,128)(2,1)S(1)} %get-tuple-element.26.refs_0_.refs_8_.refs_4_), channel_id=1, source_target_pairs={{0,3},{1,0},{2,1},{3,2},{4,7},{5,4},{6,5},{7,6},{8,11},{9,8},{10,9... | collective-permute-start | bytes 393224 | tf_op jit(solution)/shard_map/ppermute | solution.py:264
  32.2 0.8 collective-permute-start.1
  33.0 0.9 collective-permute-start
  33.9 4.2 %collective-permute-done.2.refs_2_.refs_3_.refs_11_.refs_7_ = bf16[256,256]{1,0:T(8,128)(2,1)S(1)} collective-permute-done((bf16[256,256]{1,0:T(8,128)(2,1)S(1)}, bf16[256,256]{1,0:T(8,128)(2,1)S(1)}, u32[]{:S(2)}, u32[]{:S(2)}) %collective-permute-start.2) | collective-permute-done | bytes 131104 | tf_op jit(solution)/shard_map/ppermute | solution.py:264
  38.1 2.0 %collective-permute-done.1.refs_1_.refs_2_.refs_10_.refs_6_ = bf16[256,256]{1,0:T(8,128)(2,1)S(1)} collective-permute-done((bf16[256,256]{1,0:T(8,128)(2,1)S(1)}, bf16[256,256]{1,0:T(8,128)(2,1)S(1)}, u32[]{:S(2)}, u32[]{:S(2)}) %collective-permute-start.1) | collective-permute-done | bytes 131104 | tf_op jit(solution)/shard_map/ppermute | solution.py:264
  40.1 1.7 %collective-permute-done.refs_0_.refs_1_.refs_9_.refs_5_ = bf16[256,256]{1,0:T(8,128)(2,1)S(1)} collective-permute-done((bf16[256,256]{1,0:T(8,128)(2,1)S(1)}, bf16[256,256]{1,0:T(8,128)(2,1)S(1)}, u32[]{:S(2)}, u32[]{:S(2)}) %collective-permute-start) | collective-permute-done | bytes 131104 | tf_op jit(solution)/shard_map/ppermute | solution.py:264
  41.7 18.4 %all-to-all-done.1.arrived_ref = bf16[64,8,1152]{2,1,0:T(8,128)(2,1)S(1)} async-done(((bf16[64,8,1152]{2,1,0:T(8,128)(2,1)}), bf16[64,8,1152]{2,1,0:T(8,128)(2,1)S(1)}, u32[]{:S(2)}, u32[]{:S(2)}) %all-to-all-start.1) | async-done | bytes 1179680 | tf_op jit(solution)/shard_map/all_to_all | solution.py:319
  60.1 0.0 copy-done.2
  60.1 1.0 %gather_rep.1 = (bf16[8,32,256]{2,1,0:T(8,128)(2,1)S(1)}, bf16[8,32,256]{2,1,0:T(8,128)(2,1)S(1)}, bf16[8,32,256]{2,1,0:T(8,128)(2,1)S(1)}, bf16[8,32,256]{2,1,0...) custom-call(s32[4,16]{1,0:T(4,128)S(1)} %bitcast.15, ...), custom_call_target="tpu_custom_call" | custom-call | tf_op jit(solution)/shard_map/gather_rep/pallas_call | solution.py:321
  61.1 1.6 %collective-permute-start.6 = (bf16[8,32,256]{2,1,0:T(8,128)(2,1)S(1)}, bf16[8,32,256]{2,1,0:T(8,128)(2,1)S(1)}, u32[]{:S(2)}, u32[]{:S(2)}) collective-permute-start(bf16[8,32,256]{2,1,0:T(8,128)(2,1)S(1)} %get-tuple-element.37), channel_id=1, source_target_pairs={{0,1},{1,2},{2,3},{3,0},{4,5},{5,6},{6,7},{7,4},{8,9},{9,10},{10,1... | collective-permute-start | bytes 393224 | tf_op jit(solution)/shard_map/ppermute | solution.py:264
  62.6 2.7 %collective-permute-start.7 = (bf16[8,32,256]{2,1,0:T(8,128)(2,1)S(1)}, bf16[8,32,256]{2,1,0:T(8,128)(2,1)S(1)}, u32[]{:S(2)}, u32[]{:S(2)}) collective-permute-start(bf16[8,32,256]{2,1,0:T(8,128)(2,1)S(1)} %get-tuple-element.38), channel_id=1, source_target_pairs={{0,2},{1,3},{2,0},{3,1},{4,6},{5,7},{6,4},{7,5},{8,10},{9,11},{10,... | collective-permute-start | bytes 393224 | tf_op jit(solution)/shard_map/ppermute | solution.py:264
  65.4 1.4 %collective-permute-start.8 = (bf16[8,32,256]{2,1,0:T(8,128)(2,1)S(1)}, bf16[8,32,256]{2,1,0:T(8,128)(2,1)S(1)}, u32[]{:S(2)}, u32[]{:S(2)}) collective-permute-start(bf16[8,32,256]{2,1,0:T(8,128)(2,1)S(1)} %get-tuple-element.39), channel_id=1, source_target_pairs={{0,3},{1,0},{2,1},{3,2},{4,7},{5,4},{6,5},{7,6},{8,11},{9,8},{10,9... | collective-permute-start | bytes 393224 | tf_op jit(solution)/shard_map/ppermute | solution.py:264
  66.8 0.6 collective-permute-start.3
  67.4 0.9 collective-permute-start.4
  68.3 0.0 collective-permute-done.6.refs_1_
  68.3 2.0 %collective-permute-start.5 = (bf16[8,32,256]{2,1,0:T(8,128)(2,1)S(1)}, bf16[8,32,256]{2,1,0:T(8,128)(2,1)S(1)}, u32[]{:S(2)}, u32[]{:S(2)}) collective-permute-start(bf16[8,32,256]{2,1,0:T(8,128)(2,1)S(1)} %get-tuple-element.30), channel_id=1, source_target_pairs={{0,3},{1,0},{2,1},{3,2},{4,7},{5,4},{6,5},{7,6},{8,11},{9,8},{10,9... | collective-permute-start | bytes 393224 | tf_op jit(solution)/shard_map/ppermute | solution.py:264
  70.3 0.0 copy-done
  70.3 1.8 %own_part.1 = (bf16[4,4,256,128]{3,2,1,0:T(8,128)(2,1)S(1)}, f32[4,4,144,256]{3,2,1,0:T(8,128)S(1)}, bf16[4,256,256]{2,1,0:T(8,128)(2,1)S(1)}, bf16[256,256]{1,0:T(8,128)(2,1)S(1)}) custom-call(bf16[2048,256]{1,0:T(8,128)(2,1)S(1)} %get-tuple-element.24.feat_ref, s32[16,2048]{1,0:T(8,128)S(1)} %bitcast.13, bf16[128,256]{1,0:T(8,128)(2,1)S(1)} %get-tuple-element.31.vs_ref, ...), custom_call_target="tpu_custom_call" | custom-call | tf_op jit(solution)/shard_map/own_part/pallas_call | solution.py:297
  72.0 0.5 join_virtual.1.refs_12_
  72.6 0.0 collective-permute-done.7.refs_2_
  72.6 0.3 collective-permute-done.8.refs_3_
  72.8 2.5 %shard_map.95.refs_13_ = bf16[256,256]{1,0:T(8,128)(2,1)S(1)} custom-call(bf16[8,32,256]{2,1,0:T(8,128)(2,1)S(1)} %get-tuple-element.36.refs_0_, bf16[8,32,256]{2,1,0:T(8,128)(2,1)S(1)} %collective-permute-done.6.refs_1_, bf16[8,32,256]{2,1,0:T(8,128)(2,1)S(1)} %collective-permute-done.7.refs_2_, bf16[8,32,256]{2,1,0:T(8,128)(2,1)S(1)} %collective-permute-done.8.refs_3_, ...), custom_call_target="tpu_custom_call" | custom-call | tf_op jit(solution)/shard_map/pallas_call | solution.py:345
  75.3 0.0 collective-permute-done.3.refs_1_
  75.3 2.0 %collective-permute-done.4.refs_2_ = bf16[8,32,256]{2,1,0:T(8,128)(2,1)S(1)} collective-permute-done((bf16[8,32,256]{2,1,0:T(8,128)(2,1)S(1)}, bf16[8,32,256]{2,1,0:T(8,128)(2,1)S(1)}, u32[]{:S(2)}, u32[]{:S(2)}) %collective-permute-start.4) | collective-permute-done | bytes 131104 | tf_op jit(solution)/shard_map/ppermute | solution.py:264
  77.4 0.0 collective-permute-done.5.refs_3_
  77.4 2.5 %shard_map.96 = (bf16[72,512]{1,0:T(8,128)(2,1)S(1)}, bf16[72,512]{1,0:T(8,128)(2,1)S(1)}, bf16[72,512]{1,0:T(8,128)(2,1)S(1)}, bf16[72,512]{1,0:T(8,128)(2,1)S(1)}) custom-call(bf16[8,32,256]{2,1,0:T(8,128)(2,1)S(1)} %get-tuple-element.27.refs_0_, bf16[8,32,256]{2,1,0:T(8,128)(2,1)S(1)} %collective-permute-done.3.refs_1_, ...), custom_call_target="tpu_custom_call" | custom-call | tf_op jit(solution)/shard_map/pallas_call | solution.py:345
  79.9 1.4 %collective-permute-start.9 = (bf16[72,512]{1,0:T(8,128)(2,1)S(1)}, bf16[72,512]{1,0:T(8,128)(2,1)S(1)}, u32[]{:S(2)}, u32[]{:S(2)}) collective-permute-start(bf16[72,512]{1,0:T(8,128)(2,1)S(1)} %get-tuple-element.41), channel_id=1, source_target_pairs={{0,1},{1,2},{2,3},{3,0},{4,5},{5,6},{6,7},{7,4},{8,9},{9,10},{10,1... | collective-permute-start | bytes 221192 | tf_op jit(solution)/shard_map/ppermute | solution.py:264
  81.3 2.4 %collective-permute-start.10 = (bf16[72,512]{1,0:T(8,128)(2,1)S(1)}, bf16[72,512]{1,0:T(8,128)(2,1)S(1)}, u32[]{:S(2)}, u32[]{:S(2)}) collective-permute-start(bf16[72,512]{1,0:T(8,128)(2,1)S(1)} %get-tuple-element.42), channel_id=1, source_target_pairs={{0,2},{1,3},{2,0},{3,1},{4,6},{5,7},{6,4},{7,5},{8,10},{9,11},{10,... | collective-permute-start | bytes 221192 | tf_op jit(solution)/shard_map/ppermute | solution.py:264
  83.7 1.6 %collective-permute-start.11 = (bf16[72,512]{1,0:T(8,128)(2,1)S(1)}, bf16[72,512]{1,0:T(8,128)(2,1)S(1)}, u32[]{:S(2)}, u32[]{:S(2)}) collective-permute-start(bf16[72,512]{1,0:T(8,128)(2,1)S(1)} %get-tuple-element.43), channel_id=1, source_target_pairs={{0,3},{1,0},{2,1},{3,2},{4,7},{5,4},{6,5},{7,6},{8,11},{9,8},{10,9... | collective-permute-start | bytes 221192 | tf_op jit(solution)/shard_map/ppermute | solution.py:264
  85.2 0.8 collective-permute-done.9.refs_1_
  86.1 1.1 %collective-permute-done.10.refs_2_ = bf16[72,512]{1,0:T(8,128)(2,1)S(1)} collective-permute-done((bf16[72,512]{1,0:T(8,128)(2,1)S(1)}, bf16[72,512]{1,0:T(8,128)(2,1)S(1)}, u32[]{:S(2)}, u32[]{:S(2)}) %collective-permute-start.10) | collective-permute-done | bytes 73760 | tf_op jit(solution)/shard_map/ppermute | solution.py:264
  87.2 0.9 collective-permute-done.11.refs_3_
  88.0 0.9 %assemble.1 = (bf16[64,2048]{1,0:T(8,128)(2,1)}, bf16[4,64]{1,0:T(4,128)(2,1)}) custom-call(bf16[72,512]{1,0:T(8,128)(2,1)S(1)} %get-tuple-element.40.refs_0_, bf16[72,512]{1,0:T(8,128)(2,1)S(1)} %collective-permute-done.9.refs_1_, bf16[72,512]{1,0:T(8,128)(2,1)S(1)} %collective-permute-done.10.refs_2_, bf16[72,512]{1,0:T(8,128)(2,1)S(1)} %collective-permute-done.11.refs_3_, ...), custom_call_target="tpu_custom_call" | custom-call | tf_op jit(solution)/shard_map/assemble/pallas_call | solution.py:361
Async XLA Ops:
  0.6 0.7 copy-start.1
  2.0 20.3 %all-to-all-start = ((s32[64,1,128]{2,1,0:T(1,128)}), s32[64,1,128]{2,1,0:T(1,128)S(1)}, u32[]{:S(2)}, u32[]{:S(2)}) async-start(s32[64,1,128]{2,1,0:T(1,128)} %bitcast.2), calls=%async_computation | async-start | bytes 65536 | tf_op jit(solution)/shard_map/all_to_all | solution.py:279
  13.8 0.7 copy-start.3
  23.6 36.5 %copy-start.2 = (s32[16,4]{0,1:T(4,128)S(1)}, s32[16,4]{0,1:T(4,128)}, u32[]{:S(2)}) copy-start(s32[16,4]{0,1:T(4,128)} %param.14) | copy-start | bytes 772
  23.6 36.5 %all-to-all-start.1 = ((bf16[64,8,1152]{2,1,0:T(8,128)(2,1)}), bf16[64,8,1152]{2,1,0:T(8,128)(2,1)S(1)}, u32[]{:S(2)}, u32[]{:S(2)}) async-start(bf16[64,8,1152]{2,1,0:T(8,128)(2,1)} %gather_send.1), calls=%async_computation.1 | async-start | bytes 2359296 | tf_op jit(solution)/shard_map/all_to_all | solution.py:319
  29.3 40.9 %copy-start = (s32[2048,16]{0,1:T(8,128)S(1)}, s32[2048,16]{0,1:T(8,128)}, u32[]{:S(2)}) copy-start(s32[2048,16]{0,1:T(8,128)} %param.15) | copy-start | bytes 393220
  29.3 8.7 %collective-permute-start.2 = (bf16[256,256]{1,0:T(8,128)(2,1)S(1)}, bf16[256,256]{1,0:T(8,128)(2,1)S(1)}, u32[]{:S(2)}, u32[]{:S(2)}) collective-permute-start(bf16[256,256]{1,0:T(8,128)(2,1)S(1)} %get-tuple-element.26.refs_0_.refs_8_.refs_4_), channel_id=1, source_target_pairs={{0,3},{1,0},{2,1},{3,2},{4,7},{5,4},{6,5},{7,6},{8,11},{9,8},{10,9... | collective-permute-start | bytes 393224 | tf_op jit(solution)/shard_map/ppermute | solution.py:264
  32.2 7.9 %collective-permute-start.1 = (bf16[256,256]{1,0:T(8,128)(2,1)S(1)}, bf16[256,256]{1,0:T(8,128)(2,1)S(1)}, u32[]{:S(2)}, u32[]{:S(2)}) collective-permute-start(bf16[256,256]{1,0:T(8,128)(2,1)S(1)} %get-tuple-element.26.refs_0_.refs_8_.refs_4_), channel_id=1, source_target_pairs={{0,2},{1,3},{2,0},{3,1},{4,6},{5,7},{6,4},{7,5},{8,10},{9,11},{10,... | collective-permute-start | bytes 393224 | tf_op jit(solution)/shard_map/ppermute | solution.py:264
  33.0 8.8 %collective-permute-start = (bf16[256,256]{1,0:T(8,128)(2,1)S(1)}, bf16[256,256]{1,0:T(8,128)(2,1)S(1)}, u32[]{:S(2)}, u32[]{:S(2)}) collective-permute-start(bf16[256,256]{1,0:T(8,128)(2,1)S(1)} %get-tuple-element.26.refs_0_.refs_8_.refs_4_), channel_id=1, source_target_pairs={{0,1},{1,2},{2,3},{3,0},{4,5},{5,6},{6,7},{7,4},{8,9},{9,10},{10,1... | collective-permute-start | bytes 393224 | tf_op jit(solution)/shard_map/ppermute | solution.py:264
  61.1 7.2 %collective-permute-start.6 = (bf16[8,32,256]{2,1,0:T(8,128)(2,1)S(1)}, bf16[8,32,256]{2,1,0:T(8,128)(2,1)S(1)}, u32[]{:S(2)}, u32[]{:S(2)}) collective-permute-start(bf16[8,32,256]{2,1,0:T(8,128)(2,1)S(1)} %get-tuple-element.37), channel_id=1, source_target_pairs={{0,1},{1,2},{2,3},{3,0},{4,5},{5,6},{6,7},{7,4},{8,9},{9,10},{10,1... | collective-permute-start | bytes 393224 | tf_op jit(solution)/shard_map/ppermute | solution.py:264
  62.6 9.9 %collective-permute-start.7 = (bf16[8,32,256]{2,1,0:T(8,128)(2,1)S(1)}, bf16[8,32,256]{2,1,0:T(8,128)(2,1)S(1)}, u32[]{:S(2)}, u32[]{:S(2)}) collective-permute-start(bf16[8,32,256]{2,1,0:T(8,128)(2,1)S(1)} %get-tuple-element.38), channel_id=1, source_target_pairs={{0,2},{1,3},{2,0},{3,1},{4,6},{5,7},{6,4},{7,5},{8,10},{9,11},{10,... | collective-permute-start | bytes 393224 | tf_op jit(solution)/shard_map/ppermute | solution.py:264
  65.4 7.5 %collective-permute-start.8 = (bf16[8,32,256]{2,1,0:T(8,128)(2,1)S(1)}, bf16[8,32,256]{2,1,0:T(8,128)(2,1)S(1)}, u32[]{:S(2)}, u32[]{:S(2)}) collective-permute-start(bf16[8,32,256]{2,1,0:T(8,128)(2,1)S(1)} %get-tuple-element.39), channel_id=1, source_target_pairs={{0,3},{1,0},{2,1},{3,2},{4,7},{5,4},{6,5},{7,6},{8,11},{9,8},{10,9... | collective-permute-start | bytes 393224 | tf_op jit(solution)/shard_map/ppermute | solution.py:264
  66.8 8.5 %collective-permute-start.3 = (bf16[8,32,256]{2,1,0:T(8,128)(2,1)S(1)}, bf16[8,32,256]{2,1,0:T(8,128)(2,1)S(1)}, u32[]{:S(2)}, u32[]{:S(2)}) collective-permute-start(bf16[8,32,256]{2,1,0:T(8,128)(2,1)S(1)} %get-tuple-element.28), channel_id=1, source_target_pairs={{0,1},{1,2},{2,3},{3,0},{4,5},{5,6},{6,7},{7,4},{8,9},{9,10},{10,1... | collective-permute-start | bytes 393224 | tf_op jit(solution)/shard_map/ppermute | solution.py:264
  67.4 10.0 %collective-permute-start.4 = (bf16[8,32,256]{2,1,0:T(8,128)(2,1)S(1)}, bf16[8,32,256]{2,1,0:T(8,128)(2,1)S(1)}, u32[]{:S(2)}, u32[]{:S(2)}) collective-permute-start(bf16[8,32,256]{2,1,0:T(8,128)(2,1)S(1)} %get-tuple-element.29), channel_id=1, source_target_pairs={{0,2},{1,3},{2,0},{3,1},{4,6},{5,7},{6,4},{7,5},{8,10},{9,11},{10,... | collective-permute-start | bytes 393224 | tf_op jit(solution)/shard_map/ppermute | solution.py:264
  68.3 9.1 %collective-permute-start.5 = (bf16[8,32,256]{2,1,0:T(8,128)(2,1)S(1)}, bf16[8,32,256]{2,1,0:T(8,128)(2,1)S(1)}, u32[]{:S(2)}, u32[]{:S(2)}) collective-permute-start(bf16[8,32,256]{2,1,0:T(8,128)(2,1)S(1)} %get-tuple-element.30), channel_id=1, source_target_pairs={{0,3},{1,0},{2,1},{3,2},{4,7},{5,4},{6,5},{7,6},{8,11},{9,8},{10,9... | collective-permute-start | bytes 393224 | tf_op jit(solution)/shard_map/ppermute | solution.py:264
  79.9 6.2 %collective-permute-start.9 = (bf16[72,512]{1,0:T(8,128)(2,1)S(1)}, bf16[72,512]{1,0:T(8,128)(2,1)S(1)}, u32[]{:S(2)}, u32[]{:S(2)}) collective-permute-start(bf16[72,512]{1,0:T(8,128)(2,1)S(1)} %get-tuple-element.41), channel_id=1, source_target_pairs={{0,1},{1,2},{2,3},{3,0},{4,5},{5,6},{6,7},{7,4},{8,9},{9,10},{10,1... | collective-permute-start | bytes 221192 | tf_op jit(solution)/shard_map/ppermute | solution.py:264
  81.3 5.9 %collective-permute-start.10 = (bf16[72,512]{1,0:T(8,128)(2,1)S(1)}, bf16[72,512]{1,0:T(8,128)(2,1)S(1)}, u32[]{:S(2)}, u32[]{:S(2)}) collective-permute-start(bf16[72,512]{1,0:T(8,128)(2,1)S(1)} %get-tuple-element.42), channel_id=1, source_target_pairs={{0,2},{1,3},{2,0},{3,1},{4,6},{5,7},{6,4},{7,5},{8,10},{9,11},{10,... | collective-permute-start | bytes 221192 | tf_op jit(solution)/shard_map/ppermute | solution.py:264
  83.7 4.4 %collective-permute-start.11 = (bf16[72,512]{1,0:T(8,128)(2,1)S(1)}, bf16[72,512]{1,0:T(8,128)(2,1)S(1)}, u32[]{:S(2)}, u32[]{:S(2)}) collective-permute-start(bf16[72,512]{1,0:T(8,128)(2,1)S(1)} %get-tuple-element.43), channel_id=1, source_target_pairs={{0,3},{1,0},{2,1},{3,2},{4,7},{5,4},{6,5},{7,6},{8,11},{9,8},{10,9... | collective-permute-start | bytes 221192 | tf_op jit(solution)/shard_map/ppermute | solution.py:264

commit v7 on v5

--- a/solution.py
+++ b/solution.py
@@ -25,7 +25,7 @@
 
 SMEM = pl.BlockSpec(memory_space=pltpu.SMEM)
 VMEM = pl.BlockSpec(memory_space=pltpu.VMEM)
-CHUNKS = ((0, 1, 2), (3,))
+CHUNKS = ((0, 1), (2, 3))
 KEYS = 5 * TILE + 16
 PIECES = 4
 BF16 = jnp.bfloat16
@@ -61,16 +61,10 @@
     out_ref[...] = jnp.broadcast_to(jnp.sum(found, axis=1, keepdims=True), (PEERS, TILE))
 
 
-def gather_send_kernel(want_ref, feat_ref, state_ref, out_ref, row_ref, want_smem, sem):
-    lane = lax.broadcasted_iota(jnp.int32, (PEERS, TILE), 1)
-    peer = lax.broadcasted_iota(jnp.int32, (PEERS, TILE), 0)
-    row_ref[...] = jnp.sum(jnp.where(lane == peer, want_ref[...], 0), axis=0, keepdims=True)
-    copy = pltpu.make_async_copy(row_ref, want_smem, sem)
-    copy.start()
-    copy.wait()
+def gather_send_kernel(want_ref, feat_ref, state_ref, out_ref):
     state = state_ref[...]
     for e in range(PEERS):
-        rows = feat_ref[want_smem[0, e] * REP + lax.axis_index("rep")]
+        rows = feat_ref[want_ref[e : e + 1, :][0, 0] * REP + lax.axis_index("rep")]
         for t in range(8):
             out_ref[e, :, t * TILE : (t + 1) * TILE] = rows[t // 2 * 8 : t // 2 * 8 + 8, t % 2 * TILE : (t % 2 + 1) * TILE]
         out_ref[e, :, 8 * TILE :] = state
@@ -152,7 +146,10 @@
     state_ref[...] = state.astype(BF16)
 
 
-def masks_kernel(links_ref, bias_ref):
+def masks_kernel(links_ref, *refs):
+    packs, (bias_ref, w_out_ref) = refs[:REP], refs[REP:]
+    w_out = jnp.concatenate([p[2 * WIDTH : 3 * WIDTH, :] for p in packs], axis=0)
+    w_out_ref[...] = w_out.astype(jnp.float32).T.astype(BF16)
     position = lax.broadcasted_iota(jnp.int32, (TILE, TILE), 0)
     for c in range(4):
         first = pl.multiple_of(lax.axis_index("rep") * 512 + c * TILE, TILE)
@@ -163,7 +160,7 @@
         bias_ref[:, c * TILE : (c + 1) * TILE] = jnp.where(linked, 0.0, NEG)
 
 
-def attention(blocks, feat_ref, ns, bias_ref, packs, vs_ref, key_ref, value_ref, score_ref, weight_ref, query_ref):
+def attention(blocks, feat_ref, ns, bias_ref, packs, vs_ref, w_out_ref, key_ref, value_ref, score_ref, weight_ref, query_ref):
     lane = lax.broadcasted_iota(jnp.int32, (TILE, TILE), 1)
     row = lax.broadcasted_iota(jnp.int32, (16, 2 * TILE), 0)
     w_value = jnp.concatenate([p[:WIDTH, :] for p in packs], axis=0)
@@ -218,17 +215,16 @@
         scale = weigh(n)
     parts.append(blend(4 * len(blocks) - 1, scale))
     heads = [jnp.concatenate(parts[4 * i : 4 * i + 4], axis=0) for i in range(len(blocks))]
-    w_out = jnp.concatenate([p[2 * WIDTH : 3 * WIDTH, :] for p in packs], axis=0)
-    return dot(w_out, jnp.concatenate(heads, axis=1).astype(BF16), (((0,), (0,)), ((), ()))).astype(BF16)
+    return dot(w_out_ref[...], jnp.concatenate(heads, axis=1).astype(BF16)).astype(BF16)
 
 
 def attention_kernel(chunk, feat_ref, *refs):
     ns, refs = refs[:REP], refs[REP:]
     bias_ref, refs = refs[0], refs[1:]
     packs, refs = refs[:REP], refs[REP:]
-    vs_ref, refs = refs[0], refs[1:]
+    (vs_ref, w_out_ref), refs = refs[:2], refs[2:]
     refs, scratch = refs[:-5], refs[-5:]
-    out = attention(CHUNKS[chunk], feat_ref, ns, bias_ref, packs, vs_ref, *scratch)
+    out = attention(CHUNKS[chunk], feat_ref, ns, bias_ref, packs, vs_ref, w_out_ref, *scratch)
     if chunk == 0:
         refs[0][...] = out
         return
@@ -256,9 +252,10 @@
 
 
 def send_rep(values):
-    return [values[0]] + [
-        lax.ppermute(values[d], "rep", [(i, (i + d) % REP) for i in range(REP)]) for d in range(1, REP)
-    ]
+    received = list(values)
+    for d in (1, 3, 2):
+        received[d] = lax.ppermute(values[d], "rep", [(i, (i + d) % REP) for i in range(REP)])
+    return received
 
 
 def shards(features, virtual_state, w_query, w_key, w_value, w_out, tile_map, local_nbr):
@@ -288,26 +285,22 @@
         compiler_params=params(16),
         name="prepare",
     )(*map(in_hbm, (features, w_value.T, w_key.T, w_out, w_query.T)), virtual_state)
-    bias = pl.pallas_call(
+    packs = [in_vmem(p) for p in send_rep([pack] * REP)]
+
+    bias, w_out_t = pl.pallas_call(
         masks_kernel,
-        out_shape=vmem_out((TILE, 512), jnp.float32),
-        in_specs=[VMEM],
-        out_specs=VMEM,
+        out_shape=[vmem_out((TILE, 512), jnp.float32), vmem_out((D, D), BF16)],
+        in_specs=[VMEM] * (1 + REP),
+        out_specs=[VMEM] * 2,
         compiler_params=params(2),
         name="masks",
-    )(local_nbr.T)
-    packs = [in_vmem(p) for p in send_rep([pack] * REP)]
+    )(local_nbr.T, *packs)
 
     outgoing = pl.pallas_call(
         gather_send_kernel,
         out_shape=vmem_out((PEERS, 8, 9 * TILE), BF16),
         in_specs=[VMEM] * 3,
         out_specs=VMEM,
-        scratch_shapes=[
-            pltpu.VMEM((1, TILE), jnp.int32),
-            pltpu.SMEM((1, TILE), jnp.int32),
-            pltpu.SemaphoreType.DMA,
-        ],
         compiler_params=params(2),
         name="gather_send",
     )(in_vmem(wanted.reshape(PEERS, TILE)), in_vmem(rows_in_vmem.reshape(PEERS, QUARTER, D)), in_vmem(state))
@@ -334,7 +327,7 @@
     rows = None
     for k, blocks in enumerate(CHUNKS):
         last = k == len(CHUNKS) - 1
-        args = [in_vmem(rows_in_vmem), *map(in_vmem, pieces[k]), in_vmem(bias), *packs, in_vmem(virtual_rows)]
+        args = [in_vmem(rows_in_vmem), *map(in_vmem, pieces[k]), in_vmem(bias), *packs, in_vmem(virtual_rows), in_vmem(w_out_t)]
         args += [in_vmem(heads), in_vmem(rows)] if last else []
         count = len(blocks)
         rows = pl.pallas_call(
@@ -342,7 +335,7 @@
             out_shape=[vmem_out((WIDTH + 2 * G, 512), BF16)] * REP if last else vmem_out((D, count * TILE), BF16),
             in_specs=[VMEM] * len(args),
             out_specs=[VMEM] * REP if last else VMEM,
-            scratch_shapes=[pltpu.VMEM((D, TILE), BF16)] * last
+            scratch_shapes=[pltpu.VMEM((D, count * TILE), BF16)] * last
             + [
                 pltpu.VMEM((count, KEYS, D), BF16),
                 pltpu.VMEM((count, D, 6 * TILE), BF16),

time: 91.8 us -> 90.4 us (0.985)
  transfers between devices with their start and end apart: 14 -> 14, of which waited for: 9 -> 10; matrix products, arithmetic and copies ran while one was open for 0% -> 0% of each run, Pallas kernels for 9% -> 8%
where the time goes in v7:
time: 90.4 us; the launch traced here: 89.4 us
  starting transfers between devices  37.8 us (42%)
  waiting for transfers between devices  35.9 us (40%)
  Pallas kernels  13.7 us (15%)
  local copies, waits for them, and re-layouts  1.36 us (2%)
    ppermute x12, starting transfers between devices, send_rep(): lax.ppermute(values[d], 'rep', [(i, (i + d) % REP) for i in range(REP)])  20.3 us
    all_to_all x1, waiting for transfers between devices, shards(): arrived = lax.all_to_all(outgoing, 'nodes', 0, 0, tiled=True)  20.2 us
    all_to_all x1, starting transfers between devices, shards(): lax.all_to_all(wanted_from.reshape(PEERS, 1, TILE), 'nodes', 0, 0, tiled=...  11.8 us
    ppermute x12, waiting for transfers between devices, send_rep(): lax.ppermute(values[d], 'rep', [(i, (i + d) % REP) for i in range(REP)])  11 us
    all_to_all x1, starting transfers between devices, shards(): arrived = lax.all_to_all(outgoing, 'nodes', 0, 0, tiled=True)  5.72 us
    pallas_call x2, Pallas kernels, shards(): pl.pallas_call(lambda *refs, k=k: attention_kernel(k, *refs), out_shape=[...  5.56 us
    all_to_all x1, waiting for transfers between devices, shards(): lax.all_to_all(wanted_from.reshape(PEERS, 1, TILE), 'nodes', 0, 0, tiled=...  4.72 us
    pallas_call x1, Pallas kernels, shards(): pl.pallas_call(prepare_kernel, out_shape=[vmem_out((2048, D), BF16), vmem...  3.16 us
  transfers between devices with their start and end apart: 14, of which 10 were waited for; matrix products, arithmetic and copies ran while one was open for 0% of the time, Pallas kernels for 8%

profile of v7, /device:TPU:32, one launch (start us, length us, event | category | flops | bytes accessed | tf_op | source)
XLA Modules:
  0.0 89.4 jit_solution(1483891119656589155)
XLA Ops:
  0.6 0.0 copy-start.1
  0.6 0.7 copy-done.1
  1.3 0.7 wanted_rows.1
  2.0 11.8 %all-to-all-start = ((s32[64,1,128]{2,1,0:T(1,128)}), s32[64,1,128]{2,1,0:T(1,128)S(1)}, u32[]{:S(2)}, u32[]{:S(2)}) async-start(s32[64,1,128]{2,1,0:T(1,128)} %bitcast.5), calls=%async_computation | async-start | bytes 65536 | tf_op jit(solution)/shard_map/all_to_all | solution.py:272
  13.8 0.0 copy-start.3
  13.8 0.7 copy-done.3
  14.5 3.2 %prepare.1 = (bf16[2048,256]{1,0:T(8,128)(2,1)S(1)}, bf16[256,256]{1,0:T(8,128)(2,1)S(1)}, bf16[128,256]{1,0:T(8,128)(2,1)S(1)}, bf16[8,128]{1,0:T(8,128)(2,1)S(1)}) custom-call(bf16[2048,256]{1,0:T(8,128)(2,1)} %feat_in.1, bf16[64,256]{1,0:T(8,128)(2,1)} %bitcast.16, bf16[64,256]{1,0:T(8,128)(2,1)} %bitcast.17, bf16[64,256]{1,0:T(8,128)(2,1)} %out_in.1, ...), custom_call_target="tpu_custom_call" | custom-call | tf_op jit(solution)/shard_map/prepare/pallas_call | solution.py:274
  17.7 4.7 %all-to-all-done = s32[64,1,128]{2,1,0:T(1,128)S(1)} async-done(((s32[64,1,128]{2,1,0:T(1,128)}), s32[64,1,128]{2,1,0:T(1,128)S(1)}, u32[]{:S(2)}, u32[]{:S(2)}) %all-to-all-start) | async-done | bytes 32800 | tf_op jit(solution)/shard_map/all_to_all | solution.py:272
  22.4 1.2 %gather_send.1 = bf16[64,8,1152]{2,1,0:T(8,128)(2,1)} custom-call(s32[64,128]{1,0:T(8,128)S(1)} %bitcast.12, bf16[64,32,256]{2,1,0:T(8,128)(2,1)S(1)} %bitcast.11, bf16[8,128]{1,0:T(8,128)(2,1)S(1)} %get-tuple-element.23.state_ref), custom_call_target="tpu_custom_call" | custom-call | tf_op jit(solution)/shard_map/gather_send/pallas_call | solution.py:299
  23.6 0.0 copy-start.2
  23.6 5.7 %all-to-all-start.1 = ((bf16[64,8,1152]{2,1,0:T(8,128)(2,1)}), bf16[64,8,1152]{2,1,0:T(8,128)(2,1)S(1)}, u32[]{:S(2)}, u32[]{:S(2)}) async-start(bf16[64,8,1152]{2,1,0:T(8,128)(2,1)} %gather_send.1), calls=%async_computation.1 | async-start | bytes 2359296 | tf_op jit(solution)/shard_map/all_to_all | solution.py:307
  29.3 0.0 copy-start
  29.3 1.6 %collective-permute-start = (bf16[256,256]{1,0:T(8,128)(2,1)S(1)}, bf16[256,256]{1,0:T(8,128)(2,1)S(1)}, u32[]{:S(2)}, u32[]{:S(2)}) collective-permute-start(bf16[256,256]{1,0:T(8,128)(2,1)S(1)} %get-tuple-element.24.refs_0_.refs_6_.refs_4_), channel_id=1, source_target_pairs={{0,1},{1,2},{2,3},{3,0},{4,5},{5,6},{6,7},{7,4},{8,9},{9,10},{10,1... | collective-permute-start | bytes 393224 | tf_op jit(solution)/shard_map/ppermute | solution.py:257
  30.9 2.7 %collective-permute-start.1 = (bf16[256,256]{1,0:T(8,128)(2,1)S(1)}, bf16[256,256]{1,0:T(8,128)(2,1)S(1)}, u32[]{:S(2)}, u32[]{:S(2)}) collective-permute-start(bf16[256,256]{1,0:T(8,128)(2,1)S(1)} %get-tuple-element.24.refs_0_.refs_6_.refs_4_), channel_id=1, source_target_pairs={{0,2},{1,3},{2,0},{3,1},{4,6},{5,7},{6,4},{7,5},{8,10},{9,11},{10,... | collective-permute-start | bytes 393224 | tf_op jit(solution)/shard_map/ppermute | solution.py:257
  33.6 1.4 %collective-permute-start.2 = (bf16[256,256]{1,0:T(8,128)(2,1)S(1)}, bf16[256,256]{1,0:T(8,128)(2,1)S(1)}, u32[]{:S(2)}, u32[]{:S(2)}) collective-permute-start(bf16[256,256]{1,0:T(8,128)(2,1)S(1)} %get-tuple-element.24.refs_0_.refs_6_.refs_4_), channel_id=1, source_target_pairs={{0,3},{1,0},{2,1},{3,2},{4,7},{5,4},{6,5},{7,6},{8,11},{9,8},{10,9... | collective-permute-start | bytes 393224 | tf_op jit(solution)/shard_map/ppermute | solution.py:257
  35.1 1.1 %collective-permute-done.refs_0_.refs_1_.refs_7_.refs_5_ = bf16[256,256]{1,0:T(8,128)(2,1)S(1)} collective-permute-done((bf16[256,256]{1,0:T(8,128)(2,1)S(1)}, bf16[256,256]{1,0:T(8,128)(2,1)S(1)}, u32[]{:S(2)}, u32[]{:S(2)}) %collective-permute-start) | collective-permute-done | bytes 131104 | tf_op jit(solution)/shard_map/ppermute | solution.py:257
  36.2 3.8 %collective-permute-done.1.refs_1_.refs_2_.refs_8_.refs_6_ = bf16[256,256]{1,0:T(8,128)(2,1)S(1)} collective-permute-done((bf16[256,256]{1,0:T(8,128)(2,1)S(1)}, bf16[256,256]{1,0:T(8,128)(2,1)S(1)}, u32[]{:S(2)}, u32[]{:S(2)}) %collective-permute-start.1) | collective-permute-done | bytes 131104 | tf_op jit(solution)/shard_map/ppermute | solution.py:257
  39.9 0.0 collective-permute-done.2.refs_2_.refs_3_.refs_9_.refs_7_
  40.0 20.2 %all-to-all-done.1.arrived_ref = bf16[64,8,1152]{2,1,0:T(8,128)(2,1)S(1)} async-done(((bf16[64,8,1152]{2,1,0:T(8,128)(2,1)}), bf16[64,8,1152]{2,1,0:T(8,128)(2,1)S(1)}, u32[]{:S(2)}, u32[]{:S(2)}) %all-to-all-start.1) | async-done | bytes 1179680 | tf_op jit(solution)/shard_map/all_to_all | solution.py:307
  60.1 0.0 copy-done.2
  60.1 1.0 %gather_rep.1 = (bf16[8,32,256]{2,1,0:T(8,128)(2,1)S(1)}, bf16[8,32,256]{2,1,0:T(8,128)(2,1)S(1)}, bf16[8,32,256]{2,1,0:T(8,128)(2,1)S(1)}, bf16[8,32,256]{2,1,0...) custom-call(s32[4,16]{1,0:T(4,128)S(1)} %bitcast.15, ...), custom_call_target="tpu_custom_call" | custom-call | tf_op jit(solution)/shard_map/gather_rep/pallas_call | solution.py:309
  61.1 1.6 %collective-permute-start.6 = (bf16[8,32,256]{2,1,0:T(8,128)(2,1)S(1)}, bf16[8,32,256]{2,1,0:T(8,128)(2,1)S(1)}, u32[]{:S(2)}, u32[]{:S(2)}) collective-permute-start(bf16[8,32,256]{2,1,0:T(8,128)(2,1)S(1)} %get-tuple-element.33), channel_id=1, source_target_pairs={{0,1},{1,2},{2,3},{3,0},{4,5},{5,6},{6,7},{7,4},{8,9},{9,10},{10,1... | collective-permute-start | bytes 393224 | tf_op jit(solution)/shard_map/ppermute | solution.py:257
  62.6 2.7 %collective-permute-start.7 = (bf16[8,32,256]{2,1,0:T(8,128)(2,1)S(1)}, bf16[8,32,256]{2,1,0:T(8,128)(2,1)S(1)}, u32[]{:S(2)}, u32[]{:S(2)}) collective-permute-start(bf16[8,32,256]{2,1,0:T(8,128)(2,1)S(1)} %get-tuple-element.34), channel_id=1, source_target_pairs={{0,2},{1,3},{2,0},{3,1},{4,6},{5,7},{6,4},{7,5},{8,10},{9,11},{10,... | collective-permute-start | bytes 393224 | tf_op jit(solution)/shard_map/ppermute | solution.py:257
  65.4 1.4 %collective-permute-start.8 = (bf16[8,32,256]{2,1,0:T(8,128)(2,1)S(1)}, bf16[8,32,256]{2,1,0:T(8,128)(2,1)S(1)}, u32[]{:S(2)}, u32[]{:S(2)}) collective-permute-start(bf16[8,32,256]{2,1,0:T(8,128)(2,1)S(1)} %get-tuple-element.35), channel_id=1, source_target_pairs={{0,3},{1,0},{2,1},{3,2},{4,7},{5,4},{6,5},{7,6},{8,11},{9,8},{10,9... | collective-permute-start | bytes 393224 | tf_op jit(solution)/shard_map/ppermute | solution.py:257
  66.8 0.6 collective-permute-start.3
  67.4 0.9 collective-permute-start.4
  68.3 0.0 collective-permute-done.6.refs_2_
  68.3 2.0 %collective-permute-start.5 = (bf16[8,32,256]{2,1,0:T(8,128)(2,1)S(1)}, bf16[8,32,256]{2,1,0:T(8,128)(2,1)S(1)}, u32[]{:S(2)}, u32[]{:S(2)}) collective-permute-start(bf16[8,32,256]{2,1,0:T(8,128)(2,1)S(1)} %get-tuple-element.28), channel_id=1, source_target_pairs={{0,3},{1,0},{2,1},{3,2},{4,7},{5,4},{6,5},{7,6},{8,11},{9,8},{10,9... | collective-permute-start | bytes 393224 | tf_op jit(solution)/shard_map/ppermute | solution.py:257
  70.3 0.0 copy-done
  70.3 0.6 masks.1
  70.9 0.5 join_virtual.1.refs_12_
  71.4 1.1 %collective-permute-done.7.refs_3_ = bf16[8,32,256]{2,1,0:T(8,128)(2,1)S(1)} collective-permute-done((bf16[8,32,256]{2,1,0:T(8,128)(2,1)S(1)}, bf16[8,32,256]{2,1,0:T(8,128)(2,1)S(1)}, u32[]{:S(2)}, u32[]{:S(2)}) %collective-permute-start.7) | collective-permute-done | bytes 131104 | tf_op jit(solution)/shard_map/ppermute | solution.py:257
  72.5 0.3 collective-permute-done.8.refs_4_
  72.8 2.8 %shard_map.95.refs_13_ = bf16[256,256]{1,0:T(8,128)(2,1)S(1)} custom-call(bf16[2048,256]{1,0:T(8,128)(2,1)S(1)} %get-tuple-element.22.refs_0_, bf16[8,32,256]{2,1,0:T(8,128)(2,1)S(1)} %get-tuple-element.32.refs_1_, bf16[8,32,256]{2,1,0:T(8,128)(2,1)S(1)} %collective-permute-done.6.refs_2_, bf16[8,32,256]{2,1,0:T(8,128)(2,1)S(1)} %collective-permute-done.7.refs_3_, ...), custom_call_target="tpu_custom_call" | custom-call | tf_op jit(solution)/shard_map/pallas_call | solution.py:333
  75.6 0.0 collective-permute-done.3.refs_2_
  75.6 1.7 %collective-permute-done.4.refs_3_ = bf16[8,32,256]{2,1,0:T(8,128)(2,1)S(1)} collective-permute-done((bf16[8,32,256]{2,1,0:T(8,128)(2,1)S(1)}, bf16[8,32,256]{2,1,0:T(8,128)(2,1)S(1)}, u32[]{:S(2)}, u32[]{:S(2)}) %collective-permute-start.4) | collective-permute-done | bytes 131104 | tf_op jit(solution)/shard_map/ppermute | solution.py:257
  77.4 0.0 collective-permute-done.5.refs_4_
  77.4 2.8 %shard_map.96 = (bf16[72,512]{1,0:T(8,128)(2,1)S(1)}, bf16[72,512]{1,0:T(8,128)(2,1)S(1)}, bf16[72,512]{1,0:T(8,128)(2,1)S(1)}, bf16[72,512]{1,0:T(8,128)(2,1)S(1)}) custom-call(bf16[2048,256]{1,0:T(8,128)(2,1)S(1)} %get-tuple-element.22.refs_0_, bf16[8,32,256]{2,1,0:T(8,128)(2,1)S(1)} %get-tuple-element.25.refs_1_, ...), custom_call_target="tpu_custom_call" | custom-call | tf_op jit(solution)/shard_map/pallas_call | solution.py:333
  80.2 1.4 %collective-permute-start.9 = (bf16[72,512]{1,0:T(8,128)(2,1)S(1)}, bf16[72,512]{1,0:T(8,128)(2,1)S(1)}, u32[]{:S(2)}, u32[]{:S(2)}) collective-permute-start(bf16[72,512]{1,0:T(8,128)(2,1)S(1)} %get-tuple-element.37), channel_id=1, source_target_pairs={{0,1},{1,2},{2,3},{3,0},{4,5},{5,6},{6,7},{7,4},{8,9},{9,10},{10,1... | collective-permute-start | bytes 221192 | tf_op jit(solution)/shard_map/ppermute | solution.py:257
  81.6 2.6 %collective-permute-start.10 = (bf16[72,512]{1,0:T(8,128)(2,1)S(1)}, bf16[72,512]{1,0:T(8,128)(2,1)S(1)}, u32[]{:S(2)}, u32[]{:S(2)}) collective-permute-start(bf16[72,512]{1,0:T(8,128)(2,1)S(1)} %get-tuple-element.38), channel_id=1, source_target_pairs={{0,2},{1,3},{2,0},{3,1},{4,6},{5,7},{6,4},{7,5},{8,10},{9,11},{10,... | collective-permute-start | bytes 221192 | tf_op jit(solution)/shard_map/ppermute | solution.py:257
  84.2 1.4 %collective-permute-start.11 = (bf16[72,512]{1,0:T(8,128)(2,1)S(1)}, bf16[72,512]{1,0:T(8,128)(2,1)S(1)}, u32[]{:S(2)}, u32[]{:S(2)}) collective-permute-start(bf16[72,512]{1,0:T(8,128)(2,1)S(1)} %get-tuple-element.39), channel_id=1, source_target_pairs={{0,3},{1,0},{2,1},{3,2},{4,7},{5,4},{6,5},{7,6},{8,11},{9,8},{10,9... | collective-permute-start | bytes 221192 | tf_op jit(solution)/shard_map/ppermute | solution.py:257
  85.5 0.8 collective-permute-done.9.refs_1_
  86.4 1.1 %collective-permute-done.10.refs_2_ = bf16[72,512]{1,0:T(8,128)(2,1)S(1)} collective-permute-done((bf16[72,512]{1,0:T(8,128)(2,1)S(1)}, bf16[72,512]{1,0:T(8,128)(2,1)S(1)}, u32[]{:S(2)}, u32[]{:S(2)}) %collective-permute-start.10) | collective-permute-done | bytes 73760 | tf_op jit(solution)/shard_map/ppermute | solution.py:257
  87.5 1.1 %collective-permute-done.11.refs_3_ = bf16[72,512]{1,0:T(8,128)(2,1)S(1)} collective-permute-done((bf16[72,512]{1,0:T(8,128)(2,1)S(1)}, bf16[72,512]{1,0:T(8,128)(2,1)S(1)}, u32[]{:S(2)}, u32[]{:S(2)}) %collective-permute-start.11) | collective-permute-done | bytes 73760 | tf_op jit(solution)/shard_map/ppermute | solution.py:257
  88.5 0.9 %assemble.1 = (bf16[64,2048]{1,0:T(8,128)(2,1)}, bf16[4,64]{1,0:T(4,128)(2,1)}) custom-call(bf16[72,512]{1,0:T(8,128)(2,1)S(1)} %get-tuple-element.36.refs_0_, bf16[72,512]{1,0:T(8,128)(2,1)S(1)} %collective-permute-done.9.refs_1_, bf16[72,512]{1,0:T(8,128)(2,1)S(1)} %collective-permute-done.10.refs_2_, bf16[72,512]{1,0:T(8,128)(2,1)S(1)} %collective-permute-done.11.refs_3_, ...), custom_call_target="tpu_custom_call" | custom-call | tf_op jit(solution)/shard_map/assemble/pallas_call | solution.py:350
Async XLA Ops:
  0.6 0.7 copy-start.1
  2.0 20.3 %all-to-all-start = ((s32[64,1,128]{2,1,0:T(1,128)}), s32[64,1,128]{2,1,0:T(1,128)S(1)}, u32[]{:S(2)}, u32[]{:S(2)}) async-start(s32[64,1,128]{2,1,0:T(1,128)} %bitcast.5), calls=%async_computation | async-start | bytes 65536 | tf_op jit(solution)/shard_map/all_to_all | solution.py:272
  13.8 0.7 copy-start.3
  23.6 36.5 %copy-start.2 = (s32[16,4]{0,1:T(4,128)S(1)}, s32[16,4]{0,1:T(4,128)}, u32[]{:S(2)}) copy-start(s32[16,4]{0,1:T(4,128)} %param.14) | copy-start | bytes 772
  23.6 36.5 %all-to-all-start.1 = ((bf16[64,8,1152]{2,1,0:T(8,128)(2,1)}), bf16[64,8,1152]{2,1,0:T(8,128)(2,1)S(1)}, u32[]{:S(2)}, u32[]{:S(2)}) async-start(bf16[64,8,1152]{2,1,0:T(8,128)(2,1)} %gather_send.1), calls=%async_computation.1 | async-start | bytes 2359296 | tf_op jit(solution)/shard_map/all_to_all | solution.py:307
  29.3 40.9 %copy-start = (s32[2048,16]{0,1:T(8,128)S(1)}, s32[2048,16]{0,1:T(8,128)}, u32[]{:S(2)}) copy-start(s32[2048,16]{0,1:T(8,128)} %param.15) | copy-start | bytes 393220
  29.3 6.8 %collective-permute-start = (bf16[256,256]{1,0:T(8,128)(2,1)S(1)}, bf16[256,256]{1,0:T(8,128)(2,1)S(1)}, u32[]{:S(2)}, u32[]{:S(2)}) collective-permute-start(bf16[256,256]{1,0:T(8,128)(2,1)S(1)} %get-tuple-element.24.refs_0_.refs_6_.refs_4_), channel_id=1, source_target_pairs={{0,1},{1,2},{2,3},{3,0},{4,5},{5,6},{6,7},{7,4},{8,9},{9,10},{10,1... | collective-permute-start | bytes 393224 | tf_op jit(solution)/shard_map/ppermute | solution.py:257
  30.9 9.0 %collective-permute-start.1 = (bf16[256,256]{1,0:T(8,128)(2,1)S(1)}, bf16[256,256]{1,0:T(8,128)(2,1)S(1)}, u32[]{:S(2)}, u32[]{:S(2)}) collective-permute-start(bf16[256,256]{1,0:T(8,128)(2,1)S(1)} %get-tuple-element.24.refs_0_.refs_6_.refs_4_), channel_id=1, source_target_pairs={{0,2},{1,3},{2,0},{3,1},{4,6},{5,7},{6,4},{7,5},{8,10},{9,11},{10,... | collective-permute-start | bytes 393224 | tf_op jit(solution)/shard_map/ppermute | solution.py:257
  33.6 6.3 %collective-permute-start.2 = (bf16[256,256]{1,0:T(8,128)(2,1)S(1)}, bf16[256,256]{1,0:T(8,128)(2,1)S(1)}, u32[]{:S(2)}, u32[]{:S(2)}) collective-permute-start(bf16[256,256]{1,0:T(8,128)(2,1)S(1)} %get-tuple-element.24.refs_0_.refs_6_.refs_4_), channel_id=1, source_target_pairs={{0,3},{1,0},{2,1},{3,2},{4,7},{5,4},{6,5},{7,6},{8,11},{9,8},{10,9... | collective-permute-start | bytes 393224 | tf_op jit(solution)/shard_map/ppermute | solution.py:257
  61.1 7.2 %collective-permute-start.6 = (bf16[8,32,256]{2,1,0:T(8,128)(2,1)S(1)}, bf16[8,32,256]{2,1,0:T(8,128)(2,1)S(1)}, u32[]{:S(2)}, u32[]{:S(2)}) collective-permute-start(bf16[8,32,256]{2,1,0:T(8,128)(2,1)S(1)} %get-tuple-element.33), channel_id=1, source_target_pairs={{0,1},{1,2},{2,3},{3,0},{4,5},{5,6},{6,7},{7,4},{8,9},{9,10},{10,1... | collective-permute-start | bytes 393224 | tf_op jit(solution)/shard_map/ppermute | solution.py:257
  62.6 9.9 %collective-permute-start.7 = (bf16[8,32,256]{2,1,0:T(8,128)(2,1)S(1)}, bf16[8,32,256]{2,1,0:T(8,128)(2,1)S(1)}, u32[]{:S(2)}, u32[]{:S(2)}) collective-permute-start(bf16[8,32,256]{2,1,0:T(8,128)(2,1)S(1)} %get-tuple-element.34), channel_id=1, source_target_pairs={{0,2},{1,3},{2,0},{3,1},{4,6},{5,7},{6,4},{7,5},{8,10},{9,11},{10,... | collective-permute-start | bytes 393224 | tf_op jit(solution)/shard_map/ppermute | solution.py:257
  65.4 7.5 %collective-permute-start.8 = (bf16[8,32,256]{2,1,0:T(8,128)(2,1)S(1)}, bf16[8,32,256]{2,1,0:T(8,128)(2,1)S(1)}, u32[]{:S(2)}, u32[]{:S(2)}) collective-permute-start(bf16[8,32,256]{2,1,0:T(8,128)(2,1)S(1)} %get-tuple-element.35), channel_id=1, source_target_pairs={{0,3},{1,0},{2,1},{3,2},{4,7},{5,4},{6,5},{7,6},{8,11},{9,8},{10,9... | collective-permute-start | bytes 393224 | tf_op jit(solution)/shard_map/ppermute | solution.py:257
  66.8 8.8 %collective-permute-start.3 = (bf16[8,32,256]{2,1,0:T(8,128)(2,1)S(1)}, bf16[8,32,256]{2,1,0:T(8,128)(2,1)S(1)}, u32[]{:S(2)}, u32[]{:S(2)}) collective-permute-start(bf16[8,32,256]{2,1,0:T(8,128)(2,1)S(1)} %get-tuple-element.26), channel_id=1, source_target_pairs={{0,1},{1,2},{2,3},{3,0},{4,5},{5,6},{6,7},{7,4},{8,9},{9,10},{10,1... | collective-permute-start | bytes 393224 | tf_op jit(solution)/shard_map/ppermute | solution.py:257
  67.4 10.0 %collective-permute-start.4 = (bf16[8,32,256]{2,1,0:T(8,128)(2,1)S(1)}, bf16[8,32,256]{2,1,0:T(8,128)(2,1)S(1)}, u32[]{:S(2)}, u32[]{:S(2)}) collective-permute-start(bf16[8,32,256]{2,1,0:T(8,128)(2,1)S(1)} %get-tuple-element.27), channel_id=1, source_target_pairs={{0,2},{1,3},{2,0},{3,1},{4,6},{5,7},{6,4},{7,5},{8,10},{9,11},{10,... | collective-permute-start | bytes 393224 | tf_op jit(solution)/shard_map/ppermute | solution.py:257
  68.3 9.1 %collective-permute-start.5 = (bf16[8,32,256]{2,1,0:T(8,128)(2,1)S(1)}, bf16[8,32,256]{2,1,0:T(8,128)(2,1)S(1)}, u32[]{:S(2)}, u32[]{:S(2)}) collective-permute-start(bf16[8,32,256]{2,1,0:T(8,128)(2,1)S(1)} %get-tuple-element.28), channel_id=1, source_target_pairs={{0,3},{1,0},{2,1},{3,2},{4,7},{5,4},{6,5},{7,6},{8,11},{9,8},{10,9... | collective-permute-start | bytes 393224 | tf_op jit(solution)/shard_map/ppermute | solution.py:257
  80.2 6.2 %collective-permute-start.9 = (bf16[72,512]{1,0:T(8,128)(2,1)S(1)}, bf16[72,512]{1,0:T(8,128)(2,1)S(1)}, u32[]{:S(2)}, u32[]{:S(2)}) collective-permute-start(bf16[72,512]{1,0:T(8,128)(2,1)S(1)} %get-tuple-element.37), channel_id=1, source_target_pairs={{0,1},{1,2},{2,3},{3,0},{4,5},{5,6},{6,7},{7,4},{8,9},{9,10},{10,1... | collective-permute-start | bytes 221192 | tf_op jit(solution)/shard_map/ppermute | solution.py:257
  81.6 5.9 %collective-permute-start.10 = (bf16[72,512]{1,0:T(8,128)(2,1)S(1)}, bf16[72,512]{1,0:T(8,128)(2,1)S(1)}, u32[]{:S(2)}, u32[]{:S(2)}) collective-permute-start(bf16[72,512]{1,0:T(8,128)(2,1)S(1)} %get-tuple-element.38), channel_id=1, source_target_pairs={{0,2},{1,3},{2,0},{3,1},{4,6},{5,7},{6,4},{7,5},{8,10},{9,11},{10,... | collective-permute-start | bytes 221192 | tf_op jit(solution)/shard_map/ppermute | solution.py:257
  84.2 4.4 %collective-permute-start.11 = (bf16[72,512]{1,0:T(8,128)(2,1)S(1)}, bf16[72,512]{1,0:T(8,128)(2,1)S(1)}, u32[]{:S(2)}, u32[]{:S(2)}) collective-permute-start(bf16[72,512]{1,0:T(8,128)(2,1)S(1)} %get-tuple-element.39), channel_id=1, source_target_pairs={{0,3},{1,0},{2,1},{3,2},{4,7},{5,4},{6,5},{7,6},{8,11},{9,8},{10,9... | collective-permute-start | bytes 221192 | tf_op jit(solution)/shard_map/ppermute | solution.py:257

commit v8 on v7

--- a/solution.py
+++ b/solution.py
@@ -61,25 +61,31 @@
     out_ref[...] = jnp.broadcast_to(jnp.sum(found, axis=1, keepdims=True), (PEERS, TILE))
 
 
-def gather_send_kernel(want_ref, feat_ref, state_ref, out_ref):
+def gather_send_kernel(want_ref, feat_ref, state_ref, out_ref, slots_ref, sems):
     state = state_ref[...]
-    for e in range(PEERS):
-        rows = feat_ref[want_ref[e : e + 1, :][0, 0] * REP + lax.axis_index("rep")]
-        for t in range(8):
-            out_ref[e, :, t * TILE : (t + 1) * TILE] = rows[t // 2 * 8 : t // 2 * 8 + 8, t % 2 * TILE : (t % 2 + 1) * TILE]
-        out_ref[e, :, 8 * TILE :] = state
-
-
-def gather_rep_kernel(map_ref, arrived_ref, *refs):
-    outs = refs[REP - 1 :]
-    for k, blocks in enumerate(CHUNKS):
-        for d in range(REP):
-            column = ((lax.axis_index("rep") + d) % REP) * 4 + blocks[0]
-            for j in range(4 * len(blocks)):
-                owner = map_ref[j % 4, column + j // 4] // 16
-                for t in range(8):
-                    piece = arrived_ref[owner, :, t * TILE : (t + 1) * TILE]
-                    outs[k * REP + d][j, t // 2 * 8 : t // 2 * 8 + 8, t % 2 * TILE : (t % 2 + 1) * TILE] = piece
+    size = PEERS // PIECES
+    copies = []
+    for i in range(PIECES):
+        for e in range(i * size, (i + 1) * size):
+            rows = feat_ref[want_ref[e : e + 1, :][0, 0] * REP + lax.axis_index("rep")]
+            for t in range(8):
+                part = rows[t // 2 * 8 : t // 2 * 8 + 8, t % 2 * TILE : (t % 2 + 1) * TILE]
+                slots_ref[e, :, t * TILE : (t + 1) * TILE] = part
+            slots_ref[e, :, 8 * TILE :] = state
+        part = slice(i * size, (i + 1) * size)
+        copies.append(pltpu.make_async_copy(slots_ref.at[part], out_ref.at[part], sems.at[i]))
+        copies[i].start()
+    for copy in copies:
+        copy.wait()
+
+
+def gather_rep_kernel(blocks, owner_ref, arrived_ref, *outs):
+    for d in range(REP):
+        for j in range(4 * len(blocks)):
+            owner = owner_ref[d * 16 + 4 * blocks[0] + j][0, 0]
+            for t in range(8):
+                piece = arrived_ref[owner, :, t * TILE : (t + 1) * TILE]
+                outs[d][j, t // 2 * 8 : t // 2 * 8 + 8, t % 2 * TILE : (t % 2 + 1) * TILE] = piece
 
 
 def thirds(value):
@@ -146,8 +152,15 @@
     state_ref[...] = state.astype(BF16)
 
 
-def masks_kernel(links_ref, *refs):
-    packs, (bias_ref, w_out_ref) = refs[:REP], refs[REP:]
+def masks_kernel(links_ref, map_ref, *refs):
+    packs, (bias_ref, w_out_ref, owner_ref) = refs[:REP], refs[REP:]
+    owners = map_ref[...] // 16
+    for plane in range(REP):
+        first = (plane + REP - lax.axis_index("rep")) % REP * 16
+        for j in range(16):
+            column = 4 * plane + j // 4
+            owner = owners[j % 4 : j % 4 + 1, column : column + 1]
+            owner_ref[first + j] = jnp.broadcast_to(owner, (1, TILE))
     w_out = jnp.concatenate([p[2 * WIDTH : 3 * WIDTH, :] for p in packs], axis=0)
     w_out_ref[...] = w_out.astype(jnp.float32).T.astype(BF16)
     position = lax.broadcasted_iota(jnp.int32, (TILE, TILE), 0)
@@ -240,15 +253,20 @@
 
 
 def assemble_kernel(*refs):
-    pieces, packs, (out_ref, virtual_ref, scratch) = refs[:REP], refs[REP : 2 * REP], refs[2 * REP :]
+    pieces, packs, (out_ref, virtual_ref, scratch, sems) = refs[:REP], refs[REP : 2 * REP], refs[2 * REP :]
+    copies = []
+    for d in range(REP):
+        first = pl.multiple_of(((lax.axis_index("rep") + REP - d) % REP) * 512, 512)
+        copies.append(pltpu.make_async_copy(pieces[d].at[:WIDTH], out_ref.at[:, pl.ds(first, 512)], sems.at[d]))
+        copies[d].start()
     total = jnp.zeros((2 * G, D), jnp.float32)
     for d in range(REP):
-        first = pl.multiple_of(((lax.axis_index("rep") + REP - d) % REP) * 512, 512)
-        out_ref[:, pl.ds(first, 512)] = pieces[d][:WIDTH, :]
         total = total + dot(pieces[d][WIDTH:, :TILE], packs[d][TILE:, :])
     scratch[...] = total.T
     own = scratch[pl.ds(pl.multiple_of(lax.axis_index("rep") * WIDTH, WIDTH), WIDTH), :]
     virtual_ref[...] = own.T[:G, :].astype(BF16)
+    for copy in copies:
+        copy.wait()
 
 
 def send_rep(values):
@@ -287,34 +305,40 @@
     )(*map(in_hbm, (features, w_value.T, w_key.T, w_out, w_query.T)), virtual_state)
     packs = [in_vmem(p) for p in send_rep([pack] * REP)]
 
-    bias, w_out_t = pl.pallas_call(
+    bias, w_out_t, owners = pl.pallas_call(
         masks_kernel,
-        out_shape=[vmem_out((TILE, 512), jnp.float32), vmem_out((D, D), BF16)],
-        in_specs=[VMEM] * (1 + REP),
-        out_specs=[VMEM] * 2,
+        out_shape=[
+            vmem_out((TILE, 512), jnp.float32),
+            vmem_out((D, D), BF16),
+            vmem_out((PEERS, 1, TILE), jnp.int32),
+        ],
+        in_specs=[VMEM] * (2 + REP),
+        out_specs=[VMEM] * 3,
         compiler_params=params(2),
         name="masks",
-    )(local_nbr.T, *packs)
+    )(local_nbr.T, map_t, *packs)
 
     outgoing = pl.pallas_call(
         gather_send_kernel,
-        out_shape=vmem_out((PEERS, 8, 9 * TILE), BF16),
+        out_shape=jax.ShapeDtypeStruct((PEERS, 8, 9 * TILE), BF16),
         in_specs=[VMEM] * 3,
-        out_specs=VMEM,
-        compiler_params=params(2),
+        out_specs=pl.BlockSpec(memory_space=pl.ANY),
+        scratch_shapes=[pltpu.VMEM((PEERS, 8, 9 * TILE), BF16), pltpu.SemaphoreType.DMA((PIECES,))],
+        compiler_params=params(4),
         name="gather_send",
     )(in_vmem(wanted.reshape(PEERS, TILE)), in_vmem(rows_in_vmem.reshape(PEERS, QUARTER, D)), in_vmem(state))
     arrived = lax.all_to_all(outgoing, "nodes", 0, 0, tiled=True)
 
-    sends = pl.pallas_call(
-        gather_rep_kernel,
-        out_shape=[vmem_out((4 * len(blocks), QUARTER, D), BF16) for blocks in CHUNKS for _ in range(REP)],
-        in_specs=[SMEM] + [VMEM] * REP,
-        out_specs=[VMEM] * (len(CHUNKS) * REP),
-        compiler_params=params(2),
-        name="gather_rep",
-    )(map_t, in_vmem(arrived), *packs[1:])
-    pieces = [send_rep(sends[k * REP : k * REP + REP]) for k in range(len(CHUNKS))]
+    pieces = []
+    for blocks in CHUNKS:
+        sends = pl.pallas_call(
+            lambda *refs, blocks=blocks: gather_rep_kernel(blocks, *refs),
+            out_shape=[vmem_out((4 * len(blocks), QUARTER, D), BF16)] * REP,
+            in_specs=[VMEM] * 2,
+            out_specs=[VMEM] * REP,
+            compiler_params=params(2),
+        )(in_vmem(owners), in_vmem(arrived))
+        pieces.append(send_rep(sends))
     heads = pl.pallas_call(
         join_virtual_kernel,
         out_shape=vmem_out((2 * G, TILE), BF16),
@@ -351,8 +375,8 @@
         assemble_kernel,
         out_shape=return_shape,
         in_specs=[VMEM] * (2 * REP),
-        out_specs=[VMEM] * 2,
-        scratch_shapes=[pltpu.VMEM((D, 2 * G), jnp.float32)],
+        out_specs=[pl.BlockSpec(memory_space=pl.ANY), VMEM],
+        scratch_shapes=[pltpu.VMEM((D, 2 * G), jnp.float32), pltpu.SemaphoreType.DMA((REP,))],
         compiler_params=params(4),
         name="assemble",
     )(*map(in_vmem, received), *packs)

time: 90.4 us -> 89.7 us (level)
  starting transfers between devices: 37.8 us -> 36.6 us
  waiting for transfers between devices: 35.9 us -> 36.9 us
    ppermute x12, waiting for transfers between devices: 11 us -> 14.4 us  [send_rep(): lax.ppermute(values[d], 'rep', [(i, (i + d) % REP) for i in range(REP)])]
    all_to_all x1, waiting for transfers between devices: 20.2 us -> 17.7 us  [shards(): arrived = lax.all_to_all(outgoing, 'nodes', 0, 0, tiled=True)]
    ppermute x12, starting transfers between devices: 20.3 us -> 19.1 us  [send_rep(): lax.ppermute(values[d], 'rep', [(i, (i + d) % REP) for i in range(REP)])]
    pallas_call x2 -> x3, Pallas kernels: 2.18 us -> 1.36 us  [the longest x1 1.21 us: shards(): pl.pallas_call(gather_send_kernel, out_shape=jax.ShapeDtypeStruct((PEERS,...]
  transfers between devices with their start and end apart: 14 -> 14, of which waited for: 10 -> 11; matrix products, arithmetic and copies ran while one was open for 0% -> 0% of each run, Pallas kernels for 8% -> 8%
where the time goes in v8:
time: 89.7 us; the launch traced here: 89 us
  waiting for transfers between devices  36.9 us (41%)
  starting transfers between devices  36.6 us (41%)
  Pallas kernels  13.3 us (15%)
  local copies, waits for them, and re-layouts  1.37 us (2%)
  between operations  0.91 us (1%)
    ppermute x12, starting transfers between devices, send_rep(): lax.ppermute(values[d], 'rep', [(i, (i + d) % REP) for i in range(REP)])  19.1 us
    all_to_all x1, waiting for transfers between devices, shards(): arrived = lax.all_to_all(outgoing, 'nodes', 0, 0, tiled=True)  17.7 us
    ppermute x12, waiting for transfers between devices, send_rep(): lax.ppermute(values[d], 'rep', [(i, (i + d) % REP) for i in range(REP)])  14.4 us
    all_to_all x1, starting transfers between devices, shards(): lax.all_to_all(wanted_from.reshape(PEERS, 1, TILE), 'nodes', 0, 0, tiled=...  11.8 us
    all_to_all x1, starting transfers between devices, shards(): arrived = lax.all_to_all(outgoing, 'nodes', 0, 0, tiled=True)  5.73 us
    pallas_call x2, Pallas kernels, shards(): pl.pallas_call(lambda *refs, k=k: attention_kernel(k, *refs), out_shape=[...  5.57 us
    all_to_all x1, waiting for transfers between devices, shards(): lax.all_to_all(wanted_from.reshape(PEERS, 1, TILE), 'nodes', 0, 0, tiled=...  4.72 us
    pallas_call x1, Pallas kernels, shards(): pl.pallas_call(prepare_kernel, out_shape=[vmem_out((2048, D), BF16), vmem...  3.16 us
  transfers between devices with their start and end apart: 14, of which 11 were waited for; matrix products, arithmetic and copies ran while one was open for 0% of the time, Pallas kernels for 8%

profile of v8, /device:TPU:32, one launch (start us, length us, event | category | flops | bytes accessed | tf_op | source)
XLA Modules:
  0.0 89.0 jit_solution(3136711631728212158)
XLA Ops:
  0.6 0.0 copy-start.1
  0.6 0.7 copy-done.1
  1.3 0.7 wanted_rows.1
  2.0 11.8 %all-to-all-start = ((s32[64,1,128]{2,1,0:T(1,128)}), s32[64,1,128]{2,1,0:T(1,128)S(1)}, u32[]{:S(2)}, u32[]{:S(2)}) async-start(s32[64,1,128]{2,1,0:T(1,128)} %bitcast.6), calls=%async_computation | async-start | bytes 65536 | tf_op jit(solution)/shard_map/all_to_all | solution.py:290
  13.8 0.0 copy-start.3
  13.8 0.7 copy-done.3
  14.5 3.2 %prepare.1 = (bf16[2048,256]{1,0:T(8,128)(2,1)S(1)}, bf16[256,256]{1,0:T(8,128)(2,1)S(1)}, bf16[128,256]{1,0:T(8,128)(2,1)S(1)}, bf16[8,128]{1,0:T(8,128)(2,1)S(1)}) custom-call(bf16[2048,256]{1,0:T(8,128)(2,1)} %feat_in.1, bf16[64,256]{1,0:T(8,128)(2,1)} %bitcast.16, bf16[64,256]{1,0:T(8,128)(2,1)} %bitcast.17, bf16[64,256]{1,0:T(8,128)(2,1)} %out_in.1, ...), custom_call_target="tpu_custom_call" | custom-call | tf_op jit(solution)/shard_map/prepare/pallas_call | solution.py:292
  17.7 4.7 %all-to-all-done = s32[64,1,128]{2,1,0:T(1,128)S(1)} async-done(((s32[64,1,128]{2,1,0:T(1,128)}), s32[64,1,128]{2,1,0:T(1,128)S(1)}, u32[]{:S(2)}, u32[]{:S(2)}) %all-to-all-start) | async-done | bytes 32800 | tf_op jit(solution)/shard_map/all_to_all | solution.py:290
  22.4 1.2 %gather_send.1 = bf16[64,8,1152]{2,1,0:T(8,128)(2,1)} custom-call(s32[64,128]{1,0:T(8,128)S(1)} %bitcast.12, bf16[64,32,256]{2,1,0:T(8,128)(2,1)S(1)} %bitcast.11, bf16[8,128]{1,0:T(8,128)(2,1)S(1)} %get-tuple-element.26.state_ref), custom_call_target="tpu_custom_call" | custom-call | tf_op jit(solution)/shard_map/gather_send/pallas_call | solution.py:321
  23.6 0.0 copy-start
  23.6 0.0 copy-start.2
  23.6 5.7 %all-to-all-start.1 = ((bf16[64,8,1152]{2,1,0:T(8,128)(2,1)}), bf16[64,8,1152]{2,1,0:T(8,128)(2,1)S(1)}, u32[]{:S(2)}, u32[]{:S(2)}) async-start(bf16[64,8,1152]{2,1,0:T(8,128)(2,1)} %gather_send.1), calls=%async_computation.1 | async-start | bytes 2359296 | tf_op jit(solution)/shard_map/all_to_all | solution.py:330
  29.4 2.8 %collective-permute-start.2 = (bf16[256,256]{1,0:T(8,128)(2,1)S(1)}, bf16[256,256]{1,0:T(8,128)(2,1)S(1)}, u32[]{:S(2)}, u32[]{:S(2)}) collective-permute-start(bf16[256,256]{1,0:T(8,128)(2,1)S(1)} %get-tuple-element.24.refs_0_.refs_6_.refs_4_), channel_id=1, source_target_pairs={{0,3},{1,0},{2,1},{3,2},{4,7},{5,4},{6,5},{7,6},{8,11},{9,8},{10,9... | collective-permute-start | bytes 393224 | tf_op jit(solution)/shard_map/ppermute | solution.py:275
  32.2 0.8 collective-permute-start.1
  33.0 0.9 collective-permute-start
  33.9 4.2 %collective-permute-done.2.refs_3_.refs_9_.refs_7_ = bf16[256,256]{1,0:T(8,128)(2,1)S(1)} collective-permute-done((bf16[256,256]{1,0:T(8,128)(2,1)S(1)}, bf16[256,256]{1,0:T(8,128)(2,1)S(1)}, u32[]{:S(2)}, u32[]{:S(2)}) %collective-permute-start.2) | collective-permute-done | bytes 131104 | tf_op jit(solution)/shard_map/ppermute | solution.py:275
  38.1 2.0 %collective-permute-done.1.refs_2_.refs_8_.refs_6_ = bf16[256,256]{1,0:T(8,128)(2,1)S(1)} collective-permute-done((bf16[256,256]{1,0:T(8,128)(2,1)S(1)}, bf16[256,256]{1,0:T(8,128)(2,1)S(1)}, u32[]{:S(2)}, u32[]{:S(2)}) %collective-permute-start.1) | collective-permute-done | bytes 131104 | tf_op jit(solution)/shard_map/ppermute | solution.py:275
  40.1 1.7 %collective-permute-done.refs_1_.refs_7_.refs_5_ = bf16[256,256]{1,0:T(8,128)(2,1)S(1)} collective-permute-done((bf16[256,256]{1,0:T(8,128)(2,1)S(1)}, bf16[256,256]{1,0:T(8,128)(2,1)S(1)}, u32[]{:S(2)}, u32[]{:S(2)}) %collective-permute-start) | collective-permute-done | bytes 131104 | tf_op jit(solution)/shard_map/ppermute | solution.py:275
  41.8 0.0 copy-done
  41.8 0.0 copy-done.2
  41.8 0.6 masks.1
  42.4 17.7 %all-to-all-done.1.refs_1_.arrived_ref = bf16[64,8,1152]{2,1,0:T(8,128)(2,1)S(1)} async-done(((bf16[64,8,1152]{2,1,0:T(8,128)(2,1)}), bf16[64,8,1152]{2,1,0:T(8,128)(2,1)S(1)}, u32[]{:S(2)}, u32[]{:S(2)}) %all-to-all-start.1) | async-done | bytes 1179680 | tf_op jit(solution)/shard_map/all_to_all | solution.py:330
  60.1 0.1 shard_map.96
  60.2 1.6 %collective-permute-start.6 = (bf16[8,32,256]{2,1,0:T(8,128)(2,1)S(1)}, bf16[8,32,256]{2,1,0:T(8,128)(2,1)S(1)}, u32[]{:S(2)}, u32[]{:S(2)}) collective-permute-start(bf16[8,32,256]{2,1,0:T(8,128)(2,1)S(1)} %get-tuple-element.35), channel_id=1, source_target_pairs={{0,1},{1,2},{2,3},{3,0},{4,5},{5,6},{6,7},{7,4},{8,9},{9,10},{10,1... | collective-permute-start | bytes 393224 | tf_op jit(solution)/shard_map/ppermute | solution.py:275
  61.8 2.7 %collective-permute-start.7 = (bf16[8,32,256]{2,1,0:T(8,128)(2,1)S(1)}, bf16[8,32,256]{2,1,0:T(8,128)(2,1)S(1)}, u32[]{:S(2)}, u32[]{:S(2)}) collective-permute-start(bf16[8,32,256]{2,1,0:T(8,128)(2,1)S(1)} %get-tuple-element.36), channel_id=1, source_target_pairs={{0,2},{1,3},{2,0},{3,1},{4,6},{5,7},{6,4},{7,5},{8,10},{9,11},{10,... | collective-permute-start | bytes 393224 | tf_op jit(solution)/shard_map/ppermute | solution.py:275
  64.5 1.4 %collective-permute-start.8 = (bf16[8,32,256]{2,1,0:T(8,128)(2,1)S(1)}, bf16[8,32,256]{2,1,0:T(8,128)(2,1)S(1)}, u32[]{:S(2)}, u32[]{:S(2)}) collective-permute-start(bf16[8,32,256]{2,1,0:T(8,128)(2,1)S(1)} %get-tuple-element.37), channel_id=1, source_target_pairs={{0,3},{1,0},{2,1},{3,2},{4,7},{5,4},{6,5},{7,6},{8,11},{9,8},{10,9... | collective-permute-start | bytes 393224 | tf_op jit(solution)/shard_map/ppermute | solution.py:275
  66.0 0.1 shard_map.95
  66.0 0.7 collective-permute-start.3
  66.7 0.9 collective-permute-start.4
  67.6 0.0 collective-permute-done.6.refs_2_
  67.6 1.9 %collective-permute-start.5 = (bf16[8,32,256]{2,1,0:T(8,128)(2,1)S(1)}, bf16[8,32,256]{2,1,0:T(8,128)(2,1)S(1)}, u32[]{:S(2)}, u32[]{:S(2)}) collective-permute-start(bf16[8,32,256]{2,1,0:T(8,128)(2,1)S(1)} %get-tuple-element.30), channel_id=1, source_target_pairs={{0,3},{1,0},{2,1},{3,2},{4,7},{5,4},{6,5},{7,6},{8,11},{9,8},{10,9... | collective-permute-start | bytes 393224 | tf_op jit(solution)/shard_map/ppermute | solution.py:275
  69.5 0.5 join_virtual.1.refs_12_
  70.0 1.7 %collective-permute-done.7.refs_3_ = bf16[8,32,256]{2,1,0:T(8,128)(2,1)S(1)} collective-permute-done((bf16[8,32,256]{2,1,0:T(8,128)(2,1)S(1)}, bf16[8,32,256]{2,1,0:T(8,128)(2,1)S(1)}, u32[]{:S(2)}, u32[]{:S(2)}) %collective-permute-start.7) | collective-permute-done | bytes 131104 | tf_op jit(solution)/shard_map/ppermute | solution.py:275
  71.7 0.2 collective-permute-done.8.refs_4_
  71.8 2.8 %shard_map.97.refs_13_ = bf16[256,256]{1,0:T(8,128)(2,1)S(1)} custom-call(bf16[2048,256]{1,0:T(8,128)(2,1)S(1)} %get-tuple-element.23.refs_0_, bf16[8,32,256]{2,1,0:T(8,128)(2,1)S(1)} %get-tuple-element.34.refs_1_, bf16[8,32,256]{2,1,0:T(8,128)(2,1)S(1)} %collective-permute-done.6.refs_2_, bf16[8,32,256]{2,1,0:T(8,128)(2,1)S(1)} %collective-permute-done.7.refs_3_, ...), custom_call_target="tpu_custom_call" | custom-call | tf_op jit(solution)/shard_map/pallas_call | solution.py:357
  74.6 0.0 collective-permute-done.3.refs_2_
  74.6 1.9 %collective-permute-done.4.refs_3_ = bf16[8,32,256]{2,1,0:T(8,128)(2,1)S(1)} collective-permute-done((bf16[8,32,256]{2,1,0:T(8,128)(2,1)S(1)}, bf16[8,32,256]{2,1,0:T(8,128)(2,1)S(1)}, u32[]{:S(2)}, u32[]{:S(2)}) %collective-permute-start.4) | collective-permute-done | bytes 131104 | tf_op jit(solution)/shard_map/ppermute | solution.py:275
  76.5 0.0 collective-permute-done.5.refs_4_
  76.5 2.8 %shard_map.98 = (bf16[72,512]{1,0:T(8,128)(2,1)S(1)}, bf16[72,512]{1,0:T(8,128)(2,1)S(1)}, bf16[72,512]{1,0:T(8,128)(2,1)S(1)}, bf16[72,512]{1,0:T(8,128)(2,1)S(1)}) custom-call(bf16[2048,256]{1,0:T(8,128)(2,1)S(1)} %get-tuple-element.23.refs_0_, bf16[8,32,256]{2,1,0:T(8,128)(2,1)S(1)} %get-tuple-element.27.refs_1_, ...), custom_call_target="tpu_custom_call" | custom-call | tf_op jit(solution)/shard_map/pallas_call | solution.py:357
  79.3 1.4 %collective-permute-start.9 = (bf16[72,512]{1,0:T(8,128)(2,1)S(1)}, bf16[72,512]{1,0:T(8,128)(2,1)S(1)}, u32[]{:S(2)}, u32[]{:S(2)}) collective-permute-start(bf16[72,512]{1,0:T(8,128)(2,1)S(1)} %get-tuple-element.39), channel_id=1, source_target_pairs={{0,1},{1,2},{2,3},{3,0},{4,5},{5,6},{6,7},{7,4},{8,9},{9,10},{10,1... | collective-permute-start | bytes 221192 | tf_op jit(solution)/shard_map/ppermute | solution.py:275
  80.7 2.4 %collective-permute-start.10 = (bf16[72,512]{1,0:T(8,128)(2,1)S(1)}, bf16[72,512]{1,0:T(8,128)(2,1)S(1)}, u32[]{:S(2)}, u32[]{:S(2)}) collective-permute-start(bf16[72,512]{1,0:T(8,128)(2,1)S(1)} %get-tuple-element.40), channel_id=1, source_target_pairs={{0,2},{1,3},{2,0},{3,1},{4,6},{5,7},{6,4},{7,5},{8,10},{9,11},{10,... | collective-permute-start | bytes 221192 | tf_op jit(solution)/shard_map/ppermute | solution.py:275
  83.2 1.5 %collective-permute-start.11 = (bf16[72,512]{1,0:T(8,128)(2,1)S(1)}, bf16[72,512]{1,0:T(8,128)(2,1)S(1)}, u32[]{:S(2)}, u32[]{:S(2)}) collective-permute-start(bf16[72,512]{1,0:T(8,128)(2,1)S(1)} %get-tuple-element.41), channel_id=1, source_target_pairs={{0,3},{1,0},{2,1},{3,2},{4,7},{5,4},{6,5},{7,6},{8,11},{9,8},{10,9... | collective-permute-start | bytes 221192 | tf_op jit(solution)/shard_map/ppermute | solution.py:275
  84.7 0.9 %collective-permute-done.9.refs_1_ = bf16[72,512]{1,0:T(8,128)(2,1)S(1)} collective-permute-done((bf16[72,512]{1,0:T(8,128)(2,1)S(1)}, bf16[72,512]{1,0:T(8,128)(2,1)S(1)}, u32[]{:S(2)}, u32[]{:S(2)}) %collective-permute-start.9) | collective-permute-done | bytes 73760 | tf_op jit(solution)/shard_map/ppermute | solution.py:275
  85.6 1.0 %collective-permute-done.10.refs_2_ = bf16[72,512]{1,0:T(8,128)(2,1)S(1)} collective-permute-done((bf16[72,512]{1,0:T(8,128)(2,1)S(1)}, bf16[72,512]{1,0:T(8,128)(2,1)S(1)}, u32[]{:S(2)}, u32[]{:S(2)}) %collective-permute-start.10) | collective-permute-done | bytes 73760 | tf_op jit(solution)/shard_map/ppermute | solution.py:275
  86.6 0.9 %collective-permute-done.11.refs_3_ = bf16[72,512]{1,0:T(8,128)(2,1)S(1)} collective-permute-done((bf16[72,512]{1,0:T(8,128)(2,1)S(1)}, bf16[72,512]{1,0:T(8,128)(2,1)S(1)}, u32[]{:S(2)}, u32[]{:S(2)}) %collective-permute-start.11) | collective-permute-done | bytes 73760 | tf_op jit(solution)/shard_map/ppermute | solution.py:275
  87.5 1.3 %assemble.1 = (bf16[64,2048]{1,0:T(8,128)(2,1)}, bf16[4,64]{1,0:T(4,128)(2,1)}) custom-call(bf16[72,512]{1,0:T(8,128)(2,1)S(1)} %get-tuple-element.38.refs_0_, bf16[72,512]{1,0:T(8,128)(2,1)S(1)} %collective-permute-done.9.refs_1_, bf16[72,512]{1,0:T(8,128)(2,1)S(1)} %collective-permute-done.10.refs_2_, bf16[72,512]{1,0:T(8,128)(2,1)S(1)} %collective-permute-done.11.refs_3_, ...), custom_call_target="tpu_custom_call" | custom-call | tf_op jit(solution)/shard_map/assemble/pallas_call | solution.py:374
Async XLA Ops:
  0.6 0.7 copy-start.1
  2.0 20.3 %all-to-all-start = ((s32[64,1,128]{2,1,0:T(1,128)}), s32[64,1,128]{2,1,0:T(1,128)S(1)}, u32[]{:S(2)}, u32[]{:S(2)}) async-start(s32[64,1,128]{2,1,0:T(1,128)} %bitcast.6), calls=%async_computation | async-start | bytes 65536 | tf_op jit(solution)/shard_map/all_to_all | solution.py:290
  13.8 0.7 copy-start.3
  23.6 18.2 %copy-start = (s32[2048,16]{0,1:T(8,128)S(1)}, s32[2048,16]{0,1:T(8,128)}, u32[]{:S(2)}) copy-start(s32[2048,16]{0,1:T(8,128)} %param.15) | copy-start | bytes 393220
  23.6 18.1 %copy-start.2 = (s32[16,4]{0,1:T(4,128)S(1)}, s32[16,4]{0,1:T(4,128)}, u32[]{:S(2)}) copy-start(s32[16,4]{0,1:T(4,128)} %param.14) | copy-start | bytes 772
  23.6 36.5 %all-to-all-start.1 = ((bf16[64,8,1152]{2,1,0:T(8,128)(2,1)}), bf16[64,8,1152]{2,1,0:T(8,128)(2,1)S(1)}, u32[]{:S(2)}, u32[]{:S(2)}) async-start(bf16[64,8,1152]{2,1,0:T(8,128)(2,1)} %gather_send.1), calls=%async_computation.1 | async-start | bytes 2359296 | tf_op jit(solution)/shard_map/all_to_all | solution.py:330
  29.4 8.7 %collective-permute-start.2 = (bf16[256,256]{1,0:T(8,128)(2,1)S(1)}, bf16[256,256]{1,0:T(8,128)(2,1)S(1)}, u32[]{:S(2)}, u32[]{:S(2)}) collective-permute-start(bf16[256,256]{1,0:T(8,128)(2,1)S(1)} %get-tuple-element.24.refs_0_.refs_6_.refs_4_), channel_id=1, source_target_pairs={{0,3},{1,0},{2,1},{3,2},{4,7},{5,4},{6,5},{7,6},{8,11},{9,8},{10,9... | collective-permute-start | bytes 393224 | tf_op jit(solution)/shard_map/ppermute | solution.py:275
  32.2 7.9 %collective-permute-start.1 = (bf16[256,256]{1,0:T(8,128)(2,1)S(1)}, bf16[256,256]{1,0:T(8,128)(2,1)S(1)}, u32[]{:S(2)}, u32[]{:S(2)}) collective-permute-start(bf16[256,256]{1,0:T(8,128)(2,1)S(1)} %get-tuple-element.24.refs_0_.refs_6_.refs_4_), channel_id=1, source_target_pairs={{0,2},{1,3},{2,0},{3,1},{4,6},{5,7},{6,4},{7,5},{8,10},{9,11},{10,... | collective-permute-start | bytes 393224 | tf_op jit(solution)/shard_map/ppermute | solution.py:275
  33.0 8.8 %collective-permute-start = (bf16[256,256]{1,0:T(8,128)(2,1)S(1)}, bf16[256,256]{1,0:T(8,128)(2,1)S(1)}, u32[]{:S(2)}, u32[]{:S(2)}) collective-permute-start(bf16[256,256]{1,0:T(8,128)(2,1)S(1)} %get-tuple-element.24.refs_0_.refs_6_.refs_4_), channel_id=1, source_target_pairs={{0,1},{1,2},{2,3},{3,0},{4,5},{5,6},{6,7},{7,4},{8,9},{9,10},{10,1... | collective-permute-start | bytes 393224 | tf_op jit(solution)/shard_map/ppermute | solution.py:275
  60.2 7.4 %collective-permute-start.6 = (bf16[8,32,256]{2,1,0:T(8,128)(2,1)S(1)}, bf16[8,32,256]{2,1,0:T(8,128)(2,1)S(1)}, u32[]{:S(2)}, u32[]{:S(2)}) collective-permute-start(bf16[8,32,256]{2,1,0:T(8,128)(2,1)S(1)} %get-tuple-element.35), channel_id=1, source_target_pairs={{0,1},{1,2},{2,3},{3,0},{4,5},{5,6},{6,7},{7,4},{8,9},{9,10},{10,1... | collective-permute-start | bytes 393224 | tf_op jit(solution)/shard_map/ppermute | solution.py:275
  61.8 9.9 %collective-permute-start.7 = (bf16[8,32,256]{2,1,0:T(8,128)(2,1)S(1)}, bf16[8,32,256]{2,1,0:T(8,128)(2,1)S(1)}, u32[]{:S(2)}, u32[]{:S(2)}) collective-permute-start(bf16[8,32,256]{2,1,0:T(8,128)(2,1)S(1)} %get-tuple-element.36), channel_id=1, source_target_pairs={{0,2},{1,3},{2,0},{3,1},{4,6},{5,7},{6,4},{7,5},{8,10},{9,11},{10,... | collective-permute-start | bytes 393224 | tf_op jit(solution)/shard_map/ppermute | solution.py:275
  64.5 7.3 %collective-permute-start.8 = (bf16[8,32,256]{2,1,0:T(8,128)(2,1)S(1)}, bf16[8,32,256]{2,1,0:T(8,128)(2,1)S(1)}, u32[]{:S(2)}, u32[]{:S(2)}) collective-permute-start(bf16[8,32,256]{2,1,0:T(8,128)(2,1)S(1)} %get-tuple-element.37), channel_id=1, source_target_pairs={{0,3},{1,0},{2,1},{3,2},{4,7},{5,4},{6,5},{7,6},{8,11},{9,8},{10,9... | collective-permute-start | bytes 393224 | tf_op jit(solution)/shard_map/ppermute | solution.py:275
  66.0 8.6 %collective-permute-start.3 = (bf16[8,32,256]{2,1,0:T(8,128)(2,1)S(1)}, bf16[8,32,256]{2,1,0:T(8,128)(2,1)S(1)}, u32[]{:S(2)}, u32[]{:S(2)}) collective-permute-start(bf16[8,32,256]{2,1,0:T(8,128)(2,1)S(1)} %get-tuple-element.28), channel_id=1, source_target_pairs={{0,1},{1,2},{2,3},{3,0},{4,5},{5,6},{6,7},{7,4},{8,9},{9,10},{10,1... | collective-permute-start | bytes 393224 | tf_op jit(solution)/shard_map/ppermute | solution.py:275
  66.7 9.8 %collective-permute-start.4 = (bf16[8,32,256]{2,1,0:T(8,128)(2,1)S(1)}, bf16[8,32,256]{2,1,0:T(8,128)(2,1)S(1)}, u32[]{:S(2)}, u32[]{:S(2)}) collective-permute-start(bf16[8,32,256]{2,1,0:T(8,128)(2,1)S(1)} %get-tuple-element.29), channel_id=1, source_target_pairs={{0,2},{1,3},{2,0},{3,1},{4,6},{5,7},{6,4},{7,5},{8,10},{9,11},{10,... | collective-permute-start | bytes 393224 | tf_op jit(solution)/shard_map/ppermute | solution.py:275
  67.6 9.0 %collective-permute-start.5 = (bf16[8,32,256]{2,1,0:T(8,128)(2,1)S(1)}, bf16[8,32,256]{2,1,0:T(8,128)(2,1)S(1)}, u32[]{:S(2)}, u32[]{:S(2)}) collective-permute-start(bf16[8,32,256]{2,1,0:T(8,128)(2,1)S(1)} %get-tuple-element.30), channel_id=1, source_target_pairs={{0,3},{1,0},{2,1},{3,2},{4,7},{5,4},{6,5},{7,6},{8,11},{9,8},{10,9... | collective-permute-start | bytes 393224 | tf_op jit(solution)/shard_map/ppermute | solution.py:275
  79.3 6.3 %collective-permute-start.9 = (bf16[72,512]{1,0:T(8,128)(2,1)S(1)}, bf16[72,512]{1,0:T(8,128)(2,1)S(1)}, u32[]{:S(2)}, u32[]{:S(2)}) collective-permute-start(bf16[72,512]{1,0:T(8,128)(2,1)S(1)} %get-tuple-element.39), channel_id=1, source_target_pairs={{0,1},{1,2},{2,3},{3,0},{4,5},{5,6},{6,7},{7,4},{8,9},{9,10},{10,1... | collective-permute-start | bytes 221192 | tf_op jit(solution)/shard_map/ppermute | solution.py:275
  80.7 5.9 %collective-permute-start.10 = (bf16[72,512]{1,0:T(8,128)(2,1)S(1)}, bf16[72,512]{1,0:T(8,128)(2,1)S(1)}, u32[]{:S(2)}, u32[]{:S(2)}) collective-permute-start(bf16[72,512]{1,0:T(8,128)(2,1)S(1)} %get-tuple-element.40), channel_id=1, source_target_pairs={{0,2},{1,3},{2,0},{3,1},{4,6},{5,7},{6,4},{7,5},{8,10},{9,11},{10,... | collective-permute-start | bytes 221192 | tf_op jit(solution)/shard_map/ppermute | solution.py:275
  83.2 4.4 %collective-permute-start.11 = (bf16[72,512]{1,0:T(8,128)(2,1)S(1)}, bf16[72,512]{1,0:T(8,128)(2,1)S(1)}, u32[]{:S(2)}, u32[]{:S(2)}) collective-permute-start(bf16[72,512]{1,0:T(8,128)(2,1)S(1)} %get-tuple-element.41), channel_id=1, source_target_pairs={{0,3},{1,0},{2,1},{3,2},{4,7},{5,4},{6,5},{7,6},{8,11},{9,8},{10,9... | collective-permute-start | bytes 221192 | tf_op jit(solution)/shard_map/ppermute | solution.py:275
